TPU v7x, 256 devices: a whole 4x4x8 slice. The times are simulated.
256 devices in a mesh: stat: 32 (over x_hi, z, core), tm: 8 (over y, x_lo).
Axes of the slice: x: 4 (x_hi: 2, x_lo: 2; x = x_hi * 2 + x_lo), y: 4, z: 8, core: 2. Of those that a mesh axis runs over, the one named last changes fastest.
Arguments:
- voltages: bfloat16 [2, 1024, 32, 4096], P(None, 'stat', 'tm'), may hold values from -6 to 6
- beam_weights: bfloat16 [2, 1024, 256], P(None, 'stat'), may hold values from -0.125 to 0.125
Outputs:
- beams: bfloat16 [4096, 32, 2, 256], P('stat', 'tm')
- visibilities: float32 [1024, 32, 2, 1024], P('tm', 'stat')
All inputs are finite; a program needn't handle non-finite values.
Results may differ from a plain program's by a relative error of at most 0.011.
Values may be sent and summed in bfloat16 or wider, within the bound.
No kernel may reach another device: no remote copies, remote signals or barrier semaphores. Data moves between devices by JAX's collectives and lax.ppermute only.
A program may use at most 64 MiB of HBM per device.

v0:
```python
import math

import jax
import jax.numpy as jnp
from jax import lax
from jax.sharding import Mesh
from jax.sharding import PartitionSpec as P

INPUTS = 1024
NA = 16
NB = 256
BEAMS = 256
AVG = 128
STAT = ("stat_0", "stat_1", "stat_2")
TM = ("tm_0", "tm_1")


def laid_out(pieces, dim):
    lengths = list(pieces.shape[1:])
    lengths[dim] *= pieces.shape[0]
    return jnp.moveaxis(pieces, 0, dim).reshape(lengths)


def from_everyone(array, axis):
    copies = jnp.broadcast_to(array, (lax.axis_size(axis), *array.shape))
    return lax.all_to_all(copies, axis, split_axis=0, concat_axis=0, tiled=True)


def gather_directly(array, axis, dim):
    return laid_out(from_everyone(array, axis), dim)


def in_blocks(array, dim, size):
    lengths = array.shape
    pieces = array.reshape(*lengths[:dim], size, lengths[dim] // size, *lengths[dim + 1 :])
    return jnp.moveaxis(pieces, dim, 0)


def exchange_in_order(pieces, axes, order):
    inside = pieces.shape[1:]
    out = pieces.reshape(*(lax.axis_size(a) for a in axes), *inside)
    for k in order:
        out = lax.all_to_all(out, axes[k], k, k, tiled=True)
    return out.reshape(-1, *inside)


def core_and_chips(array, groups, order, split_dim, concat_dim):
    size = lax.axis_size(groups[0]) * lax.axis_size(groups[1])
    pieces = in_blocks(array, split_dim, size)
    return laid_out(exchange_in_order(pieces, groups, order), concat_dim)


def sum_by_axis(terms, axes):
    subtotal = terms.astype(jnp.bfloat16)
    for axis in axes:
        subtotal = lax.psum_scatter(subtotal, axis, scatter_dimension=0, tiled=True)
    return subtotal.astype(jnp.float32)


def dft_block(length):
    index = jnp.arange(length, dtype=jnp.int32)
    product = index[:, None] * index[None, :] % length
    angle = product.astype(jnp.float32) * (2.0 * math.pi / length)
    cosine = jnp.cos(angle)
    sine = jnp.sin(angle)
    return jnp.stack([jnp.stack([cosine, -sine]), jnp.stack([sine, cosine])])


def fine_spectra(voltages):
    block_inputs = voltages.shape[1]
    spectra_count = voltages.shape[2]
    signal = voltages.astype(jnp.float32).reshape(2, block_inputs, spectra_count, NA, NB)
    first = jnp.einsum("poak,pisab->osikb", dft_block(NA), signal, precision=lax.Precision.HIGH)
    outer_index = jnp.arange(NA, dtype=jnp.int32)
    inner_index = jnp.arange(NB, dtype=jnp.int32)
    rotation = (outer_index[:, None] * inner_index[None, :] % (NA * NB)).astype(jnp.float32) * (
        2.0 * math.pi / (NA * NB)
    )
    cos_twist = jnp.cos(rotation)
    sin_twist = jnp.sin(rotation)
    rotated = jnp.stack(
        [first[0] * cos_twist + first[1] * sin_twist, first[1] * cos_twist - first[0] * sin_twist]
    )
    final = jnp.einsum("osikb,ocbq->csiqk", rotated, dft_block(NB), precision=lax.Precision.HIGH)
    norm_factor = 1.0 / math.sqrt(NA * NB)
    return (
        (final * norm_factor).reshape(2, spectra_count, block_inputs, NA * NB).astype(jnp.bfloat16)
    )


def stack_weights(weights):
    return jnp.stack(
        [jnp.stack([weights[0], weights[1]], 1), jnp.stack([-weights[1], weights[0]], 1)], 0
    )


def body(voltages, beam_weights):
    stat_count = lax.axis_size(STAT)
    time_count = lax.axis_size(TM)
    block_inputs = voltages.shape[1]
    spectra = fine_spectra(voltages)
    spectra_count = spectra.shape[1]
    channel_share = NA * NB // stat_count
    all_weights = gather_directly(beam_weights, STAT, 1)
    full_stack = stack_weights(all_weights)
    turned = core_and_chips(spectra, (("stat_0", "stat_1"), "stat_2"), (1, 0), 3, 2)
    item_count = turned.shape[1]

    def add_block(block_index, running):
        offset = (block_index * block_inputs).astype(jnp.int32)
        spec_block = lax.dynamic_slice_in_dim(turned, offset, block_inputs, 2)
        weight_block = lax.dynamic_slice_in_dim(full_stack, offset, block_inputs, 1)
        partial_value = jnp.einsum(
            "psic,piqb->csqb", spec_block, weight_block, preferred_element_type=jnp.float32
        )
        rounded = lax.optimization_barrier(partial_value.astype(jnp.bfloat16))
        return running + rounded.astype(jnp.float32)

    initial = jnp.zeros((turned.shape[3], item_count, 2, BEAMS), jnp.float32)
    beams = lax.fori_loop(0, stat_count, add_block, initial).astype(jnp.bfloat16)
    local_vch = channel_share // AVG
    scale = 1.0 / (spectra_count * time_count * AVG)
    split = turned.reshape(2, spectra_count, INPUTS, local_vch, AVG)
    real_gram = jnp.einsum("psiva,psjva->ivj", split, split, preferred_element_type=jnp.float32)
    mixed = jnp.einsum("siva,sjva->ivj", split[1], split[0], preferred_element_type=jnp.float32)
    mixed = mixed - jnp.einsum(
        "siva,sjva->ivj", split[0], split[1], preferred_element_type=jnp.float32
    )
    visibilities = sum_by_axis(jnp.stack([real_gram, mixed], axis=2) * scale, TM)
    return (beams, visibilities)


def solution(mesh):
    finer = Mesh(
        mesh.devices.reshape(2, 8, 2, 4, 2), ("stat_0", "stat_1", "stat_2", "tm_0", "tm_1")
    )
    return jax.shard_map(
        body,
        mesh=finer,
        in_specs=(P(None, STAT, TM, None), P(None, STAT, None)),
        out_specs=(P(STAT, TM, None, None), P(TM, STAT, None, None)),
        check_vma=False,
    )
```

profile of v0, /device:TPU:64, one launch (start us, length us, event | category | flops | bytes accessed | tf_op | source)
XLA Modules:
  0.0 220.5 jit_solution(15862437898061825587)
XLA Ops:
  9.4 3.2 %reshape.292 = bf16[2,32,4,16,256]{4,3,2,1,0:T(8,128)(2,1)S(1)} reshape(bf16[2,32,4,4096]{3,2,1,0:T(4,128)(2,1)} %param.4) | data formatting | bytes 4194304 | tf_op jit(solution)/shard_map/reshape | solution.py:72
  12.7 1.3 convolution_bitcast_fusion.2
  15.9 4.8 %fusion.11 = bf16[2,4,32,256,16]{3,2,4,1,0:T(8,128)(2,1)S(1)} fusion(f32[2,4,32,16,256]{4,3,1,2,0:T(8,128)S(1)} %pad_maximum_fusion, f32[1,2,256,256]{3,2,0,1:T(8,128)S(1)} %get-tuple-element.134, f32[1,2,256,256]{3,2,0,1:T(8,128)S(1)} %get-tuple-element.133), kind=kOutput, calls=%fused_computation.21 | convolution fusion | flops 3223584768 | bytes 7340032 | tf_op jit(solution)/shard_map/osikb,ocbq->csiqk/dot_general | solution.py:84
  20.7 8.5 %copy.27 = bf16[2,4,32,256,16]{2,4,3,1,0:T(8,128)(2,1)} copy(bf16[2,4,32,256,16]{3,2,4,1,0:T(8,128)(2,1)S(1)} %fusion.11) | data formatting | bytes 4194304 | tf_op jit(solution)/shard_map/convert_element_type | solution.py:87
  29.2 6.9 %copy.28 = bf16[16,2,2,4,32,128]{5,4,3,2,0,1:T(8,128)(2,1)S(1)} copy(bf16[16,2,2,4,32,128]{4,5,1,0,3,2:T(8,128)(2,1)} %bitcast.123) | data formatting | bytes 4194304 | tf_op jit(solution)/shard_map/reshape | solution.py:41
  36.2 5.4 %all_to_all.15 = bf16[16,2,2,4,32,128]{5,4,3,2,0,1:T(8,128)(2,1)S(1)} all-to-all(bf16[16,2,2,4,32,128]{5,4,3,2,0,1:T(8,128)(2,1)S(1)} %copy.28), channel_id=1, replica_groups=mesh['stat_0'=2,'stat_1'=8,'stat_2'=2,'tm_0'=4,'tm_1'=2] {'stat_2'}, dimensions={1} | all-to-all | bytes 4194304 | tf_op jit(solution)/shard_map/all_to_all | solution.py:43
  42.2 58.9 %all_to_all.16 = bf16[16,2,2,4,32,128]{5,4,3,2,1,0:T(8,128)(2,1)S(1)} all-to-all(bf16[16,2,2,4,32,128]{5,4,3,2,1,0:T(8,128)(2,1)S(1)} %copy.29), channel_id=1, replica_groups=mesh['stat_0'=2,'stat_1'=8,'stat_2'=2,'tm_0'=4,'tm_1'=2] {'stat_0','stat..., dimensions={0} | all-to-all | bytes 4194304 | tf_op jit(solution)/shard_map/all_to_all | solution.py:43
  102.5 1.3 fusion.50
  103.8 1.3 fusion.6
  105.1 2.4 %convolution_bitcast_fusion.1 = f32[1024,1,1,1024]{0,3,2,1:T(8,128)S(1)} fusion(bf16[2,4,1024,128]{3,2,1,0:T(8,128)(2,1)S(1)} %bitcast.131), kind=kOutput, calls=%fused_computation.19 | convolution fusion | flops 2147483648 | bytes 6291456 | tf_op jit(solution)/shard_map/psiva,psjva->ivj/dot_general | solution.py:124
  107.5 2.6 %fusion.5 = bf16[1024,1,2,1024]{0,3,2,1:T(8,128)(2,1)} fusion(f32[1024,1,1,1024]{0,3,2,1:T(8,128)S(1)} %fusion.6, f32[1024,1,1,1024]{0,3,2,1:T(8,128)S(1)} %convolution_bitcast_fusion.1), kind=kLoop, calls=%fused_computation.10 | loop fusion | flops 6291456 | bytes 12582912 | tf_op jit(solution)/shard_map/convert_element_type | solution.py:54
  111.9 7.4 %all-to-all-start = ((bf16[32,2,32,256]{3,2,1,0:T(8,128)(2,1)}), bf16[32,2,32,256]{3,2,1,0:T(8,128)(2,1)S(1)}, u32[]{:S(2)}, u32[]{:S(2)}) async-start(bf16[32,2,32,256]{3,2,1,0:T(8,128)(2,1)} %broadcast_in_dim.5), calls=%async_computation | async-start | bytes 2097152 | tf_op jit(solution)/shard_map/all_to_all | solution.py:26
  119.4 28.4 %all-to-all-done = bf16[32,2,32,256]{3,2,1,0:T(8,128)(2,1)S(1)} async-done(((bf16[32,2,32,256]{3,2,1,0:T(8,128)(2,1)}), bf16[32,2,32,256]{3,2,1,0:T(8,128)(2,1)S(1)}, u32[]{:S(2)}, u32[]{:S(2)}) %all-to-all-start) | async-done | bytes 1048608 | tf_op jit(solution)/shard_map/all_to_all | solution.py:26
  148.3 10.2 %reduce-scatter.5.cloned.1.call-done = bf16[256,1,2,1024]{0,3,2,1:T(8,128)(2,1)} async-done(((bf16[1024,1,2,1024]{0,3,2,1:T(8,128)(2,1)}), bf16[256,1,2,1024]{0,3,2,1:T(8,128)(2,1)}) %reduce-scatter.5.cloned.1.call-update) | async-done | bytes 1048592 | tf_op jit(solution)/shard_map/reduce_scatter | solution.py:56
  158.5 2.3 %copy.43 = bf16[256,2048]{1,0:T(8,128)(2,1)} copy(bf16[256,2048]{0,1:T(8,128)(2,1)} %bitcast.135) | data formatting | bytes 2097152
  160.8 49.0 %while.14 = (s32[]{:T(128)}, f32[128,4,2,256]{0,3,1,2:T(8,128)S(1)}, bf16[2,1024,2,256]{3,1,0,2:T(8,128)(2,1)S(1)}, bf16[2,4,1024,128]{3,2,1,0:T(8,128)(2,1)}, s32[]{:T(128)}, /*index=5*/s32[]{:T(128)}, s32[]{:T(128)}, s32[]{:T(128)}) while((s32[]{:T(128)}, f32[128,4,2,256]{0,3,1,2:T(8,128)S(1)}, ...), condition=%wide.region_1.2_spmd.clone, body=%wide.region_0.1_spmd.clone.sunk | while | flops 34603012 | bytes 3277973 | solution.py:120
  160.8 1.2 fusion.61
  168.5 1.2 fusion.61
  171.6 1.2 fusion.61
  174.6 1.2 fusion.61
  177.7 1.2 fusion.61
  180.8 1.2 fusion.61
  183.8 1.2 fusion.61
  186.9 1.2 fusion.61
  190.0 1.2 fusion.61
  193.0 1.2 fusion.61
  196.1 1.2 fusion.61
  199.2 1.2 fusion.61
  202.2 1.2 fusion.61
  209.9 1.3 copy.32
  211.1 1.3 copy.44
  212.5 1.2 copy.33
  (78 shorter events, 41.3 us)
Async XLA Ops:
  7.2 151.4 %reduce-scatter.5.cloned.1.call-start = ((), (), s32[]{:S(2)}) async-start(), calls=%async_computation.5 | async-start | bytes 5242880 | tf_op jit(solution)/shard_map/reduce_scatter | solution.py:56
  102.1 3.0 %copy-start = (bf16[32,2,4,32,128]{4,3,0,2,1:T(8,128)(2,1)}, bf16[32,2,4,32,128]{4,3,0,2,1:T(8,128)(2,1)S(1)}, u32[]{:S(2)}) copy-start(bf16[32,2,4,32,128]{4,3,0,2,1:T(8,128)(2,1)S(1)} %get-tuple-element.128) | copy-start | bytes 6291460
  110.0 0.8 copy-start.1
  111.9 35.8 %all-to-all-start = ((bf16[32,2,32,256]{3,2,1,0:T(8,128)(2,1)}), bf16[32,2,32,256]{3,2,1,0:T(8,128)(2,1)S(1)}, u32[]{:S(2)}, u32[]{:S(2)}) async-start(bf16[32,2,32,256]{3,2,1,0:T(8,128)(2,1)} %broadcast_in_dim.5), calls=%async_computation | async-start | bytes 2097152 | tf_op jit(solution)/shard_map/all_to_all | solution.py:26
  119.3 91.8 %reduce-scatter.7.cloned.1.call-start = ((), (), s32[]{:S(2)}) async-start(), calls=%async_computation.6 | async-start | bytes 1572864
Sparse Core Ops, SparseCore 0:
  110.2 48.3 reduce-scatter.4
  161.6 25.1 reduce-scatter.6
where the time goes:
time: 224 us; the launch traced here: 220 us
  blocking collectives  64.3 us (29%)
  matrix products  48.3 us (22%)
  waiting for transfers between devices  38.6 us (17%)
  local copies, waits for them, and re-layouts  28.6 us (13%)
  other arithmetic  17.8 us (8%)
  between operations  14.2 us (6%)
  starting transfers between devices  7.49 us (3%)
    all_to_all x2, blocking collectives, exchange_in_order(): out = lax.all_to_all(out, axes[k], k, k, tiled=True)  64.3 us
    dot_general x32, matrix products, add_block(): jnp.einsum('psic,piqb->csqb', spec_block, weight_block, preferred_element...  37.2 us
    all_to_all x1, waiting for transfers between devices, from_everyone(): return lax.all_to_all(copies, axis, split_axis=0, concat_axis=0, tiled=True)  28.4 us
    add x32, other arithmetic, add_block(): return running + rounded.astype(jnp.float32)  10.7 us
    reduce_scatter x1, waiting for transfers between devices, sum_by_axis(): subtotal = lax.psum_scatter(subtotal, axis, scatter_dimension=0, tiled=True)  10.2 us
    convert_element_type x1, local copies, waits for them, and re-layouts, fine_spectra(): (final * norm_factor).reshape(2, spectra_count, block_inputs, NA * NB)  8.53 us
    all_to_all x1, starting transfers between devices, from_everyone(): return lax.all_to_all(copies, axis, split_axis=0, concat_axis=0, tiled=True)  7.41 us
    reshape x1, local copies, waits for them, and re-layouts, exchange_in_order(): out = pieces.reshape(*(lax.axis_size(a) for a in axes), *inside)  6.92 us
  transfers between devices with their start and end apart: 3, of which 2 were waited for; matrix products, arithmetic and copies ran while one was open for 23% of the time, Pallas kernels for 0%

commit v1 on v0

v1 whole, which is shorter than its diff:
```python
import math

import jax
import jax.numpy as jnp
import numpy as np
from jax import lax
from jax.experimental import pallas as pl
from jax.experimental.pallas import tpu as pltpu
from jax.sharding import Mesh
from jax.sharding import PartitionSpec as P

STAT = ("stat_0", "stat_1", "stat_2")
TM = ("tm_0", "tm_1")
NF = 4096
N_STAT = 32
N_TM = 8
SPECTRA = 4
CHUNKS = 4
IC = 8
ROWS = N_STAT * IC
OWN = ROWS // N_TM
HALF = 512
BF16 = jnp.bfloat16
F32 = jnp.float32
VMEM = pl.BlockSpec(memory_space=pltpu.VMEM)


def rotation(angle):
    cosine, sine = np.cos(angle), np.sin(angle)
    return np.block([[cosine, sine], [-sine, cosine]])


def dft_tables():
    outer = np.arange(32)
    first = 2.0 * np.pi * np.outer(outer, outer) / 32
    cosine, sine = np.cos(first), np.sin(first)
    eye = np.eye(SPECTRA)
    spread = lambda m: np.einsum("wc,st->wsct", m, eye).reshape(128, 128)
    left = np.block([[spread(cosine), spread(sine)], [-spread(sine), spread(cosine)]])
    w0 = np.repeat(np.arange(32), SPECTRA)
    twist = 2.0 * np.pi * np.outer(w0, np.arange(128)) / NF
    inner = 2.0 * np.pi * np.outer(np.arange(128), np.arange(128)) / 128
    right = rotation(inner) / math.sqrt(NF)
    right = right.reshape(2, 32, 4, 256).transpose(1, 0, 2, 3).reshape(256, 256)
    return (
        left.astype(np.float32),
        np.cos(twist).astype(np.float32),
        np.sin(twist).astype(np.float32),
        right.astype(np.float32),
    )


def natural_order(groups):
    source = np.arange(CHUNKS * groups * 4 * IC).reshape(CHUNKS, groups, 4, IC)
    target = source.transpose(1, 2, 0, 3).reshape(-1)
    order = np.zeros((source.size, source.size), np.float32)
    order[target, np.arange(source.size)] = 1.0
    return order


def params(mib):
    return pltpu.CompilerParams(vmem_limit_bytes=mib * 1024 * 1024)


def cost(macs, moved):
    return pl.CostEstimate(flops=2 * macs, bytes_accessed=moved, transcendentals=0)


def dot_nn(a, b):
    return lax.dot_general(a, b, (((1,), (0,)), ((), ())), preferred_element_type=F32)


def dot_nt(a, b):
    return lax.dot_general(a, b, (((1,), (1,)), ((), ())), preferred_element_type=F32)


def dft_kernel(x_ref, left_ref, cos_ref, sin_ref, right_ref, out_ref, stage):
    left = left_ref[...]
    right = right_ref[...]
    cosine = cos_ref[...]
    sine = sin_ref[...]
    for pair in range(IC // 2):
        signal = [jnp.concatenate([x_ref[0, 2 * pair + k], x_ref[1, 2 * pair + k]], 0) for k in (0, 1)]
        first = dot_nn(left, jnp.concatenate(signal, 1))
        turned = []
        for k in (0, 1):
            re = first[:128, 128 * k : 128 * k + 128]
            im = first[128:, 128 * k : 128 * k + 128]
            turned.append(
                jnp.concatenate(
                    [(re * cosine + im * sine).astype(BF16), (im * cosine - re * sine).astype(BF16)], 1
                )
            )
        final = dot_nt(right, jnp.concatenate(turned, 0))
        for k in (0, 1):
            stage[pl.ds(2 * pair + k, 256, stride=IC), :] = final[:, 128 * k : 128 * k + 128]
    for v in range(N_STAT):
        for t in range(8):
            row = (v * 8 + t) * IC
            out_ref[v, :, 128 * t : 128 * t + 128] = stage[row : row + IC, :].astype(BF16)


def dft_chunk(signal, tables, chunk):
    full = lambda a: pl.BlockSpec(a.shape, lambda i: (0,) * a.ndim)
    return pl.pallas_call(
        dft_kernel,
        grid=(1,),
        in_specs=[pl.BlockSpec((2, IC, 128, 128), lambda i: (0, chunk, 0, 0))] + [full(t) for t in tables],
        out_specs=pl.BlockSpec((N_STAT, IC, 1024), lambda i: (0, 0, 0)),
        out_shape=jax.ShapeDtypeStruct((N_STAT, IC, 1024), BF16),
        scratch_shapes=[pltpu.VMEM((256 * IC, 128), F32)],
        compiler_params=params(10),
        cost_estimate=cost(1 << 28, 1 << 21),
        name=f"dft_{chunk}",
    )(signal, *tables)


def gram_kernel(*refs):
    out_ref = refs[-1]
    chunks = refs[:-1]
    mine = chunks[-1][...]
    scale = 1.0 / NF
    for c, ref in enumerate(chunks):
        other = ref[...]
        real = dot_nt(mine, other) * scale
        imag = (dot_nt(mine[:, HALF:], other[:, :HALF]) - dot_nt(mine[:, :HALF], other[:, HALF:])) * scale
        for r in range(N_TM):
            out_ref[r, 0, :, ROWS * c : ROWS * c + ROWS] = real[OWN * r : OWN * r + OWN].astype(BF16)
            out_ref[r, 1, :, ROWS * c : ROWS * c + ROWS] = imag[OWN * r : OWN * r + OWN].astype(BF16)


def gram(chunks):
    count = len(chunks)
    return pl.pallas_call(
        gram_kernel,
        in_specs=[VMEM] * count,
        out_specs=VMEM,
        out_shape=jax.ShapeDtypeStruct((N_TM, 2, OWN, ROWS * count), BF16),
        compiler_params=params(8),
        cost_estimate=cost(count << 27, count << 20),
        name=f"gram_{count}",
    )(*chunks)


def mirror_kernel(*refs):
    terms, sums_ref, mirror_ref = refs[:CHUNKS], refs[-2], refs[-1]
    for q in (0, 1):
        sums = []
        for c in range(CHUNKS):
            ref = terms[c]
            if len(ref.shape) == 4:
                total = ref[0, q].astype(F32)
                for t in range(1, N_TM):
                    total = total + ref[t, q].astype(F32)
            else:
                total = ref[q]
            sums.append(total)
            width = ROWS * (c + 1)
            sums_ref[q, OWN * c : OWN * c + OWN, :width] = total
            if width < ROWS * CHUNKS:
                sums_ref[q, OWN * c : OWN * c + OWN, width:] = jnp.zeros((OWN, ROWS * CHUNKS - width), F32)
        sign = -1.0 if q else 1.0
        for c in range(CHUNKS - 1):
            block = [jnp.zeros((OWN * (c + 1), ROWS), F32)]
            block += [sums[k][:, ROWS * c : ROWS * c + ROWS] * sign for k in range(c + 1, CHUNKS)]
            flipped = jnp.concatenate(block, 0).T.astype(BF16)
            for r in range(N_TM):
                mirror_ref[r, q, OWN * c : OWN * c + OWN, :] = flipped[OWN * r : OWN * r + OWN]


def mirror(terms):
    return pl.pallas_call(
        mirror_kernel,
        in_specs=[VMEM] * CHUNKS,
        out_specs=(VMEM, VMEM),
        out_shape=(
            jax.ShapeDtypeStruct((2, OWN * CHUNKS, ROWS * CHUNKS), F32),
            jax.ShapeDtypeStruct((N_TM, 2, OWN * (CHUNKS - 1), OWN * CHUNKS), BF16),
        ),
        compiler_params=params(8),
        cost_estimate=cost(1 << 28, 1 << 22),
        name="mirror",
    )(*terms)


def place_kernel(sums_ref, mirror_ref, wide_ref, narrow_ref, out_ref):
    wide = wide_ref[...]
    narrow = narrow_ref[...]
    lanes = OWN * CHUNKS
    spare = jnp.zeros((OWN, lanes), BF16)
    for q in (0, 1):
        for u in (0, 1):
            part = jnp.concatenate(
                [sums_ref[q, :, ROWS * c + 128 * u : ROWS * c + 128 * u + 128] for c in range(CHUNKS)], 1
            )
            high = part.astype(BF16)
            low = (part - high.astype(F32)).astype(BF16)
            placed = dot_nn(high, wide) + dot_nn(low, wide)
            for w in range(4):
                r = 4 * u + w
                other = jnp.concatenate([mirror_ref[r, q], spare], 0)
                tile = placed[:, 128 * w : 128 * w + 128] + dot_nn(other, narrow)
                for c in range(CHUNKS):
                    for s in range(4):
                        out_ref[q, 32 * s + IC * c : 32 * s + IC * c + IC, 128 * r : 128 * r + 128] = tile[
                            OWN * c + IC * s : OWN * c + IC * s + IC
                        ]


def place(sums, mirrored, wide, narrow):
    return pl.pallas_call(
        place_kernel,
        in_specs=[VMEM] * 4,
        out_specs=VMEM,
        out_shape=jax.ShapeDtypeStruct((2, OWN * CHUNKS, 1024), F32),
        compiler_params=params(8),
        cost_estimate=cost(1 << 28, 1 << 22),
        name="place",
    )(sums, mirrored, wide, narrow)


def beam_kernel(*refs):
    chunks, weight_ref, out_ref = refs[:CHUNKS], refs[CHUNKS], refs[-1]
    total = None
    for p in (0, 1):
        for c in range(CHUNKS):
            column = (p * CHUNKS + c) * ROWS
            term = dot_nn(weight_ref[:, column : column + ROWS], chunks[c][:, HALF * p : HALF * p + HALF])
            total = term if total is None else total + term
    out_ref[...] = total.T.astype(BF16)


def beam_sum(chunks, weights):
    return pl.pallas_call(
        beam_kernel,
        in_specs=[VMEM] * (CHUNKS + 1),
        out_specs=VMEM,
        out_shape=jax.ShapeDtypeStruct((HALF, HALF), BF16),
        compiler_params=params(10),
        cost_estimate=cost(1 << 29, 1 << 22),
        name="beams",
    )(*chunks, weights)


def exchange(array, axes):
    return lax.all_to_all(array, axes, 0, 0, tiled=True)


def to_everyone(array, axes, count):
    return exchange(jnp.broadcast_to(array[None], (count, *array.shape)), axes)


def body(voltages, beam_weights):
    tables = tuple(
        jnp.asarray(t, BF16 if k in (0, 3) else F32) for k, t in enumerate(dft_tables())
    )
    signal = voltages.reshape(2, N_STAT, SPECTRA, 32, 128).transpose(0, 1, 3, 2, 4)
    signal = signal.reshape(2, N_STAT, 128, 128)

    own_piece = lax.axis_index(TM)
    pieces = beam_weights.reshape(N_TM, IC, 256)
    piece = lax.dynamic_index_in_dim(pieces, own_piece, 0, keepdims=False)
    gathered = to_everyone(to_everyone(piece, STAT, N_STAT), TM, N_TM)
    flat = gathered.reshape(2, CHUNKS * ROWS, 256).transpose(0, 2, 1)
    weights = jnp.concatenate(
        [jnp.concatenate([flat[0], -flat[1]], 1), jnp.concatenate([flat[1], flat[0]], 1)], 0
    )

    chunks = []
    terms = []
    for c in range(CHUNKS):
        ready = dft_chunk(signal, tables, c)
        chunks.append(exchange(ready, STAT).reshape(ROWS, 1024))
        terms.append(exchange(gram(chunks), TM))
    terms = [t.astype(F32).sum(0) for t in terms[:-1]] + terms[-1:]
    beams = beam_sum(chunks, weights).reshape(NF // N_STAT, SPECTRA, 2, 256)
    sums, mirrored = mirror(terms)
    mirrored = exchange(mirrored, TM)
    wide = jnp.asarray(natural_order(4), BF16)
    narrow = jnp.asarray(natural_order(1), BF16)
    rows = place(sums, mirrored, wide, narrow)
    return beams, rows.transpose(1, 0, 2)[:, None]


def solution(mesh):
    finer = Mesh(
        mesh.devices.reshape(2, 8, 2, 4, 2), ("stat_0", "stat_1", "stat_2", "tm_0", "tm_1")
    )
    return jax.shard_map(
        body,
        mesh=finer,
        in_specs=(P(None, STAT, TM, None), P(None, STAT, None)),
        out_specs=(P(STAT, TM, None, None), P(TM, STAT, None, None)),
        check_vma=False,
    )
```

time: 224 us -> 215 us (0.960)
  waiting for transfers between devices: 38.6 us -> 89.2 us
  matrix products: 48.3 us -> 0 us
  starting transfers between devices: 7.49 us -> 53.4 us
  blocking collectives: 64.3 us -> 23.8 us
  Pallas kernels: 0 us -> 16.1 us
  between operations: 14.2 us -> 0.94 us
  other arithmetic: 17.8 us -> 5.04 us
  local copies, waits for them, and re-layouts: 28.6 us -> 24.7 us
    all_to_all x1 -> x10, waiting for transfers between devices: 28.4 us -> 89.2 us  [exchange(): return lax.all_to_all(array, axes, 0, 0, tiled=True)]
    dot_general x37 -> x0, matrix products: 48.3 us -> none  [the longest x32 37.2 us: add_block(): jnp.einsum('psic,piqb->csqb', spec_block, weight_block, preferred_element...]
    all_to_all x1 -> x10, starting transfers between devices: 7.41 us -> 53.4 us  [exchange(): return lax.all_to_all(array, axes, 0, 0, tiled=True)]
    all_to_all x2 -> x1, blocking collectives: 64.3 us -> 23.8 us  [exchange(): return lax.all_to_all(array, axes, 0, 0, tiled=True)]
    pallas_call x0 -> x11, Pallas kernels: none -> 16.1 us  [the longest x4 8.99 us: gram(): pl.pallas_call(gram_kernel, in_specs=[VMEM] * count, out_specs=VMEM, out_...]
    unnamed x7 -> x55, local copies, waits for them, and re-layouts: 5.47 us -> 17.7 us
    add x33 -> x0, other arithmetic: 11.6 us -> none  [the longest x32 10.7 us: add_block(): return running + rounded.astype(jnp.float32)]
    reduce_scatter x1 -> x0, waiting for transfers between devices: 10.2 us -> none  [sum_by_axis(): subtotal = lax.psum_scatter(subtotal, axis, scatter_dimension=0, tiled=True)]
  transfers between devices with their start and end apart: 3 -> 10, of which waited for: 2 -> 10; matrix products, arithmetic and copies ran while one was open for 23% -> 4% of each run, Pallas kernels for 0% -> 7%
where the time goes in v1:
time: 215 us; the launch traced here: 213 us
  waiting for transfers between devices  89.2 us (41%)
  starting transfers between devices  53.4 us (25%)
  local copies, waits for them, and re-layouts  24.7 us (11%)
  blocking collectives  23.8 us (11%)
  Pallas kernels  16.1 us (7%)
  other arithmetic  5.04 us (2%)
    all_to_all x10, waiting for transfers between devices, exchange(): return lax.all_to_all(array, axes, 0, 0, tiled=True)  89.2 us
    all_to_all x10, starting transfers between devices, exchange(): return lax.all_to_all(array, axes, 0, 0, tiled=True)  53.4 us
    all_to_all x1, blocking collectives, exchange(): return lax.all_to_all(array, axes, 0, 0, tiled=True)  23.8 us
    unnamed x55, local copies, waits for them, and re-layouts  17.7 us
    pallas_call x4, Pallas kernels, gram(): pl.pallas_call(gram_kernel, in_specs=[VMEM] * count, out_specs=VMEM, out_...  8.99 us
  transfers between devices with their start and end apart: 10, of which 10 were waited for; matrix products, arithmetic and copies ran while one was open for 4% of the time, Pallas kernels for 7%

profile of v1, /device:TPU:64, one launch (start us, length us, event | category | flops | bytes accessed | tf_op | source)
XLA Modules:
  0.0 213.2 jit_solution(16363476034616073928)
XLA Ops:
  2.1 10.7 %all-to-all-start.4 = ((bf16[32,8,256]{2,1,0:T(8,128)(2,1)}), bf16[32,8,256]{2,1,0:T(8,128)(2,1)S(1)}, u32[]{:S(2)}, u32[]{:S(2)}) async-start(bf16[32,8,256]{2,1,0:T(8,128)(2,1)} %broadcast_in_dim.18), calls=%async_computation.4 | async-start | bytes 262144 | tf_op jit(solution)/shard_map/all_to_all | solution.py:246
  12.8 1.6 copy-done.1
  19.4 2.8 %all-to-all-done.4 = bf16[32,8,256]{2,1,0:T(8,128)(2,1)S(1)} async-done(((bf16[32,8,256]{2,1,0:T(8,128)(2,1)}), bf16[32,8,256]{2,1,0:T(8,128)(2,1)S(1)}, u32[]{:S(2)}, u32[]{:S(2)}) %all-to-all-start.4) | async-done | bytes 131104 | tf_op jit(solution)/shard_map/all_to_all | solution.py:246
  22.8 7.1 %all-to-all-start = ((bf16[32,8,1024]{2,1,0:T(8,128)(2,1)}), bf16[32,8,1024]{2,1,0:T(8,128)(2,1)S(1)}, u32[]{:S(2)}, u32[]{:S(2)}) async-start(bf16[32,8,1024]{2,1,0:T(8,128)(2,1)} %copy-done.8), calls=%async_computation | async-start | bytes 1048576 | tf_op jit(solution)/shard_map/all_to_all | solution.py:246
  32.2 14.9 %all-to-all-done = bf16[32,8,1024]{2,1,0:T(8,128)(2,1)S(1)} async-done(((bf16[32,8,1024]{2,1,0:T(8,128)(2,1)}), bf16[32,8,1024]{2,1,0:T(8,128)(2,1)S(1)}, u32[]{:S(2)}, u32[]{:S(2)}) %all-to-all-start) | async-done | bytes 524320 | tf_op jit(solution)/shard_map/all_to_all | solution.py:246
  47.2 6.4 %all-to-all-start.1 = ((bf16[32,8,1024]{2,1,0:T(8,128)(2,1)}), bf16[32,8,1024]{2,1,0:T(8,128)(2,1)S(1)}, u32[]{:S(2)}, u32[]{:S(2)}) async-start(bf16[32,8,1024]{2,1,0:T(8,128)(2,1)} %copy-done.9), calls=%async_computation.1 | async-start | bytes 1048576 | tf_op jit(solution)/shard_map/all_to_all | solution.py:246
  55.9 15.1 %all-to-all-done.1 = bf16[32,8,1024]{2,1,0:T(8,128)(2,1)S(1)} async-done(((bf16[32,8,1024]{2,1,0:T(8,128)(2,1)}), bf16[32,8,1024]{2,1,0:T(8,128)(2,1)S(1)}, u32[]{:S(2)}, u32[]{:S(2)}) %all-to-all-start.1) | async-done | bytes 524320 | tf_op jit(solution)/shard_map/all_to_all | solution.py:246
  71.0 7.1 %all-to-all-start.2 = ((bf16[32,8,1024]{2,1,0:T(8,128)(2,1)}), bf16[32,8,1024]{2,1,0:T(8,128)(2,1)}, u32[]{:S(2)}, u32[]{:S(2)}) async-start(bf16[32,8,1024]{2,1,0:T(8,128)(2,1)} %copy-done.7), calls=%async_computation.2 | async-start | bytes 1048576 | tf_op jit(solution)/shard_map/all_to_all | solution.py:246
  80.4 15.1 %all-to-all-done.2 = bf16[32,8,1024]{2,1,0:T(8,128)(2,1)} async-done(((bf16[32,8,1024]{2,1,0:T(8,128)(2,1)}), bf16[32,8,1024]{2,1,0:T(8,128)(2,1)}, u32[]{:S(2)}, u32[]{:S(2)}) %all-to-all-start.2) | async-done | bytes 524320 | tf_op jit(solution)/shard_map/all_to_all | solution.py:246
  95.5 23.8 %all_to_all.55 = bf16[32,8,1024]{2,1,0:T(8,128)(2,1)S(1)} all-to-all(bf16[32,8,1024]{2,1,0:T(8,128)(2,1)} %copy-done.10), channel_id=1, replica_groups=mesh['stat_0'=2,'stat_1'=8,'stat_2'=2,'tm_0'=4,'tm_1'=2] {'stat_0','stat..., dimensions={0} | all-to-all | bytes 1048576 | tf_op jit(solution)/shard_map/all_to_all | solution.py:246
  119.3 1.9 broadcast_in_dim.19
  121.3 4.5 %all-to-all-start.5 = ((bf16[8,32,8,256]{3,2,1,0:T(8,128)(2,1)}), bf16[8,32,8,256]{3,2,1,0:T(8,128)(2,1)S(1)}, u32[]{:S(2)}, u32[]{:S(2)}) async-start(bf16[8,32,8,256]{3,2,1,0:T(8,128)(2,1)} %broadcast_in_dim.19), calls=%async_computation.5 | async-start | bytes 2097152 | tf_op jit(solution)/shard_map/all_to_all | solution.py:246
  127.0 14.8 %all-to-all-done.5 = bf16[8,32,8,256]{3,2,1,0:T(8,128)(2,1)S(1)} async-done(((bf16[8,32,8,256]{3,2,1,0:T(8,128)(2,1)}), bf16[8,32,8,256]{3,2,1,0:T(8,128)(2,1)S(1)}, u32[]{:S(2)}, u32[]{:S(2)}) %all-to-all-start.5) | async-done | bytes 1048608 | tf_op jit(solution)/shard_map/all_to_all | solution.py:246
  141.7 3.4 %all-to-all-start.6 = ((bf16[8,2,32,256]{3,2,1,0:T(8,128)(2,1)}), bf16[8,2,32,256]{3,2,1,0:T(8,128)(2,1)S(1)}, u32[]{:S(2)}, u32[]{:S(2)}) async-start(bf16[8,2,32,256]{3,2,1,0:T(8,128)(2,1)} %gram_1.1), calls=%async_computation.6 | async-start | bytes 524288 | tf_op jit(solution)/shard_map/all_to_all | solution.py:246
  145.2 1.5 gram_2.1
  146.7 5.7 %all-to-all-done.6 = bf16[8,2,32,256]{3,2,1,0:T(8,128)(2,1)S(1)} async-done(((bf16[8,2,32,256]{3,2,1,0:T(8,128)(2,1)}), bf16[8,2,32,256]{3,2,1,0:T(8,128)(2,1)S(1)}, u32[]{:S(2)}, u32[]{:S(2)}) %all-to-all-start.6) | async-done | bytes 262176 | tf_op jit(solution)/shard_map/all_to_all | solution.py:246
  153.1 3.5 %all-to-all-start.7 = ((bf16[8,2,32,512]{3,2,1,0:T(8,128)(2,1)}), bf16[8,2,32,512]{3,2,1,0:T(8,128)(2,1)S(1)}, u32[]{:S(2)}, u32[]{:S(2)}) async-start(bf16[8,2,32,512]{3,2,1,0:T(8,128)(2,1)} %gram_2.1), calls=%async_computation.7 | async-start | bytes 1048576 | tf_op jit(solution)/shard_map/all_to_all | solution.py:246
  156.6 2.9 %gram_3.1 = bf16[8,2,32,768]{3,2,1,0:T(8,128)(2,1)} custom-call(bf16[256,1024]{1,0:T(8,128)(2,1)S(1)} %bitcast.31, bf16[256,1024]{1,0:T(8,128)(2,1)S(1)} %bitcast.35, bf16[256,1024]{1,0:T(8,128)(2,1)} %bitcast.7.refs_2_), custom_call_target="tpu_custom_call" | custom-call | flops 805306368 | bytes 3145728 | tf_op jit(solution)/shard_map/gram_3/pallas_call | solution.py:134
  159.6 5.8 %all-to-all-done.7 = bf16[8,2,32,512]{3,2,1,0:T(8,128)(2,1)S(1)} async-done(((bf16[8,2,32,512]{3,2,1,0:T(8,128)(2,1)}), bf16[8,2,32,512]{3,2,1,0:T(8,128)(2,1)S(1)}, u32[]{:S(2)}, u32[]{:S(2)}) %all-to-all-start.7) | async-done | bytes 524320 | tf_op jit(solution)/shard_map/all_to_all | solution.py:246
  166.1 3.5 %all-to-all-start.8 = ((bf16[8,2,32,768]{3,2,1,0:T(8,128)(2,1)}), bf16[8,2,32,768]{3,2,1,0:T(8,128)(2,1)S(1)}, u32[]{:S(2)}, u32[]{:S(2)}) async-start(bf16[8,2,32,768]{3,2,1,0:T(8,128)(2,1)} %gram_3.1), calls=%async_computation.8 | async-start | bytes 1572864 | tf_op jit(solution)/shard_map/all_to_all | solution.py:246
  169.7 3.3 %gram_4.1 = bf16[8,2,32,1024]{3,2,1,0:T(8,128)(2,1)} custom-call(bf16[256,1024]{1,0:T(8,128)(2,1)S(1)} %bitcast.32, bf16[256,1024]{1,0:T(8,128)(2,1)S(1)} %bitcast.36, bf16[256,1024]{1,0:T(8,128)(2,1)} %bitcast.7.refs_2_, bf16[256,1024]{1,0:T(8,128)(2,1)S(1)} %bitcast.38), custom_call_target="tpu_custom_call" | custom-call | flops 1073741824 | bytes 4194304 | tf_op jit(solution)/shard_map/gram_4/pallas_call | solution.py:134
  173.0 1.3 copy.13
  174.3 5.8 %all-to-all-done.8 = bf16[8,2,32,768]{3,2,1,0:T(8,128)(2,1)S(1)} async-done(((bf16[8,2,32,768]{3,2,1,0:T(8,128)(2,1)}), bf16[8,2,32,768]{3,2,1,0:T(8,128)(2,1)S(1)}, u32[]{:S(2)}, u32[]{:S(2)}) %all-to-all-start.8) | async-done | bytes 786464 | tf_op jit(solution)/shard_map/all_to_all | solution.py:246
  180.1 3.6 %all-to-all-start.9 = ((bf16[8,2,32,1024]{3,2,1,0:T(8,128)(2,1)}), bf16[8,2,32,1024]{3,2,1,0:T(8,128)(2,1)S(1)}, u32[]{:S(2)}, u32[]{:S(2)}) async-start(bf16[8,2,32,1024]{3,2,1,0:T(8,128)(2,1)} %gram_4.1), calls=%async_computation.9 | async-start | bytes 2097152 | tf_op jit(solution)/shard_map/all_to_all | solution.py:246
  183.7 1.9 fusion
  185.6 2.2 %slice_bitcast_fusion = (bf16[256,1024]{1,0:T(8,128)(2,1)}, bf16[256,1024]{1,0:T(8,128)(2,1)}) fusion(bf16[2,256,1024]{2,1,0:T(8,128)(2,1)} %bitcast.41), kind=kLoop, calls=%fused_computation.3 | loop fusion | bytes 2097152 | tf_op jit(solution)/shard_map/squeeze | solution.py:266
  189.3 6.6 %all-to-all-done.9.refs_3_ = bf16[8,2,32,1024]{3,2,1,0:T(8,128)(2,1)S(1)} async-done(((bf16[8,2,32,1024]{3,2,1,0:T(8,128)(2,1)}), bf16[8,2,32,1024]{3,2,1,0:T(8,128)(2,1)S(1)}, u32[]{:S(2)}, u32[]{:S(2)}) %all-to-all-start.9) | async-done | bytes 1048608 | tf_op jit(solution)/shard_map/all_to_all | solution.py:246
  197.8 3.6 %all-to-all-start.10 = ((bf16[8,2,96,128]{3,2,1,0:T(8,128)(2,1)}), bf16[8,2,96,128]{3,2,1,0:T(8,128)(2,1)S(1)}, u32[]{:S(2)}, u32[]{:S(2)}) async-start(bf16[8,2,96,128]{3,2,1,0:T(8,128)(2,1)} %get-tuple-element.5), calls=%async_computation.10 | async-start | bytes 786432 | tf_op jit(solution)/shard_map/all_to_all | solution.py:246
  201.5 1.7 maximum_maximum_fusion.refs_4_
  203.2 2.4 %beams.1 = bf16[512,512]{1,0:T(8,128)(2,1)S(1)} custom-call(bf16[256,1024]{1,0:T(8,128)(2,1)S(1)} %bitcast.33, bf16[256,1024]{1,0:T(8,128)(2,1)S(1)} %bitcast.37, bf16[256,1024]{1,0:T(8,128)(2,1)} %bitcast.7.refs_2_, bf16[256,1024]{1,0:T(8,128)(2,1)S(1)} %bitcast.39, bf16[512,2048]{1,0:T(8,128)(2,1)S(1)} %maximum_maximum_fusion.refs_4_), custom_call_target="tpu_custom_call" | custom-call | flops 1073741824 | bytes 4194304 | tf_op jit(solution)/shard_map/beams/pallas_call | solution.py:234
  206.6 2.6 %all-to-all-done.10.mirror_ref = bf16[8,2,96,128]{3,2,1,0:T(8,128)(2,1)S(1)} async-done(((bf16[8,2,96,128]{3,2,1,0:T(8,128)(2,1)}), bf16[8,2,96,128]{3,2,1,0:T(8,128)(2,1)S(1)}, u32[]{:S(2)}, u32[]{:S(2)}) %all-to-all-start.10) | async-done | bytes 393248 | tf_op jit(solution)/shard_map/all_to_all | solution.py:246
  211.5 1.8 copy.14
  (66 shorter events, 23.2 us)
Async XLA Ops:
  2.1 20.1 %all-to-all-start.4 = ((bf16[32,8,256]{2,1,0:T(8,128)(2,1)}), bf16[32,8,256]{2,1,0:T(8,128)(2,1)S(1)}, u32[]{:S(2)}, u32[]{:S(2)}) async-start(bf16[32,8,256]{2,1,0:T(8,128)(2,1)} %broadcast_in_dim.18), calls=%async_computation.4 | async-start | bytes 262144 | tf_op jit(solution)/shard_map/all_to_all | solution.py:246
  12.8 1.6 copy-start.1
  14.4 0.9 copy-start.3
  15.3 0.9 copy-start.5
  16.2 0.8 copy-start.13
  17.0 0.8 copy-start.15
  17.9 12.0 %copy-start.2 = (bf16[2,32,4,4096]{3,2,1,0:T(4,128)(2,1)S(1)}, bf16[2,32,4,4096]{3,2,1,0:T(4,128)(2,1)}, u32[]{:S(2)}) copy-start(bf16[2,32,4,4096]{3,2,1,0:T(4,128)(2,1)} %param.8) | copy-start | bytes 6291460
  17.9 12.0 %copy-start.4 = (bf16[256,256]{1,0:T(8,128)(2,1)S(1)}, bf16[256,256]{1,0:T(8,128)(2,1)}, u32[]{:S(2)}) copy-start(bf16[256,256]{1,0:T(8,128)(2,1)} %constant.30.clone.left_ref) | copy-start | bytes 393220
  17.9 12.0 %copy-start.6 = (bf16[256,256]{1,0:T(8,128)(2,1)S(1)}, bf16[256,256]{1,0:T(8,128)(2,1)}, u32[]{:S(2)}) copy-start(bf16[256,256]{1,0:T(8,128)(2,1)} %constant.33.clone.right_ref) | copy-start | bytes 393220
  17.9 12.0 %copy-start.14 = (f32[128,128]{1,0:T(8,128)S(1)}, f32[128,128]{1,0:T(8,128)}, u32[]{:S(2)}) copy-start(f32[128,128]{1,0:T(8,128)} %constant.31.clone.cos_ref) | copy-start | bytes 196612
  18.6 0.8 copy-start.8
  22.8 24.4 %all-to-all-start = ((bf16[32,8,1024]{2,1,0:T(8,128)(2,1)}), bf16[32,8,1024]{2,1,0:T(8,128)(2,1)S(1)}, u32[]{:S(2)}, u32[]{:S(2)}) async-start(bf16[32,8,1024]{2,1,0:T(8,128)(2,1)} %copy-done.8), calls=%async_computation | async-start | bytes 1048576 | tf_op jit(solution)/shard_map/all_to_all | solution.py:246
  29.9 0.8 copy-start.16
  31.4 0.8 copy-start.9
  47.2 23.8 %all-to-all-start.1 = ((bf16[32,8,1024]{2,1,0:T(8,128)(2,1)}), bf16[32,8,1024]{2,1,0:T(8,128)(2,1)S(1)}, u32[]{:S(2)}, u32[]{:S(2)}) async-start(bf16[32,8,1024]{2,1,0:T(8,128)(2,1)} %copy-done.9), calls=%async_computation.1 | async-start | bytes 1048576 | tf_op jit(solution)/shard_map/all_to_all | solution.py:246
  53.6 0.8 copy-start.17
  55.1 0.8 copy-start.7
  71.0 24.5 %all-to-all-start.2 = ((bf16[32,8,1024]{2,1,0:T(8,128)(2,1)}), bf16[32,8,1024]{2,1,0:T(8,128)(2,1)}, u32[]{:S(2)}, u32[]{:S(2)}) async-start(bf16[32,8,1024]{2,1,0:T(8,128)(2,1)} %copy-done.7), calls=%async_computation.2 | async-start | bytes 1048576 | tf_op jit(solution)/shard_map/all_to_all | solution.py:246
  78.1 0.8 copy-start.18
  121.3 20.5 %all-to-all-start.5 = ((bf16[8,32,8,256]{3,2,1,0:T(8,128)(2,1)}), bf16[8,32,8,256]{3,2,1,0:T(8,128)(2,1)S(1)}, u32[]{:S(2)}, u32[]{:S(2)}) async-start(bf16[8,32,8,256]{3,2,1,0:T(8,128)(2,1)} %broadcast_in_dim.19), calls=%async_computation.5 | async-start | bytes 2097152 | tf_op jit(solution)/shard_map/all_to_all | solution.py:246
  141.7 10.6 %all-to-all-start.6 = ((bf16[8,2,32,256]{3,2,1,0:T(8,128)(2,1)}), bf16[8,2,32,256]{3,2,1,0:T(8,128)(2,1)S(1)}, u32[]{:S(2)}, u32[]{:S(2)}) async-start(bf16[8,2,32,256]{3,2,1,0:T(8,128)(2,1)} %gram_1.1), calls=%async_computation.6 | async-start | bytes 524288 | tf_op jit(solution)/shard_map/all_to_all | solution.py:246
  153.1 12.2 %all-to-all-start.7 = ((bf16[8,2,32,512]{3,2,1,0:T(8,128)(2,1)}), bf16[8,2,32,512]{3,2,1,0:T(8,128)(2,1)S(1)}, u32[]{:S(2)}, u32[]{:S(2)}) async-start(bf16[8,2,32,512]{3,2,1,0:T(8,128)(2,1)} %gram_2.1), calls=%async_computation.7 | async-start | bytes 1048576 | tf_op jit(solution)/shard_map/all_to_all | solution.py:246
  166.1 14.0 %all-to-all-start.8 = ((bf16[8,2,32,768]{3,2,1,0:T(8,128)(2,1)}), bf16[8,2,32,768]{3,2,1,0:T(8,128)(2,1)S(1)}, u32[]{:S(2)}, u32[]{:S(2)}) async-start(bf16[8,2,32,768]{3,2,1,0:T(8,128)(2,1)} %gram_3.1), calls=%async_computation.8 | async-start | bytes 1572864 | tf_op jit(solution)/shard_map/all_to_all | solution.py:246
  180.1 5.5 %copy-start.21 = (bf16[8,2,32,768]{3,2,1,0:T(8,128)(2,1)}, bf16[8,2,32,768]{3,2,1,0:T(8,128)(2,1)S(1)}, u32[]{:S(2)}) copy-start(bf16[8,2,32,768]{3,2,1,0:T(8,128)(2,1)S(1)} %all-to-all-done.8) | copy-start | bytes 2359300
  180.1 15.8 %all-to-all-start.9 = ((bf16[8,2,32,1024]{3,2,1,0:T(8,128)(2,1)}), bf16[8,2,32,1024]{3,2,1,0:T(8,128)(2,1)S(1)}, u32[]{:S(2)}, u32[]{:S(2)}) async-start(bf16[8,2,32,1024]{3,2,1,0:T(8,128)(2,1)} %gram_4.1), calls=%async_computation.9 | async-start | bytes 2097152 | tf_op jit(solution)/shard_map/all_to_all | solution.py:246
  183.7 4.2 %copy-start.25 = (bf16[8,2,32,256]{3,2,1,0:T(8,128)(2,1)S(1)}, bf16[8,2,32,256]{3,2,1,0:T(8,128)(2,1)}, u32[]{:S(2)}) copy-start(bf16[8,2,32,256]{3,2,1,0:T(8,128)(2,1)} %copy-done.24) | copy-start | bytes 786436
  183.7 4.2 %copy-start.23 = (bf16[8,2,32,512]{3,2,1,0:T(8,128)(2,1)S(1)}, bf16[8,2,32,512]{3,2,1,0:T(8,128)(2,1)}, u32[]{:S(2)}) copy-start(bf16[8,2,32,512]{3,2,1,0:T(8,128)(2,1)} %copy-done.22) | copy-start | bytes 1572868
  196.9 1.0 copy-start.11
  197.8 11.4 %all-to-all-start.10 = ((bf16[8,2,96,128]{3,2,1,0:T(8,128)(2,1)}), bf16[8,2,96,128]{3,2,1,0:T(8,128)(2,1)S(1)}, u32[]{:S(2)}, u32[]{:S(2)}) async-start(bf16[8,2,96,128]{3,2,1,0:T(8,128)(2,1)} %get-tuple-element.5), calls=%async_computation.10 | async-start | bytes 786432 | tf_op jit(solution)/shard_map/all_to_all | solution.py:246
  203.2 6.0 %copy-start.19 = (bf16[512,512]{1,0:T(8,128)(2,1)S(1)}, bf16[512,512]{1,0:T(8,128)(2,1)}, u32[]{:S(2)}) copy-start(bf16[512,512]{1,0:T(8,128)(2,1)} %constant.34.clone.wide_ref) | copy-start | bytes 1572868
  203.2 6.0 %copy-start.20 = (bf16[128,128]{1,0:T(8,128)(2,1)S(1)}, bf16[128,128]{1,0:T(8,128)(2,1)}, u32[]{:S(2)}) copy-start(bf16[128,128]{1,0:T(8,128)(2,1)} %constant.35.clone.narrow_ref) | copy-start | bytes 98308
  209.2 1.2 copy-start.12
  (5 other events, 3.7 us)

commit v2 on v1

v2 whole, which is shorter than its diff:
```python
import math

import jax
import jax.numpy as jnp
import numpy as np
from jax import lax
from jax.experimental import pallas as pl
from jax.experimental.pallas import tpu as pltpu
from jax.sharding import Mesh
from jax.sharding import PartitionSpec as P


STAT = ("stat_0", "stat_1", "stat_2")
CHIP = ("stat_0", "stat_1")
TM = ("tm_0", "tm_1")
NF = 4096
CHIPS = 16
N_TM = 8
SPECTRA = 4
FIRST, SECOND = 24, 8
SIDE_A, SIDE_B = CHIPS * FIRST, CHIPS * SECOND
OWN_A, OWN_B = SIDE_A // N_TM, SIDE_B // N_TM
COLS_A, COLS_B = 2 * SIDE_A, 2 * SIDE_B
HALF = 512
BF16 = jnp.bfloat16
F32 = jnp.float32
VMEM = pl.BlockSpec(memory_space=pltpu.VMEM)
SMEM = pl.BlockSpec(memory_space=pltpu.SMEM)
ANY = pl.BlockSpec(memory_space=pl.ANY)


def rotation(angle):
    cosine, sine = np.cos(angle), np.sin(angle)
    return np.block([[cosine, sine], [-sine, cosine]])


def dft_tables():
    outer = np.arange(32)
    angle = 2.0 * np.pi * np.outer(outer, outer) / 32
    eye = np.eye(SPECTRA)
    spread = lambda m: np.einsum("wc,st->wsct", m, eye).reshape(128, 128)
    cosine, sine = spread(np.cos(angle)), spread(np.sin(angle))
    left = np.block([[cosine, sine], [-sine, cosine]])
    w0 = np.repeat(np.arange(32), SPECTRA)
    twist = 2.0 * np.pi * np.outer(w0, np.arange(128)) / NF
    inner = 2.0 * np.pi * np.outer(np.arange(128), np.arange(128)) / 128
    right = rotation(inner) / math.sqrt(NF)
    right = right.reshape(2, 32, 4, 256).transpose(1, 0, 2, 3).reshape(256, 256)
    return (
        left.astype(np.float32),
        np.cos(twist).astype(np.float32),
        np.sin(twist).astype(np.float32),
        right.astype(np.float32),
    )


def natural_columns():
    core, chip, item = np.meshgrid(np.arange(2), np.arange(CHIPS), np.arange(32), indexing="ij")
    place = 32 * (2 * chip + core) + item
    return np.concatenate([place[:, :, :FIRST].reshape(-1), place[:, :, FIRST:].reshape(-1)])


def params(mib):
    return pltpu.CompilerParams(vmem_limit_bytes=mib * 1024 * 1024)


def cost(macs, moved):
    return pl.CostEstimate(flops=2 * macs, bytes_accessed=moved, transcendentals=0)


def dot_nn(a, b):
    return lax.dot_general(a, b, (((1,), (0,)), ((), ())), preferred_element_type=F32)


def dot_nt(a, b):
    return lax.dot_general(a, b, (((1,), (1,)), ((), ())), preferred_element_type=F32)


def dft_kernel(place_ref, x_ref, left_ref, cos_ref, sin_ref, right_ref, out_ref, stage):
    count = x_ref.shape[1]
    core = place_ref[0]
    left = left_ref[...]
    right = right_ref[...]
    cosine = cos_ref[...]
    sine = sin_ref[...]
    for pair in range(count // 2):
        signal = [jnp.concatenate([x_ref[0, 2 * pair + k], x_ref[1, 2 * pair + k]], 0) for k in (0, 1)]
        first = dot_nn(left, jnp.concatenate(signal, 1))
        turned = []
        for k in (0, 1):
            re = first[:128, 128 * k : 128 * k + 128]
            im = first[128:, 128 * k : 128 * k + 128]
            turned.append(
                jnp.concatenate(
                    [(re * cosine + im * sine).astype(BF16), (im * cosine - re * sine).astype(BF16)], 1
                )
            )
        final = dot_nt(right, jnp.concatenate(turned, 0))
        for k in (0, 1):
            stage[pl.ds(2 * pair + k, 256, stride=count), :] = final[:, 128 * k : 128 * k + 128]
    for chip in range(CHIPS):
        for side in (0, 1):
            for t in range(8):
                row = ((2 * chip + side) * 8 + t) * count
                out_ref[chip, side ^ core, :, 128 * t : 128 * t + 128] = stage[row : row + count, :].astype(BF16)


def dft_part(place, signal, tables, count, index):
    full = lambda a: pl.BlockSpec(a.shape, lambda i: (0,) * a.ndim)
    return pl.pallas_call(
        dft_kernel,
        grid=(1,),
        in_specs=[SMEM, pl.BlockSpec((2, count, 128, 128), lambda i: (0, index, 0, 0))]
        + [full(t) for t in tables],
        out_specs=pl.BlockSpec((CHIPS, 2, count, 1024), lambda i: (0, 0, 0, 0)),
        out_shape=jax.ShapeDtypeStruct((CHIPS, 2, count, 1024), BF16),
        scratch_shapes=[pltpu.VMEM((256 * count, 128), F32)],
        compiler_params=params(16),
        cost_estimate=cost(count << 25, count << 17),
    )(place, signal, *tables)


def put_sides(core, kept, swapped, out_ref):
    side = kept.shape[0]
    out_ref[pl.ds(pl.multiple_of(core * side, side), side), :] = kept
    out_ref[pl.ds(pl.multiple_of((1 - core) * side, side), side), :] = swapped


def product(rows, cols):
    scale = 1.0 / NF
    real = dot_nt(rows, cols) * scale
    imag = (dot_nt(rows[:, HALF:], cols[:, :HALF]) - dot_nt(rows[:, :HALF], cols[:, HALF:])) * scale
    return real, imag


def gram_first_kernel(place_ref, kept_ref, swapped_ref, spec_ref, *rest):
    out_refs, full = rest[:N_TM], rest[N_TM]
    put_sides(place_ref[0], kept_ref[...], swapped_ref[...], spec_ref)
    own = place_ref[1]
    for a in (0, 1):
        width = SIDE_A * (a + 1)
        start = SIDE_A * a
        values = product(spec_ref[start : start + SIDE_A, :], spec_ref[:width, :])
        for q in (0, 1):
            full[q, :, start : start + width] = values[q].astype(BF16)
    for k in range(N_TM):
        row = pl.multiple_of((own ^ k) * OWN_A, OWN_A)
        for q in (0, 1):
            out_refs[k][q] = full[q, pl.ds(row, OWN_A), :]


def gram_first(place, kept, swapped):
    width = 3 * SIDE_A
    return pl.pallas_call(
        gram_first_kernel,
        in_specs=[SMEM, VMEM, VMEM],
        out_specs=(VMEM,) * (N_TM + 1),
        out_shape=(jax.ShapeDtypeStruct((COLS_A, 1024), BF16),)
        + (jax.ShapeDtypeStruct((2, OWN_A, width), BF16),) * N_TM,
        scratch_shapes=[pltpu.VMEM((2, SIDE_A, width), BF16)],
        compiler_params=params(16),
        cost_estimate=cost(1 << 30, 6 << 20),
        name="gram_first",
    )(place, kept, swapped)


def gram_second_kernel(place_ref, kept_ref, swapped_ref, first_ref, spec_ref, out_ref):
    put_sides(place_ref[0], kept_ref[...], swapped_ref[...], spec_ref)
    mine = spec_ref[...]
    against_first = product(mine, first_ref[...])
    against_second = product(mine, mine)
    for q in (0, 1):
        flipped = against_first[q].T
        flipped = (-flipped if q else flipped).astype(BF16)
        blocks = [against_first[q][:, COLS_B * j : COLS_B * j + COLS_B].astype(BF16) for j in range(3)]
        blocks.append(against_second[q].astype(BF16))
        for r in range(N_TM):
            for j in range(4):
                for a in (0, 1):
                    row = 2 * OWN_B * j + OWN_B * a
                    src = SIDE_B * a + OWN_B * r
                    out_ref[r, q, row : row + OWN_B, :] = blocks[j][src : src + OWN_B]
            for a in (0, 1):
                row = 8 * OWN_B + OWN_A * a
                src = SIDE_A * a + OWN_A * r
                out_ref[r, q, row : row + OWN_A, :] = flipped[src : src + OWN_A]


def gram_second(place, kept, swapped, first):
    rows = 8 * OWN_B + 2 * OWN_A
    return pl.pallas_call(
        gram_second_kernel,
        in_specs=[SMEM, VMEM, VMEM, VMEM],
        out_specs=(VMEM, VMEM),
        out_shape=(
            jax.ShapeDtypeStruct((COLS_B, 1024), BF16),
            jax.ShapeDtypeStruct((N_TM, 2, rows, COLS_B), BF16),
        ),
        compiler_params=params(20),
        cost_estimate=cost(1 << 29, 6 << 20),
        name="gram_second",
    )(place, kept, swapped, first)


def mirror_kernel(place_ref, *refs):
    terms, sums_ref, mirror_refs, flip = refs[:N_TM], refs[N_TM + 1], refs[N_TM + 2 : -1], refs[-1]
    own = place_ref[1]
    for q in (0, 1):
        total = terms[0][q].astype(F32)
        for k in range(1, N_TM):
            total = total + terms[k][q].astype(F32)
        sums_ref[q, :OWN_A, :SIDE_A] = total[:, :SIDE_A]
        sums_ref[q, :OWN_A, SIDE_A:] = jnp.zeros((OWN_A, SIDE_A), F32)
        sums_ref[q, OWN_A:, :] = total[:, SIDE_A:]
        block = total[:, SIDE_A : 2 * SIDE_A] * (-1.0 if q else 1.0)
        block = jnp.concatenate([block, jnp.zeros((128 - OWN_A, SIDE_A), F32)], 0)
        flip[q] = block.T
        for k in range(1, N_TM):
            row = pl.multiple_of((own ^ k) * OWN_A, OWN_A)
            mirror_refs[k][q] = flip[q, pl.ds(row, OWN_A), :].astype(BF16)
        row = pl.multiple_of(own * OWN_A, OWN_A)
        mirror_refs[0][q] = flip[q, pl.ds(row, OWN_A), :].astype(BF16)


def mirror(place, terms, after):
    return pl.pallas_call(
        mirror_kernel,
        in_specs=[SMEM] + [VMEM] * N_TM + [ANY],
        out_specs=(VMEM,) * (N_TM + 1),
        out_shape=(jax.ShapeDtypeStruct((2, 2 * OWN_A, COLS_A), F32),)
        + (jax.ShapeDtypeStruct((2, OWN_A, 128), BF16),) * N_TM,
        scratch_shapes=[pltpu.VMEM((2, SIDE_A, 128), F32)],
        compiler_params=params(8),
        cost_estimate=cost(1 << 27, 1 << 21),
        name="mirror",
    )(place, *terms, after)


def spread_kernel(place_ref, sums_ref, order_ref, narrow_ref, *refs):
    mirrors, out_ref = refs[:N_TM], refs[-1]
    own = place_ref[1]
    order = order_ref[:COLS_A, :]
    narrow = narrow_ref[...]
    for q in (0, 1):
        total = sums_ref[q]
        high = total.astype(BF16)
        low = (total - high.astype(F32)).astype(BF16)
        out_ref[q] = dot_nn(high, order) + dot_nn(low, order)
        for k in range(N_TM):
            col = pl.multiple_of((own ^ k) * 128, 128)
            out_ref[q, :OWN_A, pl.ds(col, 128)] += dot_nn(mirrors[k][q], narrow)


def spread_first(place, sums, order, narrow, mirrors):
    return pl.pallas_call(
        spread_kernel,
        in_specs=[SMEM] + [VMEM] * (N_TM + 3),
        out_specs=VMEM,
        out_shape=jax.ShapeDtypeStruct((2, 2 * OWN_A, 1024), F32),
        compiler_params=params(8),
        cost_estimate=cost(1 << 28, 1 << 22),
        name="spread_first",
    )(place, sums, order, narrow, *mirrors)


def finish_kernel(terms_ref, base_ref, order_ref, out_ref):
    order = order_ref[...]
    for q in (0, 1):
        total = terms_ref[0, q].astype(F32)
        for t in range(1, N_TM):
            total = total + terms_ref[t, q].astype(F32)
        rows_b = 2 * OWN_B
        last = jnp.concatenate([total[rows_b * j : rows_b * j + rows_b] for j in range(4)], 1)
        extra = total[4 * rows_b :]

        def placed(value, table):
            high = value.astype(BF16)
            low = (value - high.astype(F32)).astype(BF16)
            return dot_nn(high, table) + dot_nn(low, table)

        lower = placed(last, order)
        upper = base_ref[q] + placed(extra, order[COLS_A:])
        for a in (0, 1):
            for chip in (0, 1):
                row = 64 * chip + 32 * a
                src = OWN_A * a + FIRST * chip
                out_ref[q, row : row + FIRST, :] = upper[src : src + FIRST]
                src = OWN_B * a + SECOND * chip
                out_ref[q, row + FIRST : row + 32, :] = lower[src : src + SECOND]


def finish(terms, base, order):
    return pl.pallas_call(
        finish_kernel,
        in_specs=[VMEM] * 3,
        out_specs=VMEM,
        out_shape=jax.ShapeDtypeStruct((2, 128, 1024), F32),
        compiler_params=params(8),
        cost_estimate=cost(1 << 28, 1 << 22),
        name="finish",
    )(terms, base, order)


def weight_kernel(place_ref, *refs):
    blocks, out_ref, rows_a, rows_b = refs[:N_TM], refs[N_TM], refs[-2], refs[-1]
    core, own, far, z = place_ref[0], place_ref[1], place_ref[2], place_ref[3]
    for k in range(N_TM):
        source = (z - (own ^ k)) & 7
        for dx in (0, 1):
            for dc in (0, 1):
                chip = (far ^ dx) * 8 + source
                side = core ^ dc
                row_a = pl.multiple_of(side * SIDE_A + chip * FIRST, 8)
                row_b = pl.multiple_of(side * SIDE_B + chip * SECOND, 8)
                for p in (0, 1):
                    block = blocks[k][dx, dc, p].astype(F32)
                    rows_a[p, pl.ds(row_a, FIRST), :] = block[:FIRST]
                    rows_b[p, pl.ds(row_b, SECOND), :] = block[FIRST:]
    for p in (0, 1):
        flipped = jnp.concatenate([rows_a[p].T, rows_b[p].T], 1)
        straight = flipped.astype(BF16)
        out_ref[:256, 1024 * p : 1024 * p + 1024] = (-flipped).astype(BF16) if p else straight
        out_ref[256:, 1024 * (1 - p) : 1024 * (1 - p) + 1024] = straight


def weight_stack(place, blocks):
    return pl.pallas_call(
        weight_kernel,
        in_specs=[SMEM] + [VMEM] * N_TM,
        out_specs=VMEM,
        out_shape=jax.ShapeDtypeStruct((HALF, 2048), BF16),
        scratch_shapes=[pltpu.VMEM((2, COLS_A, 256), F32), pltpu.VMEM((2, COLS_B, 256), F32)],
        compiler_params=params(12),
        cost_estimate=cost(1 << 27, 1 << 22),
        name="weights",
    )(place, *blocks)


def beam_kernel(first_ref, second_ref, weight_ref, after_ref, out_ref):
    total = None
    for p in (0, 1):
        lanes = slice(HALF * p, HALF * p + HALF)
        middle = 1024 * p + COLS_A
        term = dot_nn(weight_ref[:, 1024 * p : middle], first_ref[:, lanes])
        term = term + dot_nn(weight_ref[:, middle : middle + COLS_B], second_ref[:, lanes])
        total = term if total is None else total + term
    out_ref[...] = total.T.astype(BF16)


def beam_sum(first, second, weights, after):
    return pl.pallas_call(
        beam_kernel,
        in_specs=[VMEM] * 3 + [ANY],
        out_specs=VMEM,
        out_shape=jax.ShapeDtypeStruct((HALF, HALF), BF16),
        compiler_params=params(12),
        cost_estimate=cost(1 << 29, 1 << 22),
        name="beams",
    )(first, second, weights, after)


def swap(array, axis):
    return lax.ppermute(array, axis, [(0, 1), (1, 0)])


def with_partners(array):
    pairs = lambda k: [(i, i ^ k) for i in range(N_TM)]
    return [array] + [lax.ppermute(array, TM, pairs(k)) for k in range(1, N_TM)]


def to_partners(arrays):
    pairs = lambda k: [(i, i ^ k) for i in range(N_TM)]
    return [arrays[0]] + [lax.ppermute(arrays[k], TM, pairs(k)) for k in range(1, N_TM)]


def turn(ready, count):
    arrived = lax.all_to_all(ready, CHIP, 0, 0, tiled=True)
    kept = arrived[:, 0].reshape(CHIPS * count, 1024)
    other = arrived[:, 1].reshape(CHIPS * count, 1024)
    swapped = swap(other, "stat_2")
    return kept, swapped


def behind(value, other):
    return lax.optimization_barrier((value, other))[0]


def step(voltages, beam_weights):
    tables = tuple(jnp.asarray(t, BF16 if k in (0, 3) else F32) for k, t in enumerate(dft_tables()))
    signal = voltages.reshape(2, 32, SPECTRA, 32, 128).transpose(0, 1, 3, 2, 4)
    signal = signal.reshape(2, 32, 128, 128)
    where = ("stat_2", TM, "stat_0", "stat_1")
    place = jnp.stack([lax.axis_index(a) for a in where]).astype(jnp.int32)

    ready_a = dft_part(place, signal, tables, FIRST, 0)
    ready_b = dft_part(place, signal, tables, SECOND, FIRST // SECOND)

    block = behind(beam_weights, ready_b)
    ring = [(z * N_TM + t, (z + t) % 8 * N_TM + t) for z in range(8) for t in range(N_TM)]
    block = lax.ppermute(block, ("stat_1", *TM), ring)
    block = jnp.stack([block, swap(block, "stat_2")])
    block = jnp.stack([block, swap(block, "stat_0")])
    blocks_k = with_partners(block)
    weights = weight_stack(place, blocks_k)
    columns = behind(jnp.asarray(natural_columns(), jnp.int32), ready_b)
    order = (columns[:, None] == jnp.arange(1024, dtype=jnp.int32)[None, :]).astype(BF16)
    item = np.arange(128)
    target = np.where(item < OWN_A, 64 * (item // FIRST) + 32 + item % FIRST, -1)
    narrow = jnp.asarray((target[:, None] == item[None, :]), BF16)

    kept_a, swapped_a = turn(ready_a, FIRST)
    kept_b, swapped_b = turn(ready_b, SECOND)
    first, *terms = gram_first(place, kept_a, swapped_a)
    arrived = to_partners(terms)
    second, blocks = gram_second(place, kept_b, swapped_b, first)
    last = lax.all_to_all(blocks, TM, 0, 0, tiled=True)

    sums, *mirrors = mirror(place, arrived, blocks)
    mirrors = to_partners(mirrors)
    base = spread_first(place, sums, order, narrow, mirrors)
    beams = beam_sum(first, second, weights, blocks)
    beams = beams.reshape(NF // 32, SPECTRA, 2, 256)
    rows = finish(last, base, order)
    return beams, rows.transpose(1, 0, 2)[:, None]


def solution(mesh):
    finer = Mesh(
        mesh.devices.reshape(2, 8, 2, 4, 2), ("stat_0", "stat_1", "stat_2", "tm_0", "tm_1")
    )
    return jax.shard_map(
        step,
        mesh=finer,
        in_specs=(P(None, STAT, TM, None), P(None, STAT, None)),
        out_specs=(P(STAT, TM, None, None), P(TM, STAT, None, None)),
        check_vma=False,
    )
```

time: 215 us -> 193 us (0.90)
  the two profiles are of different devices: /device:TPU:64 before, /device:TPU:2 now
where the time goes in v2:
time: 193 us; the launch traced here: 192 us
  waiting for transfers between devices  92.4 us (48%)
  starting transfers between devices  57.3 us (30%)
  local copies, waits for them, and re-layouts  21.1 us (11%)
  Pallas kernels  20.1 us (10%)
    all_to_all x2, waiting for transfers between devices, turn(): arrived = lax.all_to_all(ready, CHIP, 0, 0, tiled=True)  53 us
    ppermute x14, starting transfers between devices, to_partners(): lax.ppermute(arrays[k], TM, pairs(k))  23.4 us
    unnamed x65, local copies, waits for them, and re-layouts  18.6 us
    ppermute x14, waiting for transfers between devices, to_partners(): lax.ppermute(arrays[k], TM, pairs(k))  17.1 us
    all_to_all x2, starting transfers between devices, turn(): arrived = lax.all_to_all(ready, CHIP, 0, 0, tiled=True)  15.3 us
    ppermute x4, waiting for transfers between devices, swap(): return lax.ppermute(array, axis, [(0, 1), (1, 0)])  13 us
    ppermute x7, starting transfers between devices, with_partners(): return [array] + [lax.ppermute(array, TM, pairs(k)) for k in range(1, N_TM)]  8.51 us
    all_to_all x1, starting transfers between devices, step(): last = lax.all_to_all(blocks, TM, 0, 0, tiled=True)  6.06 us
  transfers between devices with their start and end apart: 29, of which 10 were waited for; matrix products, arithmetic and copies ran while one was open for 1% of the time, Pallas kernels for 6%

profile of v2, /device:TPU:2, one launch (start us, length us, event | category | flops | bytes accessed | tf_op | source)
XLA Modules:
  0.0 192.3 jit_solution(9314358201271750455)
XLA Ops:
  0.7 1.6 copy-done
  5.8 2.0 %shard_map.95 = bf16[16,2,24,1024]{3,2,1,0:T(8,128)(2,1)S(1)} custom-call(s32[4]{0:T(128)S(1)} %pad_add_fusion.place_ref, bf16[2,32,128,128]{3,2,1,0:T(8,128)(2,1)S(1)} %bitcast.24, bf16[256,256]{1,0:T(8,128)(2,1)S(1)} %copy-done.9, f32[128,128]{1,0:T(8,128)S(1)} %copy-done.13, f32[128,128]{1,0:T(8,128)S(1)} %copy-done.11, bf16[256,256]{1,0:T(8,128)(2,1)S(1)} %copy-done.7), custom_call_target="tpu_custom_call" | custom-call | flops 1610612736 | bytes 3145728 | tf_op jit(solution)/shard_map/pallas_call | solution.py:110
  9.0 10.3 %all-to-all-start = ((bf16[16,2,24,1024]{3,2,1,0:T(8,128)(2,1)}), bf16[16,2,24,1024]{3,2,1,0:T(8,128)(2,1)}, u32[]{:S(2)}, u32[]{:S(2)}) async-start(bf16[16,2,24,1024]{3,2,1,0:T(8,128)(2,1)} %copy-done.2), calls=%async_computation | async-start | bytes 3145728 | tf_op jit(solution)/shard_map/all_to_all | solution.py:377
  19.3 2.0 %shard_map.96 = bf16[16,2,8,1024]{3,2,1,0:T(8,128)(2,1)} custom-call(s32[4]{0:T(128)S(1)} %pad_add_fusion.place_ref, bf16[2,32,128,128]{3,2,1,0:T(8,128)(2,1)S(1)} %bitcast.25, bf16[256,256]{1,0:T(8,128)(2,1)S(1)} %copy-done.10, f32[128,128]{1,0:T(8,128)S(1)} %copy-done.14, f32[128,128]{1,0:T(8,128)S(1)} %copy-done.12, bf16[256,256]{1,0:T(8,128)(2,1)S(1)} %copy-done.8), custom_call_target="tpu_custom_call" | custom-call | flops 536870912 | bytes 1048576 | tf_op jit(solution)/shard_map/pallas_call | solution.py:110
  21.3 37.6 %all-to-all-done = bf16[16,2,24,1024]{3,2,1,0:T(8,128)(2,1)} async-done(((bf16[16,2,24,1024]{3,2,1,0:T(8,128)(2,1)}), bf16[16,2,24,1024]{3,2,1,0:T(8,128)(2,1)}, u32[]{:S(2)}, u32[]{:S(2)}) %all-to-all-start) | async-done | bytes 1572896 | tf_op jit(solution)/shard_map/all_to_all | solution.py:377
  58.9 5.0 %all-to-all-start.1 = ((bf16[16,2,8,1024]{3,2,1,0:T(8,128)(2,1)}), bf16[16,2,8,1024]{3,2,1,0:T(8,128)(2,1)S(1)}, u32[]{:S(2)}, u32[]{:S(2)}) async-start(bf16[16,2,8,1024]{3,2,1,0:T(8,128)(2,1)} %shard_map.96), calls=%async_computation.1 | async-start | bytes 1048576 | tf_op jit(solution)/shard_map/all_to_all | solution.py:377
  63.9 1.5 fusion.2
  65.5 15.5 %all-to-all-done.1 = bf16[16,2,8,1024]{3,2,1,0:T(8,128)(2,1)S(1)} async-done(((bf16[16,2,8,1024]{3,2,1,0:T(8,128)(2,1)}), bf16[16,2,8,1024]{3,2,1,0:T(8,128)(2,1)S(1)}, u32[]{:S(2)}, u32[]{:S(2)}) %all-to-all-start.1) | async-done | bytes 524320 | tf_op jit(solution)/shard_map/all_to_all | solution.py:377
  81.1 3.7 %gram_first.1 = (bf16[768,1024]{1,0:T(8,128)(2,1)S(1)}, bf16[2,48,1152]{2,1,0:T(8,128)(2,1)S(1)}, bf16[2,48,1152]{2,1,0:T(8,128)(2,1)}, bf16[2,48,1152]{2,1,0:T(...) custom-call(s32[4]{0:T(128)S(1)} %pad_add_fusion.place_ref, ...), custom_call_target="tpu_custom_call" | custom-call | flops 2147483648 | bytes 6291456 | tf_op jit(solution)/shard_map/gram_first/pallas_call | solution.py:154
  84.9 3.1 %gram_second.1 = (bf16[256,1024]{1,0:T(8,128)(2,1)S(1)}, bf16[8,2,224,256]{3,2,1,0:T(8,128)(2,1)}) custom-call(s32[4]{0:T(128)S(1)} %pad_add_fusion.place_ref, bf16[128,1024]{1,0:T(8,128)(2,1)S(1)} %get-tuple-element.51.kept_ref, bf16[128,1024]{1,0:T(8,128)(2,1)S(1)} %collective-permute-done.1.swapped_ref, bf16[768,1024]{1,0:T(8,128)(2,1)S(1)} %get-tuple-element.24.first_ref), custom_call_target="tpu_custom_call" | custom-call | flops 1073741824 | bytes 6291456 | tf_op jit(solution)/shard_map/gram_second/pallas_call | solution.py:191
  89.9 6.1 %all-to-all-start.2 = ((bf16[8,2,224,256]{3,2,1,0:T(8,128)(2,1)}), bf16[8,2,224,256]{3,2,1,0:T(8,128)(2,1)}, u32[]{:S(2)}, u32[]{:S(2)}) async-start(bf16[8,2,224,256]{3,2,1,0:T(8,128)(2,1)} %get-tuple-element.27.after_ref.refs_8_), calls=%async_computation.2 | async-start | bytes 3670016 | tf_op jit(solution)/shard_map/all_to_all | solution.py:416
  96.0 3.0 %collective-permute-start.2 = (bf16[2,32,256]{2,1,0:T(8,128)(2,1)S(1)}, bf16[2,32,256]{2,1,0:T(8,128)(2,1)S(1)}, u32[]{:S(2)}, u32[]{:S(2)}) collective-permute-start(bf16[2,32,256]{2,1,0:T(8,128)(2,1)S(1)} %copy-done.31), channel_id=1, source_target_pairs={{0,0},{1,17},{2,34},{3,51},{4,68},{5,85},{6,102},{7,119},{16,16},{... | collective-permute-start | bytes 98312 | tf_op jit(solution)/shard_map/ppermute | solution.py:400
  99.0 4.0 %collective-permute-done.2 = bf16[2,32,256]{2,1,0:T(8,128)(2,1)S(1)} collective-permute-done((bf16[2,32,256]{2,1,0:T(8,128)(2,1)S(1)}, bf16[2,32,256]{2,1,0:T(8,128)(2,1)S(1)}, u32[]{:S(2)}, u32[]{:S(2)}) %collective-permute-start.2) | collective-permute-done | bytes 32800 | tf_op jit(solution)/shard_map/ppermute | solution.py:400
  105.1 3.7 %collective-permute-start.13 = (bf16[2,48,1152]{2,1,0:T(8,128)(2,1)}, bf16[2,48,1152]{2,1,0:T(8,128)(2,1)S(1)}, u32[]{:S(2)}, u32[]{:S(2)}) collective-permute-start(bf16[2,48,1152]{2,1,0:T(8,128)(2,1)} %get-tuple-element.30), channel_id=1, source_target_pairs={{0,2},{1,3},{2,0},{3,1},{4,6},{5,7},{6,4},{7,5},{8,10},{9,11},{10,... | collective-permute-start | bytes 663560 | tf_op jit(solution)/shard_map/ppermute | solution.py:373
  108.8 11.8 %collective-permute-done.4 = bf16[2,2,32,256]{3,2,1,0:T(8,128)(2,1)S(1)} collective-permute-done((bf16[2,2,32,256]{3,2,1,0:T(8,128)(2,1)S(1)}, bf16[2,2,32,256]{3,2,1,0:T(8,128)(2,1)S(1)}, u32[]{:S(2)}, u32[]{:S(2)}) %collective-permute-start.4) | collective-permute-done | bytes 65568 | tf_op jit(solution)/shard_map/ppermute | solution.py:363
  120.6 2.5 %collective-permute-start.11 = (bf16[2,2,2,32,256]{4,3,2,1,0:T(8,128)(2,1)S(1)}, bf16[2,2,2,32,256]{4,3,2,1,0:T(8,128)(2,1)S(1)}, u32[]{:S(2)}, u32[]{:S(2)}) collective-permute-start(bf16[2,2,2,32,256]{4,3,2,1,0:T(8,128)(2,1)S(1)} %pad_maximum_fusion.refs_0_), channel_id=1, source_target_pairs={{0,7},{1,6},{2,5},{3,4},{4,3},{5,2},{6,1},{7,0},{8,15},{9,14},{10,... | collective-permute-start | bytes 393224 | tf_op jit(solution)/shard_map/ppermute | solution.py:368
  124.2 5.0 %collective-permute-done.11.refs_7_ = bf16[2,2,2,32,256]{4,3,2,1,0:T(8,128)(2,1)S(1)} collective-permute-done((bf16[2,2,2,32,256]{4,3,2,1,0:T(8,128)(2,1)S(1)}, bf16[2,2,2,32,256]{4,3,2,1,0:T(8,128)(2,1)S(1)}, u32[]{:S(2)}, u32[]{:S(2)}) %collective-permute-start.11) | collective-permute-done | bytes 131104 | tf_op jit(solution)/shard_map/ppermute | solution.py:368
  130.8 2.8 %collective-permute-start.16 = (bf16[2,48,1152]{2,1,0:T(8,128)(2,1)S(1)}, bf16[2,48,1152]{2,1,0:T(8,128)(2,1)S(1)}, u32[]{:S(2)}, u32[]{:S(2)}) collective-permute-start(bf16[2,48,1152]{2,1,0:T(8,128)(2,1)S(1)} %get-tuple-element.33), channel_id=1, source_target_pairs={{0,5},{1,4},{2,7},{3,6},{4,1},{5,0},{6,3},{7,2},{8,13},{9,12},{10,... | collective-permute-start | bytes 663560 | tf_op jit(solution)/shard_map/ppermute | solution.py:373
  133.6 1.7 collective-permute-start.17
  135.2 1.7 collective-permute-start.18
  137.6 13.5 %collective-permute-done.15.refs_4_ = bf16[2,48,1152]{2,1,0:T(8,128)(2,1)S(1)} collective-permute-done((bf16[2,48,1152]{2,1,0:T(8,128)(2,1)S(1)}, bf16[2,48,1152]{2,1,0:T(8,128)(2,1)S(1)}, u32[]{:S(2)}, u32[]{:S(2)}) %collective-permute-start.15) | collective-permute-done | bytes 221216 | tf_op jit(solution)/shard_map/ppermute | solution.py:373
  151.6 1.9 collective-permute-start.7
  153.5 3.5 %collective-permute-done.17.refs_6_ = bf16[2,48,1152]{2,1,0:T(8,128)(2,1)S(1)} collective-permute-done((bf16[2,48,1152]{2,1,0:T(8,128)(2,1)S(1)}, bf16[2,48,1152]{2,1,0:T(8,128)(2,1)S(1)}, u32[]{:S(2)}, u32[]{:S(2)}) %collective-permute-start.17) | collective-permute-done | bytes 221216 | tf_op jit(solution)/shard_map/ppermute | solution.py:373
  157.0 2.8 %collective-permute-start.5 = (bf16[2,2,2,32,256]{4,3,2,1,0:T(8,128)(2,1)S(1)}, bf16[2,2,2,32,256]{4,3,2,1,0:T(8,128)(2,1)S(1)}, u32[]{:S(2)}, u32[]{:S(2)}) collective-permute-start(bf16[2,2,2,32,256]{4,3,2,1,0:T(8,128)(2,1)S(1)} %pad_maximum_fusion.refs_0_), channel_id=1, source_target_pairs={{0,1},{1,0},{2,3},{3,2},{4,5},{5,4},{6,7},{7,6},{8,9},{9,8},{10,11... | collective-permute-start | bytes 393224 | tf_op jit(solution)/shard_map/ppermute | solution.py:368
  160.3 1.5 mirror.1
  164.4 2.2 %collective-permute-start.21 = (bf16[2,48,128]{2,1,0:T(8,128)(2,1)}, bf16[2,48,128]{2,1,0:T(8,128)(2,1)S(1)}, u32[]{:S(2)}, u32[]{:S(2)}) collective-permute-start(bf16[2,48,128]{2,1,0:T(8,128)(2,1)} %get-tuple-element.41), channel_id=1, source_target_pairs={{0,3},{1,2},{2,1},{3,0},{4,7},{5,6},{6,5},{7,4},{8,11},{9,10},{10,... | collective-permute-start | bytes 73736 | tf_op jit(solution)/shard_map/ppermute | solution.py:373
  166.7 2.0 %collective-permute-start.22 = (bf16[2,48,128]{2,1,0:T(8,128)(2,1)}, bf16[2,48,128]{2,1,0:T(8,128)(2,1)S(1)}, u32[]{:S(2)}, u32[]{:S(2)}) collective-permute-start(bf16[2,48,128]{2,1,0:T(8,128)(2,1)} %get-tuple-element.42), channel_id=1, source_target_pairs={{0,4},{1,5},{2,6},{3,7},{4,0},{5,1},{6,2},{7,3},{8,12},{9,13},{10,... | collective-permute-start | bytes 73736 | tf_op jit(solution)/shard_map/ppermute | solution.py:373
  169.9 1.8 collective-permute-start.24
  172.3 2.7 %collective-permute-start.25 = (bf16[2,48,128]{2,1,0:T(8,128)(2,1)S(1)}, bf16[2,48,128]{2,1,0:T(8,128)(2,1)S(1)}, u32[]{:S(2)}, u32[]{:S(2)}) collective-permute-start(bf16[2,48,128]{2,1,0:T(8,128)(2,1)S(1)} %get-tuple-element.45), channel_id=1, source_target_pairs={{0,7},{1,6},{2,5},{3,4},{4,3},{5,2},{6,1},{7,0},{8,15},{9,14},{10,... | collective-permute-start | bytes 73736 | tf_op jit(solution)/shard_map/ppermute | solution.py:373
  185.3 1.8 spread_first.1.base_ref
  187.1 3.4 %finish.1 = f32[2,128,1024]{2,1,0:T(8,128)S(1)} custom-call(bf16[8,2,224,256]{3,2,1,0:T(8,128)(2,1)} %all-to-all-done.2.terms_ref, f32[2,96,1024]{2,1,0:T(8,128)S(1)} %spread_first.1.base_ref, bf16[1024,1024]{1,0:T(8,128)(2,1)S(1)} %fusion.order_ref), custom_call_target="tpu_custom_call" | custom-call | flops 536870912 | bytes 4194304 | tf_op jit(solution)/shard_map/finish/pallas_call | solution.py:293
  190.5 1.8 copy.11
  (107 shorter events, 28.0 us)
Async XLA Ops:
  0.7 162.5 %copy-start.28 = (s32[4]{0:T(128)}, s32[4]{0:T(128)S(1)}, u32[]{:S(2)}) copy-start(s32[4]{0:T(128)S(1)} %pad_add_fusion.place_ref) | copy-start | bytes 52
  9.0 50.0 %all-to-all-start = ((bf16[16,2,24,1024]{3,2,1,0:T(8,128)(2,1)}), bf16[16,2,24,1024]{3,2,1,0:T(8,128)(2,1)}, u32[]{:S(2)}, u32[]{:S(2)}) async-start(bf16[16,2,24,1024]{3,2,1,0:T(8,128)(2,1)} %copy-done.2), calls=%async_computation | async-start | bytes 3145728 | tf_op jit(solution)/shard_map/all_to_all | solution.py:377
  58.9 22.1 %all-to-all-start.1 = ((bf16[16,2,8,1024]{3,2,1,0:T(8,128)(2,1)}), bf16[16,2,8,1024]{3,2,1,0:T(8,128)(2,1)S(1)}, u32[]{:S(2)}, u32[]{:S(2)}) async-start(bf16[16,2,8,1024]{3,2,1,0:T(8,128)(2,1)} %shard_map.96), calls=%async_computation.1 | async-start | bytes 1048576 | tf_op jit(solution)/shard_map/all_to_all | solution.py:377
  65.4 15.7 %collective-permute-start = (bf16[384,1024]{1,0:T(8,128)(2,1)S(1)}, bf16[384,1024]{1,0:T(8,128)(2,1)S(1)}, u32[]{:S(2)}, u32[]{:S(2)}) collective-permute-start(bf16[384,1024]{1,0:T(8,128)(2,1)S(1)} %bitcast.27), channel_id=1, source_target_pairs={{0,8},{8,0},{1,9},{9,1},{2,10},{10,2},{3,11},{11,3},{4,12},{12,4},... | collective-permute-start | bytes 2359304 | tf_op jit(solution)/shard_map/ppermute | solution.py:363
  81.0 3.9 %collective-permute-start.1 = (bf16[128,1024]{1,0:T(8,128)(2,1)S(1)}, bf16[128,1024]{1,0:T(8,128)(2,1)S(1)}, u32[]{:S(2)}, u32[]{:S(2)}) collective-permute-start(bf16[128,1024]{1,0:T(8,128)(2,1)S(1)} %get-tuple-element.50), channel_id=1, source_target_pairs={{0,8},{8,0},{1,9},{9,1},{2,10},{10,2},{3,11},{11,3},{4,12},{12,4},... | collective-permute-start | bytes 786440 | tf_op jit(solution)/shard_map/ppermute | solution.py:363
  89.9 69.9 %copy-start.30 = (s32[1024]{0:T(1024)S(1)}, s32[1024]{0:T(1024)}, u32[]{:S(2)}) copy-start(s32[1024]{0:T(1024)} %constant.37.clone) | copy-start | bytes 12292
  89.9 97.2 %all-to-all-start.2 = ((bf16[8,2,224,256]{3,2,1,0:T(8,128)(2,1)}), bf16[8,2,224,256]{3,2,1,0:T(8,128)(2,1)}, u32[]{:S(2)}, u32[]{:S(2)}) async-start(bf16[8,2,224,256]{3,2,1,0:T(8,128)(2,1)} %get-tuple-element.27.after_ref.refs_8_), calls=%async_computation.2 | async-start | bytes 3670016 | tf_op jit(solution)/shard_map/all_to_all | solution.py:416
  96.0 7.0 %collective-permute-start.2 = (bf16[2,32,256]{2,1,0:T(8,128)(2,1)S(1)}, bf16[2,32,256]{2,1,0:T(8,128)(2,1)S(1)}, u32[]{:S(2)}, u32[]{:S(2)}) collective-permute-start(bf16[2,32,256]{2,1,0:T(8,128)(2,1)S(1)} %copy-done.31), channel_id=1, source_target_pairs={{0,0},{1,17},{2,34},{3,51},{4,68},{5,85},{6,102},{7,119},{16,16},{... | collective-permute-start | bytes 98312 | tf_op jit(solution)/shard_map/ppermute | solution.py:400
  103.0 1.2 collective-permute-start.3
  104.2 16.4 %collective-permute-start.4 = (bf16[2,2,32,256]{3,2,1,0:T(8,128)(2,1)S(1)}, bf16[2,2,32,256]{3,2,1,0:T(8,128)(2,1)S(1)}, u32[]{:S(2)}, u32[]{:S(2)}) collective-permute-start(bf16[2,2,32,256]{3,2,1,0:T(8,128)(2,1)S(1)} %get-tuple-element.53), channel_id=1, source_target_pairs={{0,128},{128,0},{1,129},{129,1},{2,130},{130,2},{3,131},{131,3},{4... | collective-permute-start | bytes 196616 | tf_op jit(solution)/shard_map/ppermute | solution.py:363
  105.1 28.4 %collective-permute-start.12 = (bf16[2,48,1152]{2,1,0:T(8,128)(2,1)}, bf16[2,48,1152]{2,1,0:T(8,128)(2,1)S(1)}, u32[]{:S(2)}, u32[]{:S(2)}) collective-permute-start(bf16[2,48,1152]{2,1,0:T(8,128)(2,1)} %get-tuple-element.29), channel_id=1, source_target_pairs={{0,1},{1,0},{2,3},{3,2},{4,5},{5,4},{6,7},{7,6},{8,9},{9,8},{10,11... | collective-permute-start | bytes 663560 | tf_op jit(solution)/shard_map/ppermute | solution.py:373
  105.1 30.1 %collective-permute-start.13 = (bf16[2,48,1152]{2,1,0:T(8,128)(2,1)}, bf16[2,48,1152]{2,1,0:T(8,128)(2,1)S(1)}, u32[]{:S(2)}, u32[]{:S(2)}) collective-permute-start(bf16[2,48,1152]{2,1,0:T(8,128)(2,1)} %get-tuple-element.30), channel_id=1, source_target_pairs={{0,2},{1,3},{2,0},{3,1},{4,6},{5,7},{6,4},{7,5},{8,10},{9,11},{10,... | collective-permute-start | bytes 663560 | tf_op jit(solution)/shard_map/ppermute | solution.py:373
  120.6 8.6 %collective-permute-start.11 = (bf16[2,2,2,32,256]{4,3,2,1,0:T(8,128)(2,1)S(1)}, bf16[2,2,2,32,256]{4,3,2,1,0:T(8,128)(2,1)S(1)}, u32[]{:S(2)}, u32[]{:S(2)}) collective-permute-start(bf16[2,2,2,32,256]{4,3,2,1,0:T(8,128)(2,1)S(1)} %pad_maximum_fusion.refs_0_), channel_id=1, source_target_pairs={{0,7},{1,6},{2,5},{3,4},{4,3},{5,2},{6,1},{7,0},{8,15},{9,14},{10,... | collective-permute-start | bytes 393224 | tf_op jit(solution)/shard_map/ppermute | solution.py:368
  123.2 7.6 %collective-permute-start.10 = (bf16[2,2,2,32,256]{4,3,2,1,0:T(8,128)(2,1)S(1)}, bf16[2,2,2,32,256]{4,3,2,1,0:T(8,128)(2,1)S(1)}, u32[]{:S(2)}, u32[]{:S(2)}) collective-permute-start(bf16[2,2,2,32,256]{4,3,2,1,0:T(8,128)(2,1)S(1)} %pad_maximum_fusion.refs_0_), channel_id=1, source_target_pairs={{0,6},{1,7},{2,4},{3,5},{4,2},{5,3},{6,0},{7,1},{8,14},{9,15},{10,... | collective-permute-start | bytes 393224 | tf_op jit(solution)/shard_map/ppermute | solution.py:368
  123.3 13.7 %collective-permute-start.14 = (bf16[2,48,1152]{2,1,0:T(8,128)(2,1)S(1)}, bf16[2,48,1152]{2,1,0:T(8,128)(2,1)S(1)}, u32[]{:S(2)}, u32[]{:S(2)}) collective-permute-start(bf16[2,48,1152]{2,1,0:T(8,128)(2,1)S(1)} %get-tuple-element.31), channel_id=1, source_target_pairs={{0,3},{1,2},{2,1},{3,0},{4,7},{5,6},{6,5},{7,4},{8,11},{9,10},{10,... | collective-permute-start | bytes 663560 | tf_op jit(solution)/shard_map/ppermute | solution.py:373
  129.2 21.9 %collective-permute-start.15 = (bf16[2,48,1152]{2,1,0:T(8,128)(2,1)S(1)}, bf16[2,48,1152]{2,1,0:T(8,128)(2,1)S(1)}, u32[]{:S(2)}, u32[]{:S(2)}) collective-permute-start(bf16[2,48,1152]{2,1,0:T(8,128)(2,1)S(1)} %get-tuple-element.32), channel_id=1, source_target_pairs={{0,4},{1,5},{2,6},{3,7},{4,0},{5,1},{6,2},{7,3},{8,12},{9,13},{10,... | collective-permute-start | bytes 663560 | tf_op jit(solution)/shard_map/ppermute | solution.py:373
  130.8 20.8 %collective-permute-start.16 = (bf16[2,48,1152]{2,1,0:T(8,128)(2,1)S(1)}, bf16[2,48,1152]{2,1,0:T(8,128)(2,1)S(1)}, u32[]{:S(2)}, u32[]{:S(2)}) collective-permute-start(bf16[2,48,1152]{2,1,0:T(8,128)(2,1)S(1)} %get-tuple-element.33), channel_id=1, source_target_pairs={{0,5},{1,4},{2,7},{3,6},{4,1},{5,0},{6,3},{7,2},{8,13},{9,12},{10,... | collective-permute-start | bytes 663560 | tf_op jit(solution)/shard_map/ppermute | solution.py:373
  133.6 23.4 %collective-permute-start.17 = (bf16[2,48,1152]{2,1,0:T(8,128)(2,1)S(1)}, bf16[2,48,1152]{2,1,0:T(8,128)(2,1)S(1)}, u32[]{:S(2)}, u32[]{:S(2)}) collective-permute-start(bf16[2,48,1152]{2,1,0:T(8,128)(2,1)S(1)} %get-tuple-element.34), channel_id=1, source_target_pairs={{0,6},{1,7},{2,4},{3,5},{4,2},{5,3},{6,0},{7,1},{8,14},{9,15},{10,... | collective-permute-start | bytes 663560 | tf_op jit(solution)/shard_map/ppermute | solution.py:373
  135.2 21.8 %collective-permute-start.18 = (bf16[2,48,1152]{2,1,0:T(8,128)(2,1)S(1)}, bf16[2,48,1152]{2,1,0:T(8,128)(2,1)S(1)}, u32[]{:S(2)}, u32[]{:S(2)}) collective-permute-start(bf16[2,48,1152]{2,1,0:T(8,128)(2,1)S(1)} %get-tuple-element.35), channel_id=1, source_target_pairs={{0,7},{1,6},{2,5},{3,4},{4,3},{5,2},{6,1},{7,0},{8,15},{9,14},{10,... | collective-permute-start | bytes 663560 | tf_op jit(solution)/shard_map/ppermute | solution.py:373
  136.9 24.9 %collective-permute-start.9 = (bf16[2,2,2,32,256]{4,3,2,1,0:T(8,128)(2,1)S(1)}, bf16[2,2,2,32,256]{4,3,2,1,0:T(8,128)(2,1)S(1)}, u32[]{:S(2)}, u32[]{:S(2)}) collective-permute-start(bf16[2,2,2,32,256]{4,3,2,1,0:T(8,128)(2,1)S(1)} %pad_maximum_fusion.refs_0_), channel_id=1, source_target_pairs={{0,5},{1,4},{2,7},{3,6},{4,1},{5,0},{6,3},{7,2},{8,13},{9,12},{10,... | collective-permute-start | bytes 393224 | tf_op jit(solution)/shard_map/ppermute | solution.py:368
  151.2 10.7 %collective-permute-start.8 = (bf16[2,2,2,32,256]{4,3,2,1,0:T(8,128)(2,1)S(1)}, bf16[2,2,2,32,256]{4,3,2,1,0:T(8,128)(2,1)S(1)}, u32[]{:S(2)}, u32[]{:S(2)}) collective-permute-start(bf16[2,2,2,32,256]{4,3,2,1,0:T(8,128)(2,1)S(1)} %pad_maximum_fusion.refs_0_), channel_id=1, source_target_pairs={{0,4},{1,5},{2,6},{3,7},{4,0},{5,1},{6,2},{7,3},{8,12},{9,13},{10,... | collective-permute-start | bytes 393224 | tf_op jit(solution)/shard_map/ppermute | solution.py:368
  151.6 11.5 %collective-permute-start.7 = (bf16[2,2,2,32,256]{4,3,2,1,0:T(8,128)(2,1)S(1)}, bf16[2,2,2,32,256]{4,3,2,1,0:T(8,128)(2,1)S(1)}, u32[]{:S(2)}, u32[]{:S(2)}) collective-permute-start(bf16[2,2,2,32,256]{4,3,2,1,0:T(8,128)(2,1)S(1)} %pad_maximum_fusion.refs_0_), channel_id=1, source_target_pairs={{0,3},{1,2},{2,1},{3,0},{4,7},{5,6},{6,5},{7,4},{8,11},{9,10},{10,... | collective-permute-start | bytes 393224 | tf_op jit(solution)/shard_map/ppermute | solution.py:368
  157.0 6.1 %collective-permute-start.6 = (bf16[2,2,2,32,256]{4,3,2,1,0:T(8,128)(2,1)S(1)}, bf16[2,2,2,32,256]{4,3,2,1,0:T(8,128)(2,1)S(1)}, u32[]{:S(2)}, u32[]{:S(2)}) collective-permute-start(bf16[2,2,2,32,256]{4,3,2,1,0:T(8,128)(2,1)S(1)} %pad_maximum_fusion.refs_0_), channel_id=1, source_target_pairs={{0,2},{1,3},{2,0},{3,1},{4,6},{5,7},{6,4},{7,5},{8,10},{9,11},{10,... | collective-permute-start | bytes 393224 | tf_op jit(solution)/shard_map/ppermute | solution.py:368
  157.0 6.2 %collective-permute-start.5 = (bf16[2,2,2,32,256]{4,3,2,1,0:T(8,128)(2,1)S(1)}, bf16[2,2,2,32,256]{4,3,2,1,0:T(8,128)(2,1)S(1)}, u32[]{:S(2)}, u32[]{:S(2)}) collective-permute-start(bf16[2,2,2,32,256]{4,3,2,1,0:T(8,128)(2,1)S(1)} %pad_maximum_fusion.refs_0_), channel_id=1, source_target_pairs={{0,1},{1,0},{2,3},{3,2},{4,5},{5,4},{6,7},{7,6},{8,9},{9,8},{10,11... | collective-permute-start | bytes 393224 | tf_op jit(solution)/shard_map/ppermute | solution.py:368
  161.8 13.2 %copy-start.6 = (bf16[256,1024]{1,0:T(8,128)(2,1)S(1)}, bf16[256,1024]{1,0:T(8,128)(2,1)}, u32[]{:S(2)}) copy-start(bf16[256,1024]{1,0:T(8,128)(2,1)} %copy-done.5) | copy-start | bytes 1572868
  161.8 8.1 %collective-permute-start.19 = (bf16[2,48,128]{2,1,0:T(8,128)(2,1)S(1)}, bf16[2,48,128]{2,1,0:T(8,128)(2,1)S(1)}, u32[]{:S(2)}, u32[]{:S(2)}) collective-permute-start(bf16[2,48,128]{2,1,0:T(8,128)(2,1)S(1)} %get-tuple-element.39), channel_id=1, source_target_pairs={{0,1},{1,0},{2,3},{3,2},{4,5},{5,4},{6,7},{7,6},{8,9},{9,8},{10,11... | collective-permute-start | bytes 73736 | tf_op jit(solution)/shard_map/ppermute | solution.py:373
  161.9 9.8 %collective-permute-start.20 = (bf16[2,48,128]{2,1,0:T(8,128)(2,1)S(1)}, bf16[2,48,128]{2,1,0:T(8,128)(2,1)S(1)}, u32[]{:S(2)}, u32[]{:S(2)}) collective-permute-start(bf16[2,48,128]{2,1,0:T(8,128)(2,1)S(1)} %get-tuple-element.40), channel_id=1, source_target_pairs={{0,2},{1,3},{2,0},{3,1},{4,6},{5,7},{6,4},{7,5},{8,10},{9,11},{10,... | collective-permute-start | bytes 73736 | tf_op jit(solution)/shard_map/ppermute | solution.py:373
  164.4 12.8 %collective-permute-start.21 = (bf16[2,48,128]{2,1,0:T(8,128)(2,1)}, bf16[2,48,128]{2,1,0:T(8,128)(2,1)S(1)}, u32[]{:S(2)}, u32[]{:S(2)}) collective-permute-start(bf16[2,48,128]{2,1,0:T(8,128)(2,1)} %get-tuple-element.41), channel_id=1, source_target_pairs={{0,3},{1,2},{2,1},{3,0},{4,7},{5,6},{6,5},{7,4},{8,11},{9,10},{10,... | collective-permute-start | bytes 73736 | tf_op jit(solution)/shard_map/ppermute | solution.py:373
  166.7 11.1 %collective-permute-start.22 = (bf16[2,48,128]{2,1,0:T(8,128)(2,1)}, bf16[2,48,128]{2,1,0:T(8,128)(2,1)S(1)}, u32[]{:S(2)}, u32[]{:S(2)}) collective-permute-start(bf16[2,48,128]{2,1,0:T(8,128)(2,1)} %get-tuple-element.42), channel_id=1, source_target_pairs={{0,4},{1,5},{2,6},{3,7},{4,0},{5,1},{6,2},{7,3},{8,12},{9,13},{10,... | collective-permute-start | bytes 73736 | tf_op jit(solution)/shard_map/ppermute | solution.py:373
  168.6 9.8 %collective-permute-start.23 = (bf16[2,48,128]{2,1,0:T(8,128)(2,1)S(1)}, bf16[2,48,128]{2,1,0:T(8,128)(2,1)S(1)}, u32[]{:S(2)}, u32[]{:S(2)}) collective-permute-start(bf16[2,48,128]{2,1,0:T(8,128)(2,1)S(1)} %get-tuple-element.43), channel_id=1, source_target_pairs={{0,5},{1,4},{2,7},{3,6},{4,1},{5,0},{6,3},{7,2},{8,13},{9,12},{10,... | collective-permute-start | bytes 73736 | tf_op jit(solution)/shard_map/ppermute | solution.py:373
  169.9 9.1 %collective-permute-start.24 = (bf16[2,48,128]{2,1,0:T(8,128)(2,1)S(1)}, bf16[2,48,128]{2,1,0:T(8,128)(2,1)S(1)}, u32[]{:S(2)}, u32[]{:S(2)}) collective-permute-start(bf16[2,48,128]{2,1,0:T(8,128)(2,1)S(1)} %get-tuple-element.44), channel_id=1, source_target_pairs={{0,6},{1,7},{2,4},{3,5},{4,2},{5,3},{6,0},{7,1},{8,14},{9,15},{10,... | collective-permute-start | bytes 73736 | tf_op jit(solution)/shard_map/ppermute | solution.py:373
  172.3 7.4 %collective-permute-start.25 = (bf16[2,48,128]{2,1,0:T(8,128)(2,1)S(1)}, bf16[2,48,128]{2,1,0:T(8,128)(2,1)S(1)}, u32[]{:S(2)}, u32[]{:S(2)}) collective-permute-start(bf16[2,48,128]{2,1,0:T(8,128)(2,1)S(1)} %get-tuple-element.45), channel_id=1, source_target_pairs={{0,7},{1,6},{2,5},{3,4},{4,3},{5,2},{6,1},{7,0},{8,15},{9,14},{10,... | collective-permute-start | bytes 73736 | tf_op jit(solution)/shard_map/ppermute | solution.py:373
  (29 other events, 93.2 us)

commit v3 on v2

v3 whole, which is shorter than its diff:
```python
import math

import jax
import jax.numpy as jnp
import numpy as np
from jax import lax
from jax.experimental import pallas as pl
from jax.experimental.pallas import tpu as pltpu
from jax.sharding import Mesh
from jax.sharding import PartitionSpec as P


STAT = ("stat_0", "stat_1", "stat_2")
CHIP = ("stat_0", "stat_1")
TM = ("tm_0", "tm_1")
NF = 4096
CHIPS = 16
N_TM = 8
SPECTRA = 4
FIRST, SECOND = 24, 8
SIDE_A, SIDE_B = CHIPS * FIRST, CHIPS * SECOND
OWN_A, OWN_B = SIDE_A // N_TM, SIDE_B // N_TM
COLS_A, COLS_B = 2 * SIDE_A, 2 * SIDE_B
HALF = 512
BF16 = jnp.bfloat16
F32 = jnp.float32
VMEM = pl.BlockSpec(memory_space=pltpu.VMEM)
SMEM = pl.BlockSpec(memory_space=pltpu.SMEM)
ANY = pl.BlockSpec(memory_space=pl.ANY)
HBM = pl.BlockSpec(memory_space=pltpu.HBM)


def rotation(angle):
    cosine, sine = np.cos(angle), np.sin(angle)
    return np.block([[cosine, sine], [-sine, cosine]])


def dft_tables():
    outer = np.arange(32)
    angle = 2.0 * np.pi * np.outer(outer, outer) / 32
    eye = np.eye(SPECTRA)
    spread = lambda m: np.einsum("wc,st->wsct", m, eye).reshape(128, 128)
    cosine, sine = spread(np.cos(angle)), spread(np.sin(angle))
    left = np.block([[cosine, sine], [-sine, cosine]])
    w0 = np.repeat(np.arange(32), SPECTRA)
    twist = 2.0 * np.pi * np.outer(w0, np.arange(128)) / NF
    inner = 2.0 * np.pi * np.outer(np.arange(128), np.arange(128)) / 128
    right = rotation(inner) / math.sqrt(NF)
    right = right.reshape(2, 32, 4, 256).transpose(1, 0, 2, 3).reshape(256, 256)
    return (
        left.astype(np.float32),
        np.cos(twist).astype(np.float32),
        np.sin(twist).astype(np.float32),
        right.astype(np.float32),
    )


def natural_columns(core):
    def of(core):
        rel, chip, item = np.meshgrid(np.arange(2), np.arange(CHIPS), np.arange(32), indexing="ij")
        place = 32 * (2 * chip + (rel ^ core)) + item
        late = place[:, :, FIRST:].transpose(1, 0, 2)
        return np.concatenate([place[:, :, :FIRST].reshape(-1), late.reshape(-1)]).astype(np.int32)

    return jnp.where(core == 0, jnp.asarray(of(0)), jnp.asarray(of(1)))


def params(mib):
    return pltpu.CompilerParams(vmem_limit_bytes=mib * 1024 * 1024)


def cost(macs, moved):
    return pl.CostEstimate(flops=2 * macs, bytes_accessed=moved, transcendentals=0)


def dot_nn(a, b):
    return lax.dot_general(a, b, (((1,), (0,)), ((), ())), preferred_element_type=F32)


def dot_nt(a, b):
    return lax.dot_general(a, b, (((1,), (1,)), ((), ())), preferred_element_type=F32)


def dft_kernel(place_ref, x_hbm, left_hbm, turn_hbm, right_hbm, *refs):
    outs, (x_ref, left_ref, turn_ref, right_ref, stage, sems, pack, out_sems) = refs[:-8], refs[-8:]
    count = x_ref.shape[1]
    start = 0 if count == FIRST else FIRST
    loads = [
        pltpu.make_async_copy(left_hbm, left_ref, sems.at[0]),
        pltpu.make_async_copy(turn_hbm, turn_ref, sems.at[1]),
        pltpu.make_async_copy(right_hbm, right_ref, sems.at[2]),
    ]
    groups = count // 8
    for g in range(groups):
        loads.append(
            pltpu.make_async_copy(
                x_hbm.at[:, start + 8 * g : start + 8 * g + 8], x_ref.at[:, 8 * g : 8 * g + 8], sems.at[3 + g]
            )
        )
    for load in [loads[0], loads[3], *loads[1:3], *loads[4:]]:
        load.start()
    for load in loads[:3]:
        load.wait()
    core = place_ref[0]
    left = left_ref[...]
    right = right_ref[...]
    cosine = turn_ref[0]
    sine = turn_ref[1]
    for pair in range(count // 2):
        if pair % 4 == 0:
            loads[3 + pair // 4].wait()
        signal = [jnp.concatenate([x_ref[0, 2 * pair + k], x_ref[1, 2 * pair + k]], 0) for k in (0, 1)]
        first = dot_nn(left, jnp.concatenate(signal, 1))
        turned = []
        for k in (0, 1):
            re = first[:128, 128 * k : 128 * k + 128]
            im = first[128:, 128 * k : 128 * k + 128]
            turned.append(
                jnp.concatenate(
                    [(re * cosine + im * sine).astype(BF16), (im * cosine - re * sine).astype(BF16)], 1
                )
            )
        final = dot_nt(right, jnp.concatenate(turned, 0))
        for k in (0, 1):
            stage[pl.ds(2 * pair + k, 256, stride=count), :] = final[:, 128 * k : 128 * k + 128]
    stores = []
    for chip in range(CHIPS):
        for rel in (0, 1):
            for t in range(8):
                row = pl.multiple_of(((2 * chip + (rel ^ core)) * 8 + t) * count, 8)
                value = stage[pl.ds(row, count), :].astype(BF16)
                if len(outs) == 1:
                    pack[chip, rel, :, 128 * t : 128 * t + 128] = value
                else:
                    outs[rel][chip, :, 128 * t : 128 * t + 128] = value
        if len(outs) == 1:
            stores.append(pltpu.make_async_copy(pack.at[chip], outs[0].at[chip], out_sems.at[chip]))
            stores[chip].start()
    for store in stores:
        store.wait()


def dft_part(place, signal, tables, count):
    full = pltpu.HBM((CHIPS, 2, count, 1024), BF16)
    half = jax.ShapeDtypeStruct((CHIPS, count, 1024), BF16)
    shapes = (full,) if count == FIRST else (half, half)
    return pl.pallas_call(
        dft_kernel,
        in_specs=[SMEM] + [HBM] * 4,
        out_specs=(HBM,) if count == FIRST else (VMEM, VMEM),
        out_shape=shapes,
        scratch_shapes=[
            pltpu.VMEM((2, count, 128, 128), BF16),
            pltpu.VMEM((256, 256), BF16),
            pltpu.VMEM((2, 128, 128), F32),
            pltpu.VMEM((256, 256), BF16),
            pltpu.VMEM((256 * count, 128), F32),
            pltpu.SemaphoreType.DMA((3 + count // 8,)),
            pltpu.VMEM((CHIPS if count == FIRST else 1, 2, count, 1024), BF16),
            pltpu.SemaphoreType.DMA((CHIPS,)),
        ],
        compiler_params=params(60 if count == FIRST else 12),
        cost_estimate=cost(count << 25, count << 17),
    )(place, signal, *tables)


def product(rows, cols):
    scale = 1.0 / NF
    real = dot_nt(rows, cols) * scale
    imag = (dot_nt(rows[:, HALF:], cols[:, :HALF]) - dot_nt(rows[:, :HALF], cols[:, HALF:])) * scale
    return real, imag


def gram_first_kernel(place_ref, kept_ref, swapped_ref, *rest):
    out_refs, full = rest[:N_TM], rest[N_TM]
    own = place_ref[1]
    sides = (kept_ref, swapped_ref)
    for a in (0, 1):
        for b in (0, 1):
            values = product(sides[a][...], sides[b][...])
            for q in (0, 1):
                full[q, a, :, SIDE_A * b : SIDE_A * b + SIDE_A] = values[q].astype(BF16)
    for k in range(N_TM):
        row = pl.multiple_of((own ^ k) * OWN_A, OWN_A)
        for q in (0, 1):
            for a in (0, 1):
                out_refs[k][q, OWN_A * a : OWN_A * a + OWN_A] = full[q, a, pl.ds(row, OWN_A), :]


def gram_first(place, kept, swapped):
    return pl.pallas_call(
        gram_first_kernel,
        in_specs=[SMEM, VMEM, VMEM],
        out_specs=(VMEM,) * N_TM,
        out_shape=(jax.ShapeDtypeStruct((2, 2 * OWN_A, COLS_A), BF16),) * N_TM,
        scratch_shapes=[pltpu.VMEM((2, 2, SIDE_A, COLS_A), BF16)],
        compiler_params=params(10),
        cost_estimate=cost(1 << 30, 6 << 20),
        name="gram_first",
    )(place, kept, swapped)


def gram_second_kernel(mine_ref, kept_ref, swapped_ref, out_hbm, out_ref, sems):
    mine = mine_ref[...]
    sides = [product(mine, kept_ref[...]), product(mine, swapped_ref[...])]
    second = product(mine, mine)
    copies = []
    for q in (0, 1):
        first = jnp.concatenate([sides[0][q], sides[1][q]], 1)
        flipped = first.T
        flipped = (-flipped if q else flipped).astype(BF16)
        blocks = [first[:, COLS_B * j : COLS_B * j + COLS_B].astype(BF16) for j in range(3)]
        blocks.append(second[q].astype(BF16))
        rows = 2 * OWN_B
        for r in range(N_TM):
            for j in range(4):
                out_ref[r, q, rows * j : rows * j + rows, :] = blocks[j][rows * r : rows * r + rows]
            for a in (0, 1):
                row = 4 * rows + OWN_A * a
                src = SIDE_A * a + OWN_A * r
                out_ref[r, q, row : row + OWN_A, :] = flipped[src : src + OWN_A]
        copies.append(pltpu.make_async_copy(out_ref.at[:, q], out_hbm.at[:, q], sems.at[q]))
        copies[q].start()
    for copy in copies:
        copy.wait()


def gram_second(mine, kept, swapped):
    rows = 8 * OWN_B + 2 * OWN_A
    return pl.pallas_call(
        gram_second_kernel,
        in_specs=[VMEM, VMEM, VMEM],
        out_specs=HBM,
        out_shape=pltpu.HBM((N_TM, 2, rows, COLS_B), BF16),
        scratch_shapes=[
            pltpu.VMEM((N_TM, 2, rows, COLS_B), BF16),
            pltpu.SemaphoreType.DMA((2,)),
        ],
        compiler_params=params(10),
        cost_estimate=cost(1 << 29, 6 << 20),
        name="gram_second",
    )(mine, kept, swapped)


def placed(values, table):
    parts = []
    for value in values:
        high = value.astype(BF16)
        parts += [high, (value - high.astype(F32)).astype(BF16)]
    result = dot_nn(jnp.concatenate(parts, 0), table)
    size = values[0].shape[0]
    return [result[2 * k * size : (2 * k + 1) * size] + result[(2 * k + 1) * size : (2 * k + 2) * size] for k in range(len(values))]


def spread_kernel(*refs):
    terms, order_ref, out_ref = refs[:N_TM], refs[N_TM], refs[-1]
    totals = []
    for q in (0, 1):
        total = terms[0][q].astype(F32)
        for k in range(1, N_TM):
            total = total + terms[k][q].astype(F32)
        totals.append(total)
    spread = placed(totals, order_ref[:COLS_A, :])
    for q in (0, 1):
        out_ref[q] = spread[q]


def spread_first(terms, order):
    return pl.pallas_call(
        spread_kernel,
        in_specs=[VMEM] * (N_TM + 1),
        out_specs=VMEM,
        out_shape=jax.ShapeDtypeStruct((2, 2 * OWN_A, 1024), F32),
        compiler_params=params(8),
        cost_estimate=cost(1 << 28, 1 << 22),
        name="spread_first",
    )(*terms, order)


def finish_kernel(place_ref, terms_ref, base_ref, order_ref, out_ref):
    core = place_ref[0]
    rows = 2 * OWN_B
    last, extra = [], []
    for q in (0, 1):
        total = terms_ref[0, q].astype(F32)
        for t in range(1, N_TM):
            total = total + terms_ref[t, q].astype(F32)
        last.append(jnp.concatenate([total[rows * j : rows * j + rows] for j in range(4)], 1))
        extra.append(total[4 * rows :])
    lower = placed(last, order_ref[...])
    upper = placed(extra, order_ref[COLS_A:, :])
    for q in (0, 1):
        top = base_ref[q] + upper[q]
        for rel in (0, 1):
            for chip in (0, 1):
                row = pl.multiple_of(64 * chip + 32 * (rel ^ core), 8)
                src = OWN_A * rel + FIRST * chip
                out_ref[q, pl.ds(row, FIRST), :] = top[src : src + FIRST]
                src = 2 * SECOND * chip + SECOND * rel
                out_ref[q, pl.ds(pl.multiple_of(row + FIRST, 8), SECOND), :] = lower[q][src : src + SECOND]


def finish(place, terms, base, order):
    return pl.pallas_call(
        finish_kernel,
        in_specs=[SMEM] + [VMEM] * 3,
        out_specs=VMEM,
        out_shape=jax.ShapeDtypeStruct((2, 128, 1024), F32),
        compiler_params=params(8),
        cost_estimate=cost(1 << 28, 1 << 22),
        name="finish",
    )(place, terms, base, order)


def weight_kernel(place_ref, *refs):
    blocks, out_ref, rows = refs[:N_TM], refs[N_TM], refs[-1]
    own, far, z = place_ref[1], place_ref[2], place_ref[3]
    for k in range(N_TM):
        source = (z - (own ^ k)) & 7
        for dx in (0, 1):
            chip = (far ^ dx) * 8 + source
            for dc in (0, 1):
                early = pl.multiple_of(dc * SIDE_A + chip * FIRST, 8)
                late = pl.multiple_of(COLS_A + chip * 2 * SECOND + dc * SECOND, 8)
                for p in (0, 1):
                    block = blocks[k][dc, dx, p].astype(F32)
                    rows[p, pl.ds(early, FIRST), :] = block[:FIRST]
                    rows[p, pl.ds(late, SECOND), :] = block[FIRST:]
    for p in (0, 1):
        flipped = rows[p].T
        straight = flipped.astype(BF16)
        out_ref[:256, 1024 * p : 1024 * p + 1024] = (-flipped).astype(BF16) if p else straight
        out_ref[256:, 1024 * (1 - p) : 1024 * (1 - p) + 1024] = straight


def weight_stack(place, blocks):
    return pl.pallas_call(
        weight_kernel,
        in_specs=[SMEM] + [VMEM] * N_TM,
        out_specs=VMEM,
        out_shape=jax.ShapeDtypeStruct((HALF, 2048), BF16),
        scratch_shapes=[pltpu.VMEM((2, 1024, 256), F32)],
        compiler_params=params(10),
        cost_estimate=cost(1 << 27, 1 << 22),
        name="weights",
    )(place, *blocks)


def beam_kernel(kept_ref, swapped_ref, second_ref, weight_ref, out_ref):
    total = None
    for p in (0, 1):
        lanes = slice(HALF * p, HALF * p + HALF)
        column = 1024 * p
        for ref in (kept_ref, swapped_ref, second_ref):
            count = ref.shape[0]
            term = dot_nn(weight_ref[:, column : column + count], ref[:, lanes])
            column += count
            total = term if total is None else total + term
    out_ref[...] = total.T.astype(BF16)


def beam_sum(kept, swapped, second, weights):
    return pl.pallas_call(
        beam_kernel,
        in_specs=[VMEM] * 4,
        out_specs=VMEM,
        out_shape=jax.ShapeDtypeStruct((HALF, HALF), BF16),
        compiler_params=params(10),
        cost_estimate=cost(1 << 29, 1 << 22),
        name="beams",
    )(kept, swapped, second, weights)


def swap(array, axis):
    return lax.ppermute(array, axis, [(0, 1), (1, 0)])


def with_partners(array):
    pairs = lambda k: [(i, i ^ k) for i in range(N_TM)]
    return [array] + [lax.ppermute(array, TM, pairs(k)) for k in range(1, N_TM)]


def to_partners(arrays):
    pairs = lambda k: [(i, i ^ k) for i in range(N_TM)]
    return [arrays[0]] + [lax.ppermute(arrays[k], TM, pairs(k)) for k in range(1, N_TM)]


def behind(value, other):
    return lax.optimization_barrier((value, other))[0]


def step(voltages, beam_weights):
    left, cosine, sine, right = dft_tables()
    tables = (jnp.asarray(left, BF16), jnp.asarray(np.stack([cosine, sine])), jnp.asarray(right, BF16))
    signal = voltages.reshape(2, 32, SPECTRA, 32, 128).transpose(0, 1, 3, 2, 4)
    signal = signal.reshape(2, 32, 128, 128)
    where = ("stat_2", TM, "stat_0", "stat_1")
    place = jnp.stack([lax.axis_index(a) for a in where]).astype(jnp.int32)

    spots = [(x, z, t) for x in (0, 1) for z in range(8) for t in range(N_TM)]
    at = lambda x, z, t: (x * 8 + z % 8) * N_TM + t
    rings = [[(at(x, z, t), at(x ^ dx, z + t, t)) for x, z, t in spots] for dx in (0, 1)]
    block = jnp.stack([lax.ppermute(beam_weights, (*CHIP, *TM), ring) for ring in rings])

    (ready_a,) = dft_part(place, signal, tables, FIRST)
    own_b, other_b = dft_part(place, signal, tables, SECOND)
    partner_b = swap(other_b, "stat_2")
    ready_b = jnp.concatenate([own_b, partner_b], 1)

    near = swap(block, "stat_2")
    block = jnp.stack([block, near])
    blocks_k = with_partners(block)
    columns = natural_columns(behind(lax.axis_index("stat_2"), ready_b))
    order = (columns[:, None] == jnp.arange(1024, dtype=jnp.int32)[None, :]).astype(BF16)

    arrived = lax.all_to_all(ready_a, CHIP, 0, 0, tiled=True)
    second = lax.all_to_all(ready_b, CHIP, 0, 0, tiled=True).reshape(COLS_B, 1024)
    kept = arrived[:, 0].reshape(SIDE_A, 1024)
    other = arrived[:, 1].reshape(SIDE_A, 1024)
    swapped = swap(other, "stat_2")
    terms = gram_first(place, kept, swapped)
    terms = to_partners(terms)
    blocks = gram_second(second, kept, swapped)
    last = lax.all_to_all(blocks, TM, 0, 0, tiled=True)

    weights = weight_stack(place, blocks_k)
    beams = beam_sum(kept, swapped, second, weights)
    beams = beams.reshape(NF // 32, SPECTRA, 2, 256)
    base = spread_first(terms, order)
    rows = finish(place, last, base, order)
    return beams, rows.transpose(1, 0, 2)[:, None]


def solution(mesh):
    finer = Mesh(
        mesh.devices.reshape(2, 8, 2, 4, 2), ("stat_0", "stat_1", "stat_2", "tm_0", "tm_1")
    )
    return jax.shard_map(
        step,
        mesh=finer,
        in_specs=(P(None, STAT, TM, None), P(None, STAT, None)),
        out_specs=(P(STAT, TM, None, None), P(TM, STAT, None, None)),
        check_vma=False,
    )
```

time: 193 us -> 177 us (0.917)
  the two profiles are of different devices: /device:TPU:2 before, /device:TPU:64 now
where the time goes in v3:
time: 177 us; the launch traced here: 175 us
  waiting for transfers between devices  88.2 us (50%)
  starting transfers between devices  47.2 us (27%)
  Pallas kernels  22.5 us (13%)
  local copies, waits for them, and re-layouts  15 us (8%)
    all_to_all x1, waiting for transfers between devices, step(): arrived = lax.all_to_all(ready_a, CHIP, 0, 0, tiled=True)  31.2 us
    ppermute x2, waiting for transfers between devices, step(): lax.ppermute(beam_weights, (*CHIP, *TM), ring)  19 us
    ppermute x7, waiting for transfers between devices, to_partners(): lax.ppermute(arrays[k], TM, pairs(k))  17.1 us
    all_to_all x1, waiting for transfers between devices, step(): lax.all_to_all(ready_b, CHIP, 0, 0, tiled=True).reshape(COLS_B, 1024)  12.9 us
    unnamed x40, local copies, waits for them, and re-layouts  10.8 us
    all_to_all x1, starting transfers between devices, step(): arrived = lax.all_to_all(ready_a, CHIP, 0, 0, tiled=True)  10.7 us
    ppermute x7, starting transfers between devices, to_partners(): lax.ppermute(arrays[k], TM, pairs(k))  10.7 us
    all_to_all x1, starting transfers between devices, step(): lax.all_to_all(ready_b, CHIP, 0, 0, tiled=True).reshape(COLS_B, 1024)  9.07 us
  transfers between devices with their start and end apart: 22, of which 10 were waited for; matrix products, arithmetic and copies ran while one was open for 3% of the time, Pallas kernels for 7%

profile of v3, /device:TPU:64, one launch (start us, length us, event | category | flops | bytes accessed | tf_op | source)
XLA Modules:
  0.0 174.8 jit_solution(5916738782514236919)
XLA Ops:
  1.3 5.2 %shard_map.86 = bf16[16,2,24,1024]{3,2,1,0:T(8,128)(2,1)} custom-call(s32[4]{0:T(128)} %pad_add_fusion.place_ref, bf16[2,32,128,128]{3,2,1,0:T(8,128)(2,1)} %bitcast.26, bf16[256,256]{1,0:T(8,128)(2,1)} %constant.33.clone.left_hbm, f32[2,128,128]{2,1,0:T(8,128)} %constant.34.clone.turn_hbm, bf16[256,256]{1,0:T(8,128)(2,1)} %constant.35.clone.right_hbm), custom_call_target="tpu_custom_call" | custom-call | flops 1610612736 | bytes 3145728 | tf_op jit(solution)/shard_map/pallas_call | solution.py:147
  6.5 10.7 %all-to-all-start = ((bf16[16,2,24,1024]{3,2,1,0:T(8,128)(2,1)}), bf16[16,2,24,1024]{3,2,1,0:T(8,128)(2,1)}, u32[]{:S(2)}, u32[]{:S(2)}) async-start(bf16[16,2,24,1024]{3,2,1,0:T(8,128)(2,1)} %shard_map.86), calls=%async_computation | async-start | bytes 3145728 | tf_op jit(solution)/shard_map/all_to_all | solution.py:416
  17.3 2.0 %shard_map.87 = (bf16[16,8,1024]{2,1,0:T(8,128)(2,1)S(1)}, bf16[16,8,1024]{2,1,0:T(8,128)(2,1)S(1)}) custom-call(s32[4]{0:T(128)S(1)} %copy-done.15, bf16[2,32,128,128]{3,2,1,0:T(8,128)(2,1)S(1)} %bitcast.27, bf16[256,256]{1,0:T(8,128)(2,1)S(1)} %copy-done.14, f32[2,128,128]{2,1,0:T(8,128)S(1)} %copy-done.13, bf16[256,256]{1,0:T(8,128)(2,1)S(1)} %copy-done.12), custom_call_target="tpu_custom_call" | custom-call | flops 536870912 | bytes 1048576 | tf_op jit(solution)/shard_map/pallas_call | solution.py:147
  21.6 31.2 %all-to-all-done = bf16[16,2,24,1024]{3,2,1,0:T(8,128)(2,1)} async-done(((bf16[16,2,24,1024]{3,2,1,0:T(8,128)(2,1)}), bf16[16,2,24,1024]{3,2,1,0:T(8,128)(2,1)}, u32[]{:S(2)}, u32[]{:S(2)}) %all-to-all-start) | async-done | bytes 1572896 | tf_op jit(solution)/shard_map/all_to_all | solution.py:416
  52.8 9.1 %all-to-all-start.1 = ((bf16[16,16,1024]{2,1,0:T(8,128)(2,1)}), bf16[16,16,1024]{2,1,0:T(8,128)(2,1)S(1)}, u32[]{:S(2)}, u32[]{:S(2)}) async-start(bf16[16,16,1024]{2,1,0:T(8,128)(2,1)} %constant_dynamic-update-slice_fusion), calls=%async_computation.1 | async-start | bytes 1048576 | tf_op jit(solution)/shard_map/all_to_all | solution.py:417
  61.9 1.5 fusion.2
  63.5 12.9 %all-to-all-done.1 = bf16[16,16,1024]{2,1,0:T(8,128)(2,1)S(1)} async-done(((bf16[16,16,1024]{2,1,0:T(8,128)(2,1)}), bf16[16,16,1024]{2,1,0:T(8,128)(2,1)S(1)}, u32[]{:S(2)}, u32[]{:S(2)}) %all-to-all-start.1) | async-done | bytes 524320 | tf_op jit(solution)/shard_map/all_to_all | solution.py:417
  76.4 2.8 %gram_second.1 = bf16[8,2,224,256]{3,2,1,0:T(8,128)(2,1)} custom-call(bf16[256,1024]{1,0:T(8,128)(2,1)S(1)} %bitcast.24, bf16[384,1024]{1,0:T(8,128)(2,1)S(1)} %bitcast.21, bf16[384,1024]{1,0:T(8,128)(2,1)S(1)} %collective-permute-done.swapped_ref), custom_call_target="tpu_custom_call" | custom-call | flops 1073741824 | bytes 6291456 | tf_op jit(solution)/shard_map/gram_second/pallas_call | solution.py:230
  79.2 4.5 %all-to-all-start.2 = ((bf16[8,2,224,256]{3,2,1,0:T(8,128)(2,1)}), bf16[8,2,224,256]{3,2,1,0:T(8,128)(2,1)}, u32[]{:S(2)}, u32[]{:S(2)}) async-start(bf16[8,2,224,256]{3,2,1,0:T(8,128)(2,1)} %gram_second.1), calls=%async_computation.2 | async-start | bytes 3670016 | tf_op jit(solution)/shard_map/all_to_all | solution.py:424
  83.7 3.5 %collective-permute-start.3 = (bf16[2,32,256]{2,1,0:T(8,128)(2,1)S(1)}, bf16[2,32,256]{2,1,0:T(8,128)(2,1)S(1)}, u32[]{:S(2)}, u32[]{:S(2)}) collective-permute-start(bf16[2,32,256]{2,1,0:T(8,128)(2,1)S(1)} %copy-done.18), channel_id=1, source_target_pairs={{0,128},{1,145},{2,162},{3,179},{4,196},{5,213},{6,230},{7,247},{1... | collective-permute-start | bytes 98312 | tf_op jit(solution)/shard_map/ppermute | solution.py:403
  87.9 19.0 %collective-permute-done.3 = bf16[2,32,256]{2,1,0:T(8,128)(2,1)S(1)} collective-permute-done((bf16[2,32,256]{2,1,0:T(8,128)(2,1)S(1)}, bf16[2,32,256]{2,1,0:T(8,128)(2,1)S(1)}, u32[]{:S(2)}, u32[]{:S(2)}) %collective-permute-start.3) | collective-permute-done | bytes 32800 | tf_op jit(solution)/shard_map/ppermute | solution.py:403
  107.0 1.2 collective-permute-done.4
  108.6 7.5 %collective-permute-start.8 = (bf16[2,2,2,32,256]{4,3,2,1,0:T(8,128)(2,1)S(1)}, bf16[2,2,2,32,256]{4,3,2,1,0:T(8,128)(2,1)S(1)}, u32[]{:S(2)}, u32[]{:S(2)}) collective-permute-start(bf16[2,2,2,32,256]{4,3,2,1,0:T(8,128)(2,1)S(1)} %pad_maximum_fusion.refs_0_), channel_id=1, source_target_pairs={{0,4},{1,5},{2,6},{3,7},{4,0},{5,1},{6,2},{7,3},{8,12},{9,13},{10,... | collective-permute-start | bytes 393224 | tf_op jit(solution)/shard_map/ppermute | solution.py:380
  116.0 2.6 %collective-permute-done.11.refs_7_ = bf16[2,2,2,32,256]{4,3,2,1,0:T(8,128)(2,1)S(1)} collective-permute-done((bf16[2,2,2,32,256]{4,3,2,1,0:T(8,128)(2,1)S(1)}, bf16[2,2,2,32,256]{4,3,2,1,0:T(8,128)(2,1)S(1)}, u32[]{:S(2)}, u32[]{:S(2)}) %collective-permute-start.11) | collective-permute-done | bytes 131104 | tf_op jit(solution)/shard_map/ppermute | solution.py:380
  118.6 3.3 %collective-permute-done.10.refs_6_ = bf16[2,2,2,32,256]{4,3,2,1,0:T(8,128)(2,1)S(1)} collective-permute-done((bf16[2,2,2,32,256]{4,3,2,1,0:T(8,128)(2,1)S(1)}, bf16[2,2,2,32,256]{4,3,2,1,0:T(8,128)(2,1)S(1)}, u32[]{:S(2)}, u32[]{:S(2)}) %collective-permute-start.10) | collective-permute-done | bytes 131104 | tf_op jit(solution)/shard_map/ppermute | solution.py:380
  121.9 5.2 %gram_first.1 = (bf16[2,96,768]{2,1,0:T(8,128)(2,1)S(1)}, bf16[2,96,768]{2,1,0:T(8,128)(2,1)S(1)}, bf16[2,96,768]{2,1,0:T(8,128)(2,1)S(1)}, bf16[2,96,768]{2,1,0...) custom-call(s32[4]{0:T(128)S(1)} %copy-done.15, ...), custom_call_target="tpu_custom_call" | custom-call | flops 2147483648 | bytes 6291456 | tf_op jit(solution)/shard_map/gram_first/pallas_call | solution.py:191
  127.8 2.0 %collective-permute-start.12 = (bf16[2,96,768]{2,1,0:T(8,128)(2,1)S(1)}, bf16[2,96,768]{2,1,0:T(8,128)(2,1)S(1)}, u32[]{:S(2)}, u32[]{:S(2)}) collective-permute-start(bf16[2,96,768]{2,1,0:T(8,128)(2,1)S(1)} %get-tuple-element.16), channel_id=1, source_target_pairs={{0,1},{1,0},{2,3},{3,2},{4,5},{5,4},{6,7},{7,6},{8,9},{9,8},{10,11... | collective-permute-start | bytes 884744 | tf_op jit(solution)/shard_map/ppermute | solution.py:385
  129.8 1.2 weights.1.weight_ref
  131.0 1.3 copy-done
  132.4 1.6 collective-permute-start.14
  134.0 1.1 collective-permute-start.15
  135.1 3.8 %collective-permute-start.16 = (bf16[2,96,768]{2,1,0:T(8,128)(2,1)}, bf16[2,96,768]{2,1,0:T(8,128)(2,1)}, u32[]{:S(2)}, u32[]{:S(2)}) collective-permute-start(bf16[2,96,768]{2,1,0:T(8,128)(2,1)} %get-tuple-element.20), channel_id=1, source_target_pairs={{0,5},{1,4},{2,7},{3,6},{4,1},{5,0},{6,3},{7,2},{8,13},{9,12},{10,... | collective-permute-start | bytes 884744 | tf_op jit(solution)/shard_map/ppermute | solution.py:385
  140.1 11.7 %collective-permute-done.13.refs_2_ = bf16[2,96,768]{2,1,0:T(8,128)(2,1)S(1)} collective-permute-done((bf16[2,96,768]{2,1,0:T(8,128)(2,1)S(1)}, bf16[2,96,768]{2,1,0:T(8,128)(2,1)S(1)}, u32[]{:S(2)}, u32[]{:S(2)}) %collective-permute-start.13) | collective-permute-done | bytes 294944 | tf_op jit(solution)/shard_map/ppermute | solution.py:385
  152.5 1.7 collective-permute-start.18
  154.6 1.1 copy-done.5
  155.8 1.6 beams.1
  158.2 2.0 %reshape.20 = bf16[128,4,2,256]{3,2,1,0:T(2,128)(2,1)} reshape(bf16[512,512]{1,0:T(8,128)(2,1)} %copy-done.2) | data formatting | bytes 1048576 | tf_op jit(solution)/shard_map/reshape | solution.py:428
  160.7 4.9 %collective-permute-done.17.refs_6_ = bf16[2,96,768]{2,1,0:T(8,128)(2,1)} collective-permute-done((bf16[2,96,768]{2,1,0:T(8,128)(2,1)}, bf16[2,96,768]{2,1,0:T(8,128)(2,1)}, u32[]{:S(2)}, u32[]{:S(2)}) %collective-permute-start.17) | collective-permute-done | bytes 294944 | tf_op jit(solution)/shard_map/ppermute | solution.py:385
  165.6 1.0 copy-done.7
  168.4 2.2 %spread_first.1.base_ref = f32[2,96,1024]{2,1,0:T(8,128)S(1)} custom-call(bf16[2,96,768]{2,1,0:T(8,128)(2,1)S(1)} %copy-done.7, bf16[2,96,768]{2,1,0:T(8,128)(2,1)S(1)} %copy-done.9, bf16[2,96,768]{2,1,0:T(8,128)(2,1)S(1)} %copy-done.11, bf16[2,96,768]{2,1,0:T(8,128)(2,1)} %collective-permute-done.14.refs_3_, ...), custom_call_target="tpu_custom_call" | custom-call | flops 536870912 | bytes 4194304 | tf_op jit(solution)/shard_map/spread_first/pallas_call | solution.py:269
  170.7 2.3 %finish.1 = f32[2,128,1024]{2,1,0:T(8,128)S(1)} custom-call(s32[4]{0:T(128)S(1)} %copy-done.15, bf16[8,2,224,256]{3,2,1,0:T(8,128)(2,1)} %all-to-all-done.2.terms_ref, f32[2,96,1024]{2,1,0:T(8,128)S(1)} %spread_first.1.base_ref, bf16[1024,1024]{1,0:T(8,128)(2,1)S(1)} %fusion.refs_8_.order_ref), custom_call_target="tpu_custom_call" | custom-call | flops 536870912 | bytes 4194304 | tf_op jit(solution)/shard_map/finish/pallas_call | solution.py:304
  173.0 1.8 %copy.10 = f32[128,1,2,1024]{3,2,1,0:T(2,128)} copy(f32[128,1,2,1024]{3,0,2,1:T(8,128)S(1)} %bitcast.20) | data formatting | bytes 2097152
  (68 shorter events, 10.5 us)
Async XLA Ops:
  6.4 10.8 %copy-start.3 = (bf16[2,32,4,4096]{3,2,1,0:T(4,128)(2,1)S(1)}, bf16[2,32,4,4096]{3,2,1,0:T(4,128)(2,1)}, u32[]{:S(2)}) copy-start(bf16[2,32,4,4096]{3,2,1,0:T(4,128)(2,1)} %param.7) | copy-start | bytes 6291460
  6.4 10.8 %copy-start.12 = (bf16[256,256]{1,0:T(8,128)(2,1)S(1)}, bf16[256,256]{1,0:T(8,128)(2,1)}, u32[]{:S(2)}) copy-start(bf16[256,256]{1,0:T(8,128)(2,1)} %constant.35.clone.right_hbm) | copy-start | bytes 393220
  6.4 10.8 %copy-start.13 = (f32[2,128,128]{2,1,0:T(8,128)S(1)}, f32[2,128,128]{2,1,0:T(8,128)}, u32[]{:S(2)}) copy-start(f32[2,128,128]{2,1,0:T(8,128)} %constant.34.clone.turn_hbm) | copy-start | bytes 393220
  6.5 10.8 %copy-start.14 = (bf16[256,256]{1,0:T(8,128)(2,1)S(1)}, bf16[256,256]{1,0:T(8,128)(2,1)}, u32[]{:S(2)}) copy-start(bf16[256,256]{1,0:T(8,128)(2,1)} %constant.33.clone.left_hbm) | copy-start | bytes 393220
  6.5 10.8 %copy-start.15 = (s32[4]{0:T(128)S(1)}, s32[4]{0:T(128)}, u32[]{:S(2)}) copy-start(s32[4]{0:T(128)} %pad_add_fusion.place_ref) | copy-start | bytes 52
  6.5 46.3 %all-to-all-start = ((bf16[16,2,24,1024]{3,2,1,0:T(8,128)(2,1)}), bf16[16,2,24,1024]{3,2,1,0:T(8,128)(2,1)}, u32[]{:S(2)}, u32[]{:S(2)}) async-start(bf16[16,2,24,1024]{3,2,1,0:T(8,128)(2,1)} %shard_map.86), calls=%async_computation | async-start | bytes 3145728 | tf_op jit(solution)/shard_map/all_to_all | solution.py:416
  19.3 1.6 collective-permute-start.1
  52.8 23.6 %all-to-all-start.1 = ((bf16[16,16,1024]{2,1,0:T(8,128)(2,1)}), bf16[16,16,1024]{2,1,0:T(8,128)(2,1)S(1)}, u32[]{:S(2)}, u32[]{:S(2)}) async-start(bf16[16,16,1024]{2,1,0:T(8,128)(2,1)} %constant_dynamic-update-slice_fusion), calls=%async_computation.1 | async-start | bytes 1048576 | tf_op jit(solution)/shard_map/all_to_all | solution.py:417
  63.4 13.0 %collective-permute-start = (bf16[384,1024]{1,0:T(8,128)(2,1)S(1)}, bf16[384,1024]{1,0:T(8,128)(2,1)S(1)}, u32[]{:S(2)}, u32[]{:S(2)}) collective-permute-start(bf16[384,1024]{1,0:T(8,128)(2,1)S(1)} %bitcast.28), channel_id=1, source_target_pairs={{0,8},{8,0},{1,9},{9,1},{2,10},{10,2},{3,11},{11,3},{4,12},{12,4},... | collective-permute-start | bytes 2359304 | tf_op jit(solution)/shard_map/ppermute | solution.py:375
  76.4 45.4 %copy-start.4 = (bf16[384,1024]{1,0:T(8,128)(2,1)}, bf16[384,1024]{1,0:T(8,128)(2,1)S(1)}, u32[]{:S(2)}) copy-start(bf16[384,1024]{1,0:T(8,128)(2,1)S(1)} %collective-permute-done.swapped_ref) | copy-start | bytes 2359300
  79.2 4.5 %copy-start.18 = (bf16[2,32,256]{2,1,0:T(8,128)(2,1)S(1)}, bf16[2,32,256]{2,1,0:T(8,128)(2,1)}, u32[]{:S(2)}) copy-start(bf16[2,32,256]{2,1,0:T(8,128)(2,1)} %param.8) | copy-start | bytes 98308
  79.2 91.5 %all-to-all-start.2 = ((bf16[8,2,224,256]{3,2,1,0:T(8,128)(2,1)}), bf16[8,2,224,256]{3,2,1,0:T(8,128)(2,1)}, u32[]{:S(2)}, u32[]{:S(2)}) async-start(bf16[8,2,224,256]{3,2,1,0:T(8,128)(2,1)} %gram_second.1), calls=%async_computation.2 | async-start | bytes 3670016 | tf_op jit(solution)/shard_map/all_to_all | solution.py:424
  83.7 23.1 %collective-permute-start.3 = (bf16[2,32,256]{2,1,0:T(8,128)(2,1)S(1)}, bf16[2,32,256]{2,1,0:T(8,128)(2,1)S(1)}, u32[]{:S(2)}, u32[]{:S(2)}) collective-permute-start(bf16[2,32,256]{2,1,0:T(8,128)(2,1)S(1)} %copy-done.18), channel_id=1, source_target_pairs={{0,128},{1,145},{2,162},{3,179},{4,196},{5,213},{6,230},{7,247},{1... | collective-permute-start | bytes 98312 | tf_op jit(solution)/shard_map/ppermute | solution.py:403
  87.2 19.7 %collective-permute-start.2 = (bf16[2,32,256]{2,1,0:T(8,128)(2,1)S(1)}, bf16[2,32,256]{2,1,0:T(8,128)(2,1)S(1)}, u32[]{:S(2)}, u32[]{:S(2)}) collective-permute-start(bf16[2,32,256]{2,1,0:T(8,128)(2,1)S(1)} %copy-done.18), channel_id=1, source_target_pairs={{0,0},{1,17},{2,34},{3,51},{4,68},{5,85},{6,102},{7,119},{16,16},{... | collective-permute-start | bytes 98312 | tf_op jit(solution)/shard_map/ppermute | solution.py:403
  106.9 1.3 collective-permute-start.4
  108.3 10.3 %collective-permute-start.11 = (bf16[2,2,2,32,256]{4,3,2,1,0:T(8,128)(2,1)S(1)}, bf16[2,2,2,32,256]{4,3,2,1,0:T(8,128)(2,1)S(1)}, u32[]{:S(2)}, u32[]{:S(2)}) collective-permute-start(bf16[2,2,2,32,256]{4,3,2,1,0:T(8,128)(2,1)S(1)} %pad_maximum_fusion.refs_0_), channel_id=1, source_target_pairs={{0,7},{1,6},{2,5},{3,4},{4,3},{5,2},{6,1},{7,0},{8,15},{9,14},{10,... | collective-permute-start | bytes 393224 | tf_op jit(solution)/shard_map/ppermute | solution.py:380
  108.4 13.5 %collective-permute-start.10 = (bf16[2,2,2,32,256]{4,3,2,1,0:T(8,128)(2,1)S(1)}, bf16[2,2,2,32,256]{4,3,2,1,0:T(8,128)(2,1)S(1)}, u32[]{:S(2)}, u32[]{:S(2)}) collective-permute-start(bf16[2,2,2,32,256]{4,3,2,1,0:T(8,128)(2,1)S(1)} %pad_maximum_fusion.refs_0_), channel_id=1, source_target_pairs={{0,6},{1,7},{2,4},{3,5},{4,2},{5,3},{6,0},{7,1},{8,14},{9,15},{10,... | collective-permute-start | bytes 393224 | tf_op jit(solution)/shard_map/ppermute | solution.py:380
  108.5 19.3 %collective-permute-start.9 = (bf16[2,2,2,32,256]{4,3,2,1,0:T(8,128)(2,1)S(1)}, bf16[2,2,2,32,256]{4,3,2,1,0:T(8,128)(2,1)S(1)}, u32[]{:S(2)}, u32[]{:S(2)}) collective-permute-start(bf16[2,2,2,32,256]{4,3,2,1,0:T(8,128)(2,1)S(1)} %pad_maximum_fusion.refs_0_), channel_id=1, source_target_pairs={{0,5},{1,4},{2,7},{3,6},{4,1},{5,0},{6,3},{7,2},{8,13},{9,12},{10,... | collective-permute-start | bytes 393224 | tf_op jit(solution)/shard_map/ppermute | solution.py:380
  108.6 21.3 %collective-permute-start.8 = (bf16[2,2,2,32,256]{4,3,2,1,0:T(8,128)(2,1)S(1)}, bf16[2,2,2,32,256]{4,3,2,1,0:T(8,128)(2,1)S(1)}, u32[]{:S(2)}, u32[]{:S(2)}) collective-permute-start(bf16[2,2,2,32,256]{4,3,2,1,0:T(8,128)(2,1)S(1)} %pad_maximum_fusion.refs_0_), channel_id=1, source_target_pairs={{0,4},{1,5},{2,6},{3,7},{4,0},{5,1},{6,2},{7,3},{8,12},{9,13},{10,... | collective-permute-start | bytes 393224 | tf_op jit(solution)/shard_map/ppermute | solution.py:380
  116.0 13.8 %collective-permute-start.7 = (bf16[2,2,2,32,256]{4,3,2,1,0:T(8,128)(2,1)S(1)}, bf16[2,2,2,32,256]{4,3,2,1,0:T(8,128)(2,1)S(1)}, u32[]{:S(2)}, u32[]{:S(2)}) collective-permute-start(bf16[2,2,2,32,256]{4,3,2,1,0:T(8,128)(2,1)S(1)} %pad_maximum_fusion.refs_0_), channel_id=1, source_target_pairs={{0,3},{1,2},{2,1},{3,0},{4,7},{5,6},{6,5},{7,4},{8,11},{9,10},{10,... | collective-permute-start | bytes 393224 | tf_op jit(solution)/shard_map/ppermute | solution.py:380
  118.6 11.2 %collective-permute-start.6 = (bf16[2,2,2,32,256]{4,3,2,1,0:T(8,128)(2,1)S(1)}, bf16[2,2,2,32,256]{4,3,2,1,0:T(8,128)(2,1)S(1)}, u32[]{:S(2)}, u32[]{:S(2)}) collective-permute-start(bf16[2,2,2,32,256]{4,3,2,1,0:T(8,128)(2,1)S(1)} %pad_maximum_fusion.refs_0_), channel_id=1, source_target_pairs={{0,2},{1,3},{2,0},{3,1},{4,6},{5,7},{6,4},{7,5},{8,10},{9,11},{10,... | collective-permute-start | bytes 393224 | tf_op jit(solution)/shard_map/ppermute | solution.py:380
  121.8 8.0 %collective-permute-start.5 = (bf16[2,2,2,32,256]{4,3,2,1,0:T(8,128)(2,1)S(1)}, bf16[2,2,2,32,256]{4,3,2,1,0:T(8,128)(2,1)S(1)}, u32[]{:S(2)}, u32[]{:S(2)}) collective-permute-start(bf16[2,2,2,32,256]{4,3,2,1,0:T(8,128)(2,1)S(1)} %pad_maximum_fusion.refs_0_), channel_id=1, source_target_pairs={{0,1},{1,0},{2,3},{3,2},{4,5},{5,4},{6,7},{7,6},{8,9},{9,8},{10,11... | collective-permute-start | bytes 393224 | tf_op jit(solution)/shard_map/ppermute | solution.py:380
  127.8 4.6 %copy-start.16 = (s32[1024]{0:T(1024)S(1)}, s32[1024]{0:T(1024)}, u32[]{:S(2)}) copy-start(s32[1024]{0:T(1024)} %constant.37.clone) | copy-start | bytes 12292
  127.8 4.6 %copy-start.17 = (s32[1024]{0:T(1024)S(1)}, s32[1024]{0:T(1024)}, u32[]{:S(2)}) copy-start(s32[1024]{0:T(1024)} %constant.36.clone) | copy-start | bytes 12292
  127.8 11.1 %collective-permute-start.12 = (bf16[2,96,768]{2,1,0:T(8,128)(2,1)S(1)}, bf16[2,96,768]{2,1,0:T(8,128)(2,1)S(1)}, u32[]{:S(2)}, u32[]{:S(2)}) collective-permute-start(bf16[2,96,768]{2,1,0:T(8,128)(2,1)S(1)} %get-tuple-element.16), channel_id=1, source_target_pairs={{0,1},{1,0},{2,3},{3,2},{4,5},{5,4},{6,7},{7,6},{8,9},{9,8},{10,11... | collective-permute-start | bytes 884744 | tf_op jit(solution)/shard_map/ppermute | solution.py:385
  129.8 22.0 %collective-permute-start.13 = (bf16[2,96,768]{2,1,0:T(8,128)(2,1)S(1)}, bf16[2,96,768]{2,1,0:T(8,128)(2,1)S(1)}, u32[]{:S(2)}, u32[]{:S(2)}) collective-permute-start(bf16[2,96,768]{2,1,0:T(8,128)(2,1)S(1)} %get-tuple-element.17), channel_id=1, source_target_pairs={{0,2},{1,3},{2,0},{3,1},{4,6},{5,7},{6,4},{7,5},{8,10},{9,11},{10,... | collective-permute-start | bytes 884744 | tf_op jit(solution)/shard_map/ppermute | solution.py:385
  132.4 22.2 %copy-start.1 = (bf16[512,2048]{1,0:T(8,128)(2,1)S(1)}, bf16[512,2048]{1,0:T(8,128)(2,1)}, u32[]{:S(2)}) copy-start(bf16[512,2048]{1,0:T(8,128)(2,1)} %copy-done) | copy-start | bytes 6291460
  132.4 27.7 %collective-permute-start.14 = (bf16[2,96,768]{2,1,0:T(8,128)(2,1)}, bf16[2,96,768]{2,1,0:T(8,128)(2,1)}, u32[]{:S(2)}, u32[]{:S(2)}) collective-permute-start(bf16[2,96,768]{2,1,0:T(8,128)(2,1)} %get-tuple-element.18), channel_id=1, source_target_pairs={{0,3},{1,2},{2,1},{3,0},{4,7},{5,6},{6,5},{7,4},{8,11},{9,10},{10,... | collective-permute-start | bytes 884744 | tf_op jit(solution)/shard_map/ppermute | solution.py:385
  134.0 26.7 %collective-permute-start.15 = (bf16[2,96,768]{2,1,0:T(8,128)(2,1)}, bf16[2,96,768]{2,1,0:T(8,128)(2,1)}, u32[]{:S(2)}, u32[]{:S(2)}) collective-permute-start(bf16[2,96,768]{2,1,0:T(8,128)(2,1)} %get-tuple-element.19), channel_id=1, source_target_pairs={{0,4},{1,5},{2,6},{3,7},{4,0},{5,1},{6,2},{7,3},{8,12},{9,13},{10,... | collective-permute-start | bytes 884744 | tf_op jit(solution)/shard_map/ppermute | solution.py:385
  135.1 25.6 %collective-permute-start.16 = (bf16[2,96,768]{2,1,0:T(8,128)(2,1)}, bf16[2,96,768]{2,1,0:T(8,128)(2,1)}, u32[]{:S(2)}, u32[]{:S(2)}) collective-permute-start(bf16[2,96,768]{2,1,0:T(8,128)(2,1)} %get-tuple-element.20), channel_id=1, source_target_pairs={{0,5},{1,4},{2,7},{3,6},{4,1},{5,0},{6,3},{7,2},{8,13},{9,12},{10,... | collective-permute-start | bytes 884744 | tf_op jit(solution)/shard_map/ppermute | solution.py:385
  139.6 25.9 %collective-permute-start.17 = (bf16[2,96,768]{2,1,0:T(8,128)(2,1)}, bf16[2,96,768]{2,1,0:T(8,128)(2,1)}, u32[]{:S(2)}, u32[]{:S(2)}) collective-permute-start(bf16[2,96,768]{2,1,0:T(8,128)(2,1)} %get-tuple-element.21), channel_id=1, source_target_pairs={{0,6},{1,7},{2,4},{3,5},{4,2},{5,3},{6,0},{7,1},{8,14},{9,15},{10,... | collective-permute-start | bytes 884744 | tf_op jit(solution)/shard_map/ppermute | solution.py:385
  152.5 13.1 %collective-permute-start.18 = (bf16[2,96,768]{2,1,0:T(8,128)(2,1)}, bf16[2,96,768]{2,1,0:T(8,128)(2,1)}, u32[]{:S(2)}, u32[]{:S(2)}) collective-permute-start(bf16[2,96,768]{2,1,0:T(8,128)(2,1)} %get-tuple-element.22), channel_id=1, source_target_pairs={{0,7},{1,6},{2,5},{3,4},{4,3},{5,2},{6,1},{7,0},{8,15},{9,14},{10,... | collective-permute-start | bytes 884744 | tf_op jit(solution)/shard_map/ppermute | solution.py:385
  (9 other events, 8.3 us)

commit v4 on v3

--- a/solution.py
+++ b/solution.py
@@ -17,10 +17,11 @@
 CHIPS = 16
 N_TM = 8
 SPECTRA = 4
-FIRST, SECOND = 24, 8
+FIRST, SECOND = 16, 16
 SIDE_A, SIDE_B = CHIPS * FIRST, CHIPS * SECOND
 OWN_A, OWN_B = SIDE_A // N_TM, SIDE_B // N_TM
 COLS_A, COLS_B = 2 * SIDE_A, 2 * SIDE_B
+PIECES = COLS_A // COLS_B
 HALF = 512
 BF16 = jnp.bfloat16
 F32 = jnp.float32
@@ -84,7 +85,7 @@
 def dft_kernel(place_ref, x_hbm, left_hbm, turn_hbm, right_hbm, *refs):
     outs, (x_ref, left_ref, turn_ref, right_ref, stage, sems, pack, out_sems) = refs[:-8], refs[-8:]
     count = x_ref.shape[1]
-    start = 0 if count == FIRST else FIRST
+    start = 0 if len(outs) == 1 else FIRST
     loads = [
         pltpu.make_async_copy(left_hbm, left_ref, sems.at[0]),
         pltpu.make_async_copy(turn_hbm, turn_ref, sems.at[1]),
@@ -140,14 +141,14 @@
         store.wait()
 
 
-def dft_part(place, signal, tables, count):
+def dft_part(place, signal, tables, count, lead):
     full = pltpu.HBM((CHIPS, 2, count, 1024), BF16)
     half = jax.ShapeDtypeStruct((CHIPS, count, 1024), BF16)
-    shapes = (full,) if count == FIRST else (half, half)
+    shapes = (full,) if lead else (half, half)
     return pl.pallas_call(
         dft_kernel,
         in_specs=[SMEM] + [HBM] * 4,
-        out_specs=(HBM,) if count == FIRST else (VMEM, VMEM),
+        out_specs=(HBM,) if lead else (VMEM, VMEM),
         out_shape=shapes,
         scratch_shapes=[
             pltpu.VMEM((2, count, 128, 128), BF16),
@@ -156,11 +157,12 @@
             pltpu.VMEM((256, 256), BF16),
             pltpu.VMEM((256 * count, 128), F32),
             pltpu.SemaphoreType.DMA((3 + count // 8,)),
-            pltpu.VMEM((CHIPS if count == FIRST else 1, 2, count, 1024), BF16),
+            pltpu.VMEM((CHIPS if lead else 1, 2, count, 1024), BF16),
             pltpu.SemaphoreType.DMA((CHIPS,)),
         ],
-        compiler_params=params(60 if count == FIRST else 12),
+        compiler_params=params(60 if lead else 12),
         cost_estimate=cost(count << 25, count << 17),
+        name="dft_lead" if lead else "dft_rest",
     )(place, signal, *tables)
 
 
@@ -209,14 +211,14 @@
         first = jnp.concatenate([sides[0][q], sides[1][q]], 1)
         flipped = first.T
         flipped = (-flipped if q else flipped).astype(BF16)
-        blocks = [first[:, COLS_B * j : COLS_B * j + COLS_B].astype(BF16) for j in range(3)]
+        blocks = [first[:, COLS_B * j : COLS_B * j + COLS_B].astype(BF16) for j in range(PIECES)]
         blocks.append(second[q].astype(BF16))
         rows = 2 * OWN_B
         for r in range(N_TM):
-            for j in range(4):
+            for j in range(PIECES + 1):
                 out_ref[r, q, rows * j : rows * j + rows, :] = blocks[j][rows * r : rows * r + rows]
             for a in (0, 1):
-                row = 4 * rows + OWN_A * a
+                row = (PIECES + 1) * rows + OWN_A * a
                 src = SIDE_A * a + OWN_A * r
                 out_ref[r, q, row : row + OWN_A, :] = flipped[src : src + OWN_A]
         copies.append(pltpu.make_async_copy(out_ref.at[:, q], out_hbm.at[:, q], sems.at[q]))
@@ -226,7 +228,7 @@
 
 
 def gram_second(mine, kept, swapped):
-    rows = 8 * OWN_B + 2 * OWN_A
+    rows = 2 * (PIECES + 1) * OWN_B + 2 * OWN_A
     return pl.pallas_call(
         gram_second_kernel,
         in_specs=[VMEM, VMEM, VMEM],
@@ -236,7 +238,7 @@
             pltpu.VMEM((N_TM, 2, rows, COLS_B), BF16),
             pltpu.SemaphoreType.DMA((2,)),
         ],
-        compiler_params=params(10),
+        compiler_params=params(14),
         cost_estimate=cost(1 << 29, 6 << 20),
         name="gram_second",
     )(mine, kept, swapped)
@@ -285,8 +287,8 @@
         total = terms_ref[0, q].astype(F32)
         for t in range(1, N_TM):
             total = total + terms_ref[t, q].astype(F32)
-        last.append(jnp.concatenate([total[rows * j : rows * j + rows] for j in range(4)], 1))
-        extra.append(total[4 * rows :])
+        last.append(jnp.concatenate([total[rows * j : rows * j + rows] for j in range(PIECES + 1)], 1))
+        extra.append(total[(PIECES + 1) * rows :])
     lower = placed(last, order_ref[...])
     upper = placed(extra, order_ref[COLS_A:, :])
     for q in (0, 1):
@@ -402,8 +404,8 @@
     rings = [[(at(x, z, t), at(x ^ dx, z + t, t)) for x, z, t in spots] for dx in (0, 1)]
     block = jnp.stack([lax.ppermute(beam_weights, (*CHIP, *TM), ring) for ring in rings])
 
-    (ready_a,) = dft_part(place, signal, tables, FIRST)
-    own_b, other_b = dft_part(place, signal, tables, SECOND)
+    (ready_a,) = dft_part(place, signal, tables, FIRST, True)
+    own_b, other_b = dft_part(place, signal, tables, SECOND, False)
     partner_b = swap(other_b, "stat_2")
     ready_b = jnp.concatenate([own_b, partner_b], 1)
 

time: 177 us -> 177 us (level)
  waiting for transfers between devices: 88.2 us -> 91.4 us
  local copies, waits for them, and re-layouts: 15 us -> 12.9 us
    ppermute x2, waiting for transfers between devices: 19 us -> 35.1 us  [step(): lax.ppermute(beam_weights, (*CHIP, *TM), ring)]
    ppermute x7, waiting for transfers between devices: 17.1 us -> 1.18 us  [to_partners(): lax.ppermute(arrays[k], TM, pairs(k))]
    all_to_all x1, waiting for transfers between devices: 31.2 us -> 18.8 us  [step(): arrived = lax.all_to_all(ready_a, CHIP, 0, 0, tiled=True)]
    all_to_all x1, waiting for transfers between devices: 12.9 us -> 21.3 us  [step(): lax.all_to_all(ready_b, CHIP, 0, 0, tiled=True).reshape(COLS_B, 1024)]
    ppermute x7, waiting for transfers between devices: 5.85 us -> 10.8 us  [with_partners(): return [array] + [lax.ppermute(array, TM, pairs(k)) for k in range(1, N_TM)]]
    pallas_call x1, Pallas kernels: 5.22 us -> 2.73 us  [gram_first(): pl.pallas_call(gram_first_kernel, in_specs=[SMEM, VMEM, VMEM], out_specs=...]
    ppermute x3, waiting for transfers between devices: 2.04 us -> 4.18 us  [swap(): return lax.ppermute(array, axis, [(0, 1), (1, 0)])]
    unnamed x40 -> x36, local copies, waits for them, and re-layouts: 10.8 us -> 8.78 us
  transfers between devices with their start and end apart: 22 -> 22, of which waited for: 10 -> 12; matrix products, arithmetic and copies ran while one was open for 3% -> 3% of each run, Pallas kernels for 7% -> 6%
where the time goes in v4:
time: 177 us; the launch traced here: 176 us
  waiting for transfers between devices  91.4 us (52%)
  starting transfers between devices  48.5 us (27%)
  Pallas kernels  21.3 us (12%)
  local copies, waits for them, and re-layouts  12.9 us (7%)
    ppermute x2, waiting for transfers between devices, step(): lax.ppermute(beam_weights, (*CHIP, *TM), ring)  35.1 us
    all_to_all x1, waiting for transfers between devices, step(): lax.all_to_all(ready_b, CHIP, 0, 0, tiled=True).reshape(COLS_B, 1024)  21.3 us
    all_to_all x1, waiting for transfers between devices, step(): arrived = lax.all_to_all(ready_a, CHIP, 0, 0, tiled=True)  18.8 us
    ppermute x7, starting transfers between devices, to_partners(): lax.ppermute(arrays[k], TM, pairs(k))  12.7 us
    ppermute x7, waiting for transfers between devices, with_partners(): return [array] + [lax.ppermute(array, TM, pairs(k)) for k in range(1, N_TM)]  10.8 us
    all_to_all x1, starting transfers between devices, step(): arrived = lax.all_to_all(ready_a, CHIP, 0, 0, tiled=True)  10.6 us
    unnamed x36, local copies, waits for them, and re-layouts  8.78 us
    all_to_all x1, starting transfers between devices, step(): lax.all_to_all(ready_b, CHIP, 0, 0, tiled=True).reshape(COLS_B, 1024)  8.37 us
  transfers between devices with their start and end apart: 22, of which 12 were waited for; matrix products, arithmetic and copies ran while one was open for 3% of the time, Pallas kernels for 6%

profile of v4, /device:TPU:64, one launch (start us, length us, event | category | flops | bytes accessed | tf_op | source)
XLA Modules:
  0.0 176.0 jit_solution(7686926640455021950)
XLA Ops:
  1.4 4.7 %dft_lead.1 = bf16[16,2,16,1024]{3,2,1,0:T(8,128)(2,1)} custom-call(s32[4]{0:T(128)} %pad_add_fusion.place_ref, bf16[2,32,128,128]{3,2,1,0:T(8,128)(2,1)} %bitcast.26, bf16[256,256]{1,0:T(8,128)(2,1)} %constant.33.clone.left_hbm, f32[2,128,128]{2,1,0:T(8,128)} %constant.34.clone.turn_hbm, bf16[256,256]{1,0:T(8,128)(2,1)} %constant.35.clone.right_hbm), custom_call_target="tpu_custom_call" | custom-call | flops 1073741824 | bytes 2097152 | tf_op jit(solution)/shard_map/dft_lead/pallas_call | solution.py:148
  6.0 10.6 %all-to-all-start = ((bf16[16,2,16,1024]{3,2,1,0:T(8,128)(2,1)}), bf16[16,2,16,1024]{3,2,1,0:T(8,128)(2,1)}, u32[]{:S(2)}, u32[]{:S(2)}) async-start(bf16[16,2,16,1024]{3,2,1,0:T(8,128)(2,1)} %dft_lead.1), calls=%async_computation | async-start | bytes 2097152 | tf_op jit(solution)/shard_map/all_to_all | solution.py:418
  16.7 3.0 %dft_rest.1 = (bf16[16,16,1024]{2,1,0:T(8,128)(2,1)S(1)}, bf16[16,16,1024]{2,1,0:T(8,128)(2,1)S(1)}) custom-call(s32[4]{0:T(128)S(1)} %copy-done.9, bf16[2,32,128,128]{3,2,1,0:T(8,128)(2,1)S(1)} %bitcast.27, bf16[256,256]{1,0:T(8,128)(2,1)S(1)} %copy-done.13, f32[2,128,128]{2,1,0:T(8,128)S(1)} %copy-done.12, bf16[256,256]{1,0:T(8,128)(2,1)S(1)} %copy-done.11), custom_call_target="tpu_custom_call" | custom-call | flops 1073741824 | bytes 2097152 | tf_op jit(solution)/shard_map/dft_rest/pallas_call | solution.py:148
  22.5 18.8 %all-to-all-done = bf16[16,2,16,1024]{3,2,1,0:T(8,128)(2,1)} async-done(((bf16[16,2,16,1024]{3,2,1,0:T(8,128)(2,1)}), bf16[16,2,16,1024]{3,2,1,0:T(8,128)(2,1)}, u32[]{:S(2)}, u32[]{:S(2)}) %all-to-all-start) | async-done | bytes 1048608 | tf_op jit(solution)/shard_map/all_to_all | solution.py:418
  41.4 8.4 %all-to-all-start.1 = ((bf16[16,32,1024]{2,1,0:T(8,128)(2,1)}), bf16[16,32,1024]{2,1,0:T(8,128)(2,1)S(1)}, u32[]{:S(2)}, u32[]{:S(2)}) async-start(bf16[16,32,1024]{2,1,0:T(8,128)(2,1)} %constant_dynamic-update-slice_fusion), calls=%async_computation.1 | async-start | bytes 2097152 | tf_op jit(solution)/shard_map/all_to_all | solution.py:419
  49.7 1.3 fusion.2
  51.1 1.9 %collective-permute-done.swapped_ref = bf16[256,1024]{1,0:T(8,128)(2,1)S(1)} collective-permute-done((bf16[256,1024]{1,0:T(8,128)(2,1)S(1)}, bf16[256,1024]{1,0:T(8,128)(2,1)S(1)}, u32[]{:S(2)}, u32[]{:S(2)}) %collective-permute-start) | collective-permute-done | bytes 524320 | tf_op jit(solution)/shard_map/ppermute | solution.py:377
  53.0 21.3 %all-to-all-done.1 = bf16[16,32,1024]{2,1,0:T(8,128)(2,1)S(1)} async-done(((bf16[16,32,1024]{2,1,0:T(8,128)(2,1)}), bf16[16,32,1024]{2,1,0:T(8,128)(2,1)S(1)}, u32[]{:S(2)}, u32[]{:S(2)}) %all-to-all-start.1) | async-done | bytes 1048608 | tf_op jit(solution)/shard_map/all_to_all | solution.py:419
  74.3 3.6 %gram_second.1 = bf16[8,2,192,512]{3,2,1,0:T(8,128)(2,1)} custom-call(bf16[512,1024]{1,0:T(8,128)(2,1)S(1)} %bitcast.20, bf16[256,1024]{1,0:T(8,128)(2,1)S(1)} %bitcast.22, bf16[256,1024]{1,0:T(8,128)(2,1)S(1)} %collective-permute-done.swapped_ref), custom_call_target="tpu_custom_call" | custom-call | flops 1073741824 | bytes 6291456 | tf_op jit(solution)/shard_map/gram_second/pallas_call | solution.py:232
  78.0 4.5 %all-to-all-start.2 = ((bf16[8,2,192,512]{3,2,1,0:T(8,128)(2,1)}), bf16[8,2,192,512]{3,2,1,0:T(8,128)(2,1)}, u32[]{:S(2)}, u32[]{:S(2)}) async-start(bf16[8,2,192,512]{3,2,1,0:T(8,128)(2,1)} %gram_second.1), calls=%async_computation.2 | async-start | bytes 6291456 | tf_op jit(solution)/shard_map/all_to_all | solution.py:426
  82.5 3.6 %collective-permute-start.3 = (bf16[2,32,256]{2,1,0:T(8,128)(2,1)S(1)}, bf16[2,32,256]{2,1,0:T(8,128)(2,1)S(1)}, u32[]{:S(2)}, u32[]{:S(2)}) collective-permute-start(bf16[2,32,256]{2,1,0:T(8,128)(2,1)S(1)} %copy-done.16), channel_id=1, source_target_pairs={{0,128},{1,145},{2,162},{3,179},{4,196},{5,213},{6,230},{7,247},{1... | collective-permute-start | bytes 98312 | tf_op jit(solution)/shard_map/ppermute | solution.py:405
  86.8 35.1 %collective-permute-done.3 = bf16[2,32,256]{2,1,0:T(8,128)(2,1)S(1)} collective-permute-done((bf16[2,32,256]{2,1,0:T(8,128)(2,1)S(1)}, bf16[2,32,256]{2,1,0:T(8,128)(2,1)S(1)}, u32[]{:S(2)}, u32[]{:S(2)}) %collective-permute-start.3) | collective-permute-done | bytes 32800 | tf_op jit(solution)/shard_map/ppermute | solution.py:405
  122.0 1.2 collective-permute-done.4
  123.6 7.5 %collective-permute-start.8 = (bf16[2,2,2,32,256]{4,3,2,1,0:T(8,128)(2,1)S(1)}, bf16[2,2,2,32,256]{4,3,2,1,0:T(8,128)(2,1)S(1)}, u32[]{:S(2)}, u32[]{:S(2)}) collective-permute-start(bf16[2,2,2,32,256]{4,3,2,1,0:T(8,128)(2,1)S(1)} %pad_maximum_fusion.refs_0_), channel_id=1, source_target_pairs={{0,4},{1,5},{2,6},{3,7},{4,0},{5,1},{6,2},{7,3},{8,12},{9,13},{10,... | collective-permute-start | bytes 393224 | tf_op jit(solution)/shard_map/ppermute | solution.py:382
  131.0 2.6 %collective-permute-done.11.refs_7_ = bf16[2,2,2,32,256]{4,3,2,1,0:T(8,128)(2,1)S(1)} collective-permute-done((bf16[2,2,2,32,256]{4,3,2,1,0:T(8,128)(2,1)S(1)}, bf16[2,2,2,32,256]{4,3,2,1,0:T(8,128)(2,1)S(1)}, u32[]{:S(2)}, u32[]{:S(2)}) %collective-permute-start.11) | collective-permute-done | bytes 131104 | tf_op jit(solution)/shard_map/ppermute | solution.py:382
  133.6 3.3 %collective-permute-done.10.refs_6_ = bf16[2,2,2,32,256]{4,3,2,1,0:T(8,128)(2,1)S(1)} collective-permute-done((bf16[2,2,2,32,256]{4,3,2,1,0:T(8,128)(2,1)S(1)}, bf16[2,2,2,32,256]{4,3,2,1,0:T(8,128)(2,1)S(1)}, u32[]{:S(2)}, u32[]{:S(2)}) %collective-permute-start.10) | collective-permute-done | bytes 131104 | tf_op jit(solution)/shard_map/ppermute | solution.py:382
  136.9 2.3 %collective-permute-done.8.refs_4_ = bf16[2,2,2,32,256]{4,3,2,1,0:T(8,128)(2,1)S(1)} collective-permute-done((bf16[2,2,2,32,256]{4,3,2,1,0:T(8,128)(2,1)S(1)}, bf16[2,2,2,32,256]{4,3,2,1,0:T(8,128)(2,1)S(1)}, u32[]{:S(2)}, u32[]{:S(2)}) %collective-permute-start.8) | collective-permute-done | bytes 131104 | tf_op jit(solution)/shard_map/ppermute | solution.py:382
  140.0 1.8 %collective-permute-done.5.refs_1_ = bf16[2,2,2,32,256]{4,3,2,1,0:T(8,128)(2,1)S(1)} collective-permute-done((bf16[2,2,2,32,256]{4,3,2,1,0:T(8,128)(2,1)S(1)}, bf16[2,2,2,32,256]{4,3,2,1,0:T(8,128)(2,1)S(1)}, u32[]{:S(2)}, u32[]{:S(2)}) %collective-permute-start.5) | collective-permute-done | bytes 131104 | tf_op jit(solution)/shard_map/ppermute | solution.py:382
  141.8 1.2 weights.1.weight_ref
  143.0 1.4 copy-done
  144.4 2.7 %gram_first.1 = (bf16[2,64,512]{2,1,0:T(8,128)(2,1)S(1)}, bf16[2,64,512]{2,1,0:T(8,128)(2,1)S(1)}, bf16[2,64,512]{2,1,0:T(8,128)(2,1)S(1)}, bf16[2,64,512]{2,1,0...) custom-call(s32[4]{0:T(128)S(1)} %copy-done.9, ...), custom_call_target="tpu_custom_call" | custom-call | flops 2147483648 | bytes 6291456 | tf_op jit(solution)/shard_map/gram_first/pallas_call | solution.py:193
  147.2 3.5 %collective-permute-start.14 = (bf16[2,64,512]{2,1,0:T(8,128)(2,1)}, bf16[2,64,512]{2,1,0:T(8,128)(2,1)}, u32[]{:S(2)}, u32[]{:S(2)}) collective-permute-start(bf16[2,64,512]{2,1,0:T(8,128)(2,1)} %get-tuple-element.18), channel_id=1, source_target_pairs={{0,3},{1,2},{2,1},{3,0},{4,7},{5,6},{6,5},{7,4},{8,11},{9,10},{10,... | collective-permute-start | bytes 393224 | tf_op jit(solution)/shard_map/ppermute | solution.py:387
  150.8 1.9 %collective-permute-start.15 = (bf16[2,64,512]{2,1,0:T(8,128)(2,1)}, bf16[2,64,512]{2,1,0:T(8,128)(2,1)}, u32[]{:S(2)}, u32[]{:S(2)}) collective-permute-start(bf16[2,64,512]{2,1,0:T(8,128)(2,1)} %get-tuple-element.19), channel_id=1, source_target_pairs={{0,4},{1,5},{2,6},{3,7},{4,0},{5,1},{6,2},{7,3},{8,12},{9,13},{10,... | collective-permute-start | bytes 393224 | tf_op jit(solution)/shard_map/ppermute | solution.py:387
  152.7 1.1 collective-permute-start.16
  153.7 2.0 %collective-permute-start.17 = (bf16[2,64,512]{2,1,0:T(8,128)(2,1)}, bf16[2,64,512]{2,1,0:T(8,128)(2,1)}, u32[]{:S(2)}, u32[]{:S(2)}) collective-permute-start(bf16[2,64,512]{2,1,0:T(8,128)(2,1)} %get-tuple-element.21), channel_id=1, source_target_pairs={{0,6},{1,7},{2,4},{3,5},{4,2},{5,3},{6,0},{7,1},{8,14},{9,15},{10,... | collective-permute-start | bytes 393224 | tf_op jit(solution)/shard_map/ppermute | solution.py:387
  155.7 1.2 collective-permute-done.13.refs_2_
  156.9 4.2 %collective-permute-start.18 = (bf16[2,64,512]{2,1,0:T(8,128)(2,1)}, bf16[2,64,512]{2,1,0:T(8,128)(2,1)}, u32[]{:S(2)}, u32[]{:S(2)}) collective-permute-start(bf16[2,64,512]{2,1,0:T(8,128)(2,1)} %get-tuple-element.22), channel_id=1, source_target_pairs={{0,7},{1,6},{2,5},{3,4},{4,3},{5,2},{6,1},{7,0},{8,15},{9,14},{10,... | collective-permute-start | bytes 393224 | tf_op jit(solution)/shard_map/ppermute | solution.py:387
  163.6 1.3 beams.1
  165.7 2.0 %reshape.20 = bf16[128,4,2,256]{3,2,1,0:T(2,128)(2,1)} reshape(bf16[512,512]{1,0:T(8,128)(2,1)} %copy-done.6) | data formatting | bytes 1048576 | tf_op jit(solution)/shard_map/reshape | solution.py:430
  167.7 1.7 spread_first.1.base_ref
  171.2 3.0 %finish.1 = f32[2,128,1024]{2,1,0:T(8,128)S(1)} custom-call(s32[4]{0:T(128)S(1)} %copy-done.9, bf16[8,2,192,512]{3,2,1,0:T(8,128)(2,1)} %all-to-all-done.2.terms_ref, f32[2,64,1024]{2,1,0:T(8,128)S(1)} %copy-done.8, bf16[1024,1024]{1,0:T(8,128)(2,1)S(1)} %fusion.refs_8_.order_ref), custom_call_target="tpu_custom_call" | custom-call | flops 536870912 | bytes 4194304 | tf_op jit(solution)/shard_map/finish/pallas_call | solution.py:306
  174.3 1.8 %copy.10 = f32[128,1,2,1024]{3,2,1,0:T(2,128)} copy(f32[128,1,2,1024]{3,0,2,1:T(8,128)S(1)} %bitcast.25) | data formatting | bytes 2097152
  (64 shorter events, 10.7 us)
Async XLA Ops:
  0.6 16.0 %copy-start.11 = (bf16[256,256]{1,0:T(8,128)(2,1)S(1)}, bf16[256,256]{1,0:T(8,128)(2,1)}, u32[]{:S(2)}) copy-start(bf16[256,256]{1,0:T(8,128)(2,1)} %constant.35.clone.right_hbm) | copy-start | bytes 393220
  0.6 16.0 %copy-start.12 = (f32[2,128,128]{2,1,0:T(8,128)S(1)}, f32[2,128,128]{2,1,0:T(8,128)}, u32[]{:S(2)}) copy-start(f32[2,128,128]{2,1,0:T(8,128)} %constant.34.clone.turn_hbm) | copy-start | bytes 393220
  0.7 16.0 %copy-start.13 = (bf16[256,256]{1,0:T(8,128)(2,1)S(1)}, bf16[256,256]{1,0:T(8,128)(2,1)}, u32[]{:S(2)}) copy-start(bf16[256,256]{1,0:T(8,128)(2,1)} %constant.33.clone.left_hbm) | copy-start | bytes 393220
  0.7 16.0 %copy-start.10 = (bf16[2,32,4,4096]{3,2,1,0:T(4,128)(2,1)S(1)}, bf16[2,32,4,4096]{3,2,1,0:T(4,128)(2,1)}, u32[]{:S(2)}) copy-start(bf16[2,32,4,4096]{3,2,1,0:T(4,128)(2,1)} %param.7) | copy-start | bytes 6291460
  1.4 15.3 %copy-start.9 = (s32[4]{0:T(128)S(1)}, s32[4]{0:T(128)}, u32[]{:S(2)}) copy-start(s32[4]{0:T(128)} %pad_add_fusion.place_ref) | copy-start | bytes 52
  6.0 35.3 %all-to-all-start = ((bf16[16,2,16,1024]{3,2,1,0:T(8,128)(2,1)}), bf16[16,2,16,1024]{3,2,1,0:T(8,128)(2,1)}, u32[]{:S(2)}, u32[]{:S(2)}) async-start(bf16[16,2,16,1024]{3,2,1,0:T(8,128)(2,1)} %dft_lead.1), calls=%async_computation | async-start | bytes 2097152 | tf_op jit(solution)/shard_map/all_to_all | solution.py:418
  19.7 2.0 %collective-permute-start.1 = (bf16[16,16,1024]{2,1,0:T(8,128)(2,1)S(1)}, bf16[16,16,1024]{2,1,0:T(8,128)(2,1)S(1)}, u32[]{:S(2)}, u32[]{:S(2)}) collective-permute-start(bf16[16,16,1024]{2,1,0:T(8,128)(2,1)S(1)} %get-tuple-element.14), channel_id=1, source_target_pairs={{0,8},{8,0},{1,9},{9,1},{2,10},{10,2},{3,11},{11,3},{4,12},{12,4},... | collective-permute-start | bytes 1572872 | tf_op jit(solution)/shard_map/ppermute | solution.py:377
  41.4 33.0 %all-to-all-start.1 = ((bf16[16,32,1024]{2,1,0:T(8,128)(2,1)}), bf16[16,32,1024]{2,1,0:T(8,128)(2,1)S(1)}, u32[]{:S(2)}, u32[]{:S(2)}) async-start(bf16[16,32,1024]{2,1,0:T(8,128)(2,1)} %constant_dynamic-update-slice_fusion), calls=%async_computation.1 | async-start | bytes 2097152 | tf_op jit(solution)/shard_map/all_to_all | solution.py:419
  51.0 93.4 %copy-start.2 = (bf16[16,1,16,1024]{3,2,1,0:T(8,128)(2,1)}, bf16[16,1,16,1024]{3,2,1,0:T(8,128)(2,1)S(1)}, u32[]{:S(2)}) copy-start(bf16[16,1,16,1024]{3,2,1,0:T(8,128)(2,1)S(1)} %get-tuple-element.27) | copy-start | bytes 1572868
  51.0 2.0 %collective-permute-start = (bf16[256,1024]{1,0:T(8,128)(2,1)S(1)}, bf16[256,1024]{1,0:T(8,128)(2,1)S(1)}, u32[]{:S(2)}, u32[]{:S(2)}) collective-permute-start(bf16[256,1024]{1,0:T(8,128)(2,1)S(1)} %bitcast.28), channel_id=1, source_target_pairs={{0,8},{8,0},{1,9},{9,1},{2,10},{10,2},{3,11},{11,3},{4,12},{12,4},... | collective-permute-start | bytes 1572872 | tf_op jit(solution)/shard_map/ppermute | solution.py:377
  53.0 91.4 %copy-start.4 = (bf16[256,1024]{1,0:T(8,128)(2,1)}, bf16[256,1024]{1,0:T(8,128)(2,1)S(1)}, u32[]{:S(2)}) copy-start(bf16[256,1024]{1,0:T(8,128)(2,1)S(1)} %collective-permute-done.swapped_ref) | copy-start | bytes 1572868
  78.0 4.5 %copy-start.16 = (bf16[2,32,256]{2,1,0:T(8,128)(2,1)S(1)}, bf16[2,32,256]{2,1,0:T(8,128)(2,1)}, u32[]{:S(2)}) copy-start(bf16[2,32,256]{2,1,0:T(8,128)(2,1)} %param.8) | copy-start | bytes 98308
  78.0 92.2 %all-to-all-start.2 = ((bf16[8,2,192,512]{3,2,1,0:T(8,128)(2,1)}), bf16[8,2,192,512]{3,2,1,0:T(8,128)(2,1)}, u32[]{:S(2)}, u32[]{:S(2)}) async-start(bf16[8,2,192,512]{3,2,1,0:T(8,128)(2,1)} %gram_second.1), calls=%async_computation.2 | async-start | bytes 6291456 | tf_op jit(solution)/shard_map/all_to_all | solution.py:426
  82.5 39.4 %collective-permute-start.3 = (bf16[2,32,256]{2,1,0:T(8,128)(2,1)S(1)}, bf16[2,32,256]{2,1,0:T(8,128)(2,1)S(1)}, u32[]{:S(2)}, u32[]{:S(2)}) collective-permute-start(bf16[2,32,256]{2,1,0:T(8,128)(2,1)S(1)} %copy-done.16), channel_id=1, source_target_pairs={{0,128},{1,145},{2,162},{3,179},{4,196},{5,213},{6,230},{7,247},{1... | collective-permute-start | bytes 98312 | tf_op jit(solution)/shard_map/ppermute | solution.py:405
  86.1 35.7 %collective-permute-start.2 = (bf16[2,32,256]{2,1,0:T(8,128)(2,1)S(1)}, bf16[2,32,256]{2,1,0:T(8,128)(2,1)S(1)}, u32[]{:S(2)}, u32[]{:S(2)}) collective-permute-start(bf16[2,32,256]{2,1,0:T(8,128)(2,1)S(1)} %copy-done.16), channel_id=1, source_target_pairs={{0,0},{1,17},{2,34},{3,51},{4,68},{5,85},{6,102},{7,119},{16,16},{... | collective-permute-start | bytes 98312 | tf_op jit(solution)/shard_map/ppermute | solution.py:405
  121.9 1.3 collective-permute-start.4
  123.3 10.3 %collective-permute-start.11 = (bf16[2,2,2,32,256]{4,3,2,1,0:T(8,128)(2,1)S(1)}, bf16[2,2,2,32,256]{4,3,2,1,0:T(8,128)(2,1)S(1)}, u32[]{:S(2)}, u32[]{:S(2)}) collective-permute-start(bf16[2,2,2,32,256]{4,3,2,1,0:T(8,128)(2,1)S(1)} %pad_maximum_fusion.refs_0_), channel_id=1, source_target_pairs={{0,7},{1,6},{2,5},{3,4},{4,3},{5,2},{6,1},{7,0},{8,15},{9,14},{10,... | collective-permute-start | bytes 393224 | tf_op jit(solution)/shard_map/ppermute | solution.py:382
  123.4 13.5 %collective-permute-start.10 = (bf16[2,2,2,32,256]{4,3,2,1,0:T(8,128)(2,1)S(1)}, bf16[2,2,2,32,256]{4,3,2,1,0:T(8,128)(2,1)S(1)}, u32[]{:S(2)}, u32[]{:S(2)}) collective-permute-start(bf16[2,2,2,32,256]{4,3,2,1,0:T(8,128)(2,1)S(1)} %pad_maximum_fusion.refs_0_), channel_id=1, source_target_pairs={{0,6},{1,7},{2,4},{3,5},{4,2},{5,3},{6,0},{7,1},{8,14},{9,15},{10,... | collective-permute-start | bytes 393224 | tf_op jit(solution)/shard_map/ppermute | solution.py:382
  123.5 13.4 %collective-permute-start.9 = (bf16[2,2,2,32,256]{4,3,2,1,0:T(8,128)(2,1)S(1)}, bf16[2,2,2,32,256]{4,3,2,1,0:T(8,128)(2,1)S(1)}, u32[]{:S(2)}, u32[]{:S(2)}) collective-permute-start(bf16[2,2,2,32,256]{4,3,2,1,0:T(8,128)(2,1)S(1)} %pad_maximum_fusion.refs_0_), channel_id=1, source_target_pairs={{0,5},{1,4},{2,7},{3,6},{4,1},{5,0},{6,3},{7,2},{8,13},{9,12},{10,... | collective-permute-start | bytes 393224 | tf_op jit(solution)/shard_map/ppermute | solution.py:382
  123.6 15.6 %collective-permute-start.8 = (bf16[2,2,2,32,256]{4,3,2,1,0:T(8,128)(2,1)S(1)}, bf16[2,2,2,32,256]{4,3,2,1,0:T(8,128)(2,1)S(1)}, u32[]{:S(2)}, u32[]{:S(2)}) collective-permute-start(bf16[2,2,2,32,256]{4,3,2,1,0:T(8,128)(2,1)S(1)} %pad_maximum_fusion.refs_0_), channel_id=1, source_target_pairs={{0,4},{1,5},{2,6},{3,7},{4,0},{5,1},{6,2},{7,3},{8,12},{9,13},{10,... | collective-permute-start | bytes 393224 | tf_op jit(solution)/shard_map/ppermute | solution.py:382
  131.0 8.1 %collective-permute-start.7 = (bf16[2,2,2,32,256]{4,3,2,1,0:T(8,128)(2,1)S(1)}, bf16[2,2,2,32,256]{4,3,2,1,0:T(8,128)(2,1)S(1)}, u32[]{:S(2)}, u32[]{:S(2)}) collective-permute-start(bf16[2,2,2,32,256]{4,3,2,1,0:T(8,128)(2,1)S(1)} %pad_maximum_fusion.refs_0_), channel_id=1, source_target_pairs={{0,3},{1,2},{2,1},{3,0},{4,7},{5,6},{6,5},{7,4},{8,11},{9,10},{10,... | collective-permute-start | bytes 393224 | tf_op jit(solution)/shard_map/ppermute | solution.py:382
  133.6 6.4 %collective-permute-start.6 = (bf16[2,2,2,32,256]{4,3,2,1,0:T(8,128)(2,1)S(1)}, bf16[2,2,2,32,256]{4,3,2,1,0:T(8,128)(2,1)S(1)}, u32[]{:S(2)}, u32[]{:S(2)}) collective-permute-start(bf16[2,2,2,32,256]{4,3,2,1,0:T(8,128)(2,1)S(1)} %pad_maximum_fusion.refs_0_), channel_id=1, source_target_pairs={{0,2},{1,3},{2,0},{3,1},{4,6},{5,7},{6,4},{7,5},{8,10},{9,11},{10,... | collective-permute-start | bytes 393224 | tf_op jit(solution)/shard_map/ppermute | solution.py:382
  136.9 5.0 %collective-permute-start.5 = (bf16[2,2,2,32,256]{4,3,2,1,0:T(8,128)(2,1)S(1)}, bf16[2,2,2,32,256]{4,3,2,1,0:T(8,128)(2,1)S(1)}, u32[]{:S(2)}, u32[]{:S(2)}) collective-permute-start(bf16[2,2,2,32,256]{4,3,2,1,0:T(8,128)(2,1)S(1)} %pad_maximum_fusion.refs_0_), channel_id=1, source_target_pairs={{0,1},{1,0},{2,3},{3,2},{4,5},{5,4},{6,7},{7,6},{8,9},{9,8},{10,11... | collective-permute-start | bytes 393224 | tf_op jit(solution)/shard_map/ppermute | solution.py:382
  144.4 2.8 %copy-start.15 = (s32[1024]{0:T(1024)S(1)}, s32[1024]{0:T(1024)}, u32[]{:S(2)}) copy-start(s32[1024]{0:T(1024)} %constant.36.clone) | copy-start | bytes 12292
  144.4 17.1 %copy-start.1 = (bf16[512,2048]{1,0:T(8,128)(2,1)S(1)}, bf16[512,2048]{1,0:T(8,128)(2,1)}, u32[]{:S(2)}) copy-start(bf16[512,2048]{1,0:T(8,128)(2,1)} %copy-done) | copy-start | bytes 6291460
  147.2 6.6 %collective-permute-start.12 = (bf16[2,64,512]{2,1,0:T(8,128)(2,1)S(1)}, bf16[2,64,512]{2,1,0:T(8,128)(2,1)S(1)}, u32[]{:S(2)}, u32[]{:S(2)}) collective-permute-start(bf16[2,64,512]{2,1,0:T(8,128)(2,1)S(1)} %get-tuple-element.16), channel_id=1, source_target_pairs={{0,1},{1,0},{2,3},{3,2},{4,5},{5,4},{6,7},{7,6},{8,9},{9,8},{10,11... | collective-permute-start | bytes 393224 | tf_op jit(solution)/shard_map/ppermute | solution.py:387
  147.2 9.7 %collective-permute-start.13 = (bf16[2,64,512]{2,1,0:T(8,128)(2,1)S(1)}, bf16[2,64,512]{2,1,0:T(8,128)(2,1)S(1)}, u32[]{:S(2)}, u32[]{:S(2)}) collective-permute-start(bf16[2,64,512]{2,1,0:T(8,128)(2,1)S(1)} %get-tuple-element.17), channel_id=1, source_target_pairs={{0,2},{1,3},{2,0},{3,1},{4,6},{5,7},{6,4},{7,5},{8,10},{9,11},{10,... | collective-permute-start | bytes 393224 | tf_op jit(solution)/shard_map/ppermute | solution.py:387
  147.2 20.5 %collective-permute-start.14 = (bf16[2,64,512]{2,1,0:T(8,128)(2,1)}, bf16[2,64,512]{2,1,0:T(8,128)(2,1)}, u32[]{:S(2)}, u32[]{:S(2)}) collective-permute-start(bf16[2,64,512]{2,1,0:T(8,128)(2,1)} %get-tuple-element.18), channel_id=1, source_target_pairs={{0,3},{1,2},{2,1},{3,0},{4,7},{5,6},{6,5},{7,4},{8,11},{9,10},{10,... | collective-permute-start | bytes 393224 | tf_op jit(solution)/shard_map/ppermute | solution.py:387
  150.8 16.9 %collective-permute-start.15 = (bf16[2,64,512]{2,1,0:T(8,128)(2,1)}, bf16[2,64,512]{2,1,0:T(8,128)(2,1)}, u32[]{:S(2)}, u32[]{:S(2)}) collective-permute-start(bf16[2,64,512]{2,1,0:T(8,128)(2,1)} %get-tuple-element.19), channel_id=1, source_target_pairs={{0,4},{1,5},{2,6},{3,7},{4,0},{5,1},{6,2},{7,3},{8,12},{9,13},{10,... | collective-permute-start | bytes 393224 | tf_op jit(solution)/shard_map/ppermute | solution.py:387
  152.7 15.0 %collective-permute-start.16 = (bf16[2,64,512]{2,1,0:T(8,128)(2,1)}, bf16[2,64,512]{2,1,0:T(8,128)(2,1)}, u32[]{:S(2)}, u32[]{:S(2)}) collective-permute-start(bf16[2,64,512]{2,1,0:T(8,128)(2,1)} %get-tuple-element.20), channel_id=1, source_target_pairs={{0,5},{1,4},{2,7},{3,6},{4,1},{5,0},{6,3},{7,2},{8,13},{9,12},{10,... | collective-permute-start | bytes 393224 | tf_op jit(solution)/shard_map/ppermute | solution.py:387
  153.7 14.0 %collective-permute-start.17 = (bf16[2,64,512]{2,1,0:T(8,128)(2,1)}, bf16[2,64,512]{2,1,0:T(8,128)(2,1)}, u32[]{:S(2)}, u32[]{:S(2)}) collective-permute-start(bf16[2,64,512]{2,1,0:T(8,128)(2,1)} %get-tuple-element.21), channel_id=1, source_target_pairs={{0,6},{1,7},{2,4},{3,5},{4,2},{5,3},{6,0},{7,1},{8,14},{9,15},{10,... | collective-permute-start | bytes 393224 | tf_op jit(solution)/shard_map/ppermute | solution.py:387
  156.9 10.8 %collective-permute-start.18 = (bf16[2,64,512]{2,1,0:T(8,128)(2,1)}, bf16[2,64,512]{2,1,0:T(8,128)(2,1)}, u32[]{:S(2)}, u32[]{:S(2)}) collective-permute-start(bf16[2,64,512]{2,1,0:T(8,128)(2,1)} %get-tuple-element.22), channel_id=1, source_target_pairs={{0,7},{1,6},{2,5},{3,4},{4,3},{5,2},{6,1},{7,0},{8,15},{9,14},{10,... | collective-permute-start | bytes 393224 | tf_op jit(solution)/shard_map/ppermute | solution.py:387
  (7 other events, 8.9 us)

commit v5 on v4

--- a/solution.py
+++ b/solution.py
@@ -21,7 +21,7 @@
 SIDE_A, SIDE_B = CHIPS * FIRST, CHIPS * SECOND
 OWN_A, OWN_B = SIDE_A // N_TM, SIDE_B // N_TM
 COLS_A, COLS_B = 2 * SIDE_A, 2 * SIDE_B
-PIECES = COLS_A // COLS_B
+ROWS_B = 2 * OWN_B
 HALF = 512
 BF16 = jnp.bfloat16
 F32 = jnp.float32
@@ -202,46 +202,68 @@
     )(place, kept, swapped)
 
 
-def gram_second_kernel(mine_ref, kept_ref, swapped_ref, out_hbm, out_ref, sems):
+def gram_late_kernel(mine_ref, *refs):
+    col_refs, (out_hbm, out_ref, sems) = refs[:-3], refs[-3:]
     mine = mine_ref[...]
-    sides = [product(mine, kept_ref[...]), product(mine, swapped_ref[...])]
-    second = product(mine, mine)
+    sides = [product(mine, ref[...]) for ref in (col_refs or (mine_ref,))]
     copies = []
     for q in (0, 1):
-        first = jnp.concatenate([sides[0][q], sides[1][q]], 1)
-        flipped = first.T
-        flipped = (-flipped if q else flipped).astype(BF16)
-        blocks = [first[:, COLS_B * j : COLS_B * j + COLS_B].astype(BF16) for j in range(PIECES)]
-        blocks.append(second[q].astype(BF16))
-        rows = 2 * OWN_B
-        for r in range(N_TM):
-            for j in range(PIECES + 1):
-                out_ref[r, q, rows * j : rows * j + rows, :] = blocks[j][rows * r : rows * r + rows]
-            for a in (0, 1):
-                row = (PIECES + 1) * rows + OWN_A * a
-                src = SIDE_A * a + OWN_A * r
-                out_ref[r, q, row : row + OWN_A, :] = flipped[src : src + OWN_A]
+        start = 0
+        for side in sides:
+            value = side[q].astype(BF16)
+            width = value.shape[1]
+            for r in range(N_TM):
+                out_ref[r, q, :, start : start + width] = value[ROWS_B * r : ROWS_B * r + ROWS_B]
+            start += width
         copies.append(pltpu.make_async_copy(out_ref.at[:, q], out_hbm.at[:, q], sems.at[q]))
         copies[q].start()
     for copy in copies:
         copy.wait()
 
 
-def gram_second(mine, kept, swapped):
-    rows = 2 * (PIECES + 1) * OWN_B + 2 * OWN_A
-    return pl.pallas_call(
-        gram_second_kernel,
-        in_specs=[VMEM, VMEM, VMEM],
+def gram_late(mine, *others):
+    width = COLS_A if others else COLS_B
+    shape = (N_TM, 2, ROWS_B, width)
+    return pl.pallas_call(
+        gram_late_kernel,
+        in_specs=[VMEM] * (1 + len(others)),
         out_specs=HBM,
-        out_shape=pltpu.HBM((N_TM, 2, rows, COLS_B), BF16),
-        scratch_shapes=[
-            pltpu.VMEM((N_TM, 2, rows, COLS_B), BF16),
-            pltpu.SemaphoreType.DMA((2,)),
-        ],
-        compiler_params=params(14),
-        cost_estimate=cost(1 << 29, 6 << 20),
-        name="gram_second",
-    )(mine, kept, swapped)
+        out_shape=pltpu.HBM(shape, BF16),
+        scratch_shapes=[pltpu.VMEM(shape, BF16), pltpu.SemaphoreType.DMA((2,))],
+        compiler_params=params(10),
+        cost_estimate=cost(1 << 29, 4 << 20),
+        name="gram_cross" if others else "gram_second",
+    )(mine, *others)
+
+
+def mirror_kernel(place_ref, terms_ref, sums_ref, *refs):
+    mirror_refs, flip = refs[:N_TM], refs[N_TM]
+    own = place_ref[1]
+    for q in (0, 1):
+        total = terms_ref[0, q].astype(F32)
+        for t in range(1, N_TM):
+            total = total + terms_ref[t, q].astype(F32)
+        sums_ref[q] = total
+        block = jnp.concatenate([-total if q else total, jnp.zeros((128 - ROWS_B, COLS_A), F32)], 0)
+        flip[q] = block.T
+        for k in range(N_TM):
+            for a in (0, 1):
+                row = pl.multiple_of(SIDE_A * a + (own ^ k) * OWN_A, OWN_A)
+                mirror_refs[k][q, OWN_A * a : OWN_A * a + OWN_A] = flip[q, pl.ds(row, OWN_A), :].astype(BF16)
+
+
+def mirror(place, terms):
+    return pl.pallas_call(
+        mirror_kernel,
+        in_specs=[SMEM, VMEM],
+        out_specs=(VMEM,) * (N_TM + 1),
+        out_shape=(jax.ShapeDtypeStruct((2, ROWS_B, COLS_A), F32),)
+        + (jax.ShapeDtypeStruct((2, 2 * OWN_A, 128), BF16),) * N_TM,
+        scratch_shapes=[pltpu.VMEM((2, COLS_A, 128), F32)],
+        compiler_params=params(8),
+        cost_estimate=cost(1 << 27, 1 << 21),
+        name="mirror",
+    )(place, terms)
 
 
 def placed(values, table):
@@ -279,27 +301,53 @@
     )(*terms, order)
 
 
+def cross_kernel(place_ref, base_ref, sums_ref, order_ref, *refs):
+    mirrors, out_ref = refs[:N_TM], refs[-1]
+    core, own = place_ref[0], place_ref[1]
+    spread = placed([sums_ref[0], sums_ref[1]], order_ref[:COLS_A, :])
+    item = lax.broadcasted_iota(jnp.int32, (128, 128), 0)
+    lane = lax.broadcasted_iota(jnp.int32, (128, 128), 1)
+    chip, rel = item // (2 * SECOND), item // SECOND % 2
+    target = 64 * chip + 32 * (rel ^ core) + FIRST + item % SECOND
+    narrow = jnp.where((target == lane) & (item < ROWS_B), 1.0, 0.0).astype(BF16)
+    for q in (0, 1):
+        out_ref[q, : 2 * OWN_A, :] = base_ref[q]
+        out_ref[q, 2 * OWN_A :, :] = spread[q]
+        for k in range(N_TM):
+            col = pl.multiple_of((own ^ k) * 128, 128)
+            out_ref[q, : 2 * OWN_A, pl.ds(col, 128)] += dot_nn(mirrors[k][q], narrow)
+
+
+def spread_cross(place, base, sums, order, mirrors):
+    return pl.pallas_call(
+        cross_kernel,
+        in_specs=[SMEM] + [VMEM] * (N_TM + 3),
+        out_specs=VMEM,
+        out_shape=jax.ShapeDtypeStruct((2, 128, 1024), F32),
+        compiler_params=params(8),
+        cost_estimate=cost(1 << 28, 1 << 22),
+        name="spread_cross",
+    )(place, base, sums, order, *mirrors)
+
+
 def finish_kernel(place_ref, terms_ref, base_ref, order_ref, out_ref):
     core = place_ref[0]
-    rows = 2 * OWN_B
-    last, extra = [], []
+    totals = []
     for q in (0, 1):
         total = terms_ref[0, q].astype(F32)
         for t in range(1, N_TM):
             total = total + terms_ref[t, q].astype(F32)
-        last.append(jnp.concatenate([total[rows * j : rows * j + rows] for j in range(PIECES + 1)], 1))
-        extra.append(total[(PIECES + 1) * rows :])
-    lower = placed(last, order_ref[...])
-    upper = placed(extra, order_ref[COLS_A:, :])
-    for q in (0, 1):
-        top = base_ref[q] + upper[q]
+        totals.append(total)
+    lower = placed(totals, order_ref[COLS_A:, :])
+    for q in (0, 1):
+        low = base_ref[q, 2 * OWN_A :, :] + lower[q]
         for rel in (0, 1):
             for chip in (0, 1):
                 row = pl.multiple_of(64 * chip + 32 * (rel ^ core), 8)
                 src = OWN_A * rel + FIRST * chip
-                out_ref[q, pl.ds(row, FIRST), :] = top[src : src + FIRST]
+                out_ref[q, pl.ds(row, FIRST), :] = base_ref[q, src : src + FIRST, :]
                 src = 2 * SECOND * chip + SECOND * rel
-                out_ref[q, pl.ds(pl.multiple_of(row + FIRST, 8), SECOND), :] = lower[q][src : src + SECOND]
+                out_ref[q, pl.ds(pl.multiple_of(row + FIRST, 8), SECOND), :] = low[src : src + SECOND]
 
 
 def finish(place, terms, base, order):
@@ -422,14 +470,19 @@
     swapped = swap(other, "stat_2")
     terms = gram_first(place, kept, swapped)
     terms = to_partners(terms)
-    blocks = gram_second(second, kept, swapped)
-    last = lax.all_to_all(blocks, TM, 0, 0, tiled=True)
+    cross = gram_late(second, kept, swapped)
+    cross = lax.all_to_all(cross, TM, 0, 0, tiled=True)
+    late = gram_late(second)
+    late = lax.all_to_all(late, TM, 0, 0, tiled=True)
 
     weights = weight_stack(place, blocks_k)
     beams = beam_sum(kept, swapped, second, weights)
     beams = beams.reshape(NF // 32, SPECTRA, 2, 256)
     base = spread_first(terms, order)
-    rows = finish(place, last, base, order)
+    sums, *mirrors = mirror(place, cross)
+    mirrors = to_partners(mirrors)
+    base = spread_cross(place, base, sums, order, mirrors)
+    rows = finish(place, late, base, order)
     return beams, rows.transpose(1, 0, 2)[:, None]
 
 

time: 177 us -> 183 us (1.034)
  starting transfers between devices: 48.5 us -> 68.3 us
  waiting for transfers between devices: 91.4 us -> 75 us
  Pallas kernels: 21.3 us -> 23.3 us
    ppermute x2, waiting for transfers between devices: 35.1 us -> 11.8 us  [step(): lax.ppermute(beam_weights, (*CHIP, *TM), ring)]
    ppermute x7 -> x14, starting transfers between devices: 12.7 us -> 26.3 us  [to_partners(): lax.ppermute(arrays[k], TM, pairs(k))]
    ppermute x7 -> x14, waiting for transfers between devices: 1.18 us -> 8.57 us  [to_partners(): lax.ppermute(arrays[k], TM, pairs(k))]
    all_to_all x1 -> x2, starting transfers between devices: 4.5 us -> 8.76 us  [the longest x1 4.52 us: step(): cross = lax.all_to_all(cross, TM, 0, 0, tiled=True)]
    pallas_call x1 -> x4, Pallas kernels: 3.65 us -> 7.19 us  [the longest x2 4.42 us: gram_late(): pl.pallas_call(gram_late_kernel, in_specs=[VMEM] * (1 + len(others)), out...]
    ppermute x7, starting transfers between devices: 7.74 us -> 9.7 us  [with_partners(): return [array] + [lax.ppermute(array, TM, pairs(k)) for k in range(1, N_TM)]]
    unnamed x36 -> x64, local copies, waits for them, and re-layouts: 8.78 us -> 9.97 us
  transfers between devices with their start and end apart: 22 -> 30, of which waited for: 12 -> 12; matrix products, arithmetic and copies ran while one was open for 3% -> 2% of each run, Pallas kernels for 6% -> 8%
where the time goes in v5:
time: 183 us; the launch traced here: 182 us
  waiting for transfers between devices  75 us (41%)
  starting transfers between devices  68.3 us (37%)
  Pallas kernels  23.3 us (13%)
  local copies, waits for them, and re-layouts  13 us (7%)
    ppermute x14, starting transfers between devices, to_partners(): lax.ppermute(arrays[k], TM, pairs(k))  26.3 us
    all_to_all x1, waiting for transfers between devices, step(): lax.all_to_all(ready_b, CHIP, 0, 0, tiled=True).reshape(COLS_B, 1024)  21.3 us
    all_to_all x1, waiting for transfers between devices, step(): arrived = lax.all_to_all(ready_a, CHIP, 0, 0, tiled=True)  18.8 us
    ppermute x2, waiting for transfers between devices, step(): lax.ppermute(beam_weights, (*CHIP, *TM), ring)  11.8 us
    all_to_all x1, starting transfers between devices, step(): arrived = lax.all_to_all(ready_a, CHIP, 0, 0, tiled=True)  10.6 us
    ppermute x7, waiting for transfers between devices, with_partners(): return [array] + [lax.ppermute(array, TM, pairs(k)) for k in range(1, N_TM)]  10.4 us
    unnamed x64, local copies, waits for them, and re-layouts  9.97 us
    ppermute x7, starting transfers between devices, with_partners(): return [array] + [lax.ppermute(array, TM, pairs(k)) for k in range(1, N_TM)]  9.7 us
  transfers between devices with their start and end apart: 30, of which 12 were waited for; matrix products, arithmetic and copies ran while one was open for 2% of the time, Pallas kernels for 8%

profile of v5, /device:TPU:64, one launch (start us, length us, event | category | flops | bytes accessed | tf_op | source)
XLA Modules:
  0.0 181.7 jit_solution(13383124723913853607)
XLA Ops:
  1.2 4.7 %dft_lead.1 = bf16[16,2,16,1024]{3,2,1,0:T(8,128)(2,1)} custom-call(s32[4]{0:T(128)} %pad_add_fusion.place_ref, bf16[2,32,128,128]{3,2,1,0:T(8,128)(2,1)} %bitcast.27, bf16[256,256]{1,0:T(8,128)(2,1)} %constant.33.clone.left_hbm, f32[2,128,128]{2,1,0:T(8,128)} %constant.34.clone.turn_hbm, bf16[256,256]{1,0:T(8,128)(2,1)} %constant.35.clone.right_hbm), custom_call_target="tpu_custom_call" | custom-call | flops 1073741824 | bytes 2097152 | tf_op jit(solution)/shard_map/dft_lead/pallas_call | solution.py:148
  5.9 10.6 %all-to-all-start = ((bf16[16,2,16,1024]{3,2,1,0:T(8,128)(2,1)}), bf16[16,2,16,1024]{3,2,1,0:T(8,128)(2,1)}, u32[]{:S(2)}, u32[]{:S(2)}) async-start(bf16[16,2,16,1024]{3,2,1,0:T(8,128)(2,1)} %dft_lead.1), calls=%async_computation | async-start | bytes 2097152 | tf_op jit(solution)/shard_map/all_to_all | solution.py:466
  16.6 3.0 %dft_rest.1 = (bf16[16,16,1024]{2,1,0:T(8,128)(2,1)S(1)}, bf16[16,16,1024]{2,1,0:T(8,128)(2,1)S(1)}) custom-call(s32[4]{0:T(128)S(1)} %copy-done.18, bf16[2,32,128,128]{3,2,1,0:T(8,128)(2,1)S(1)} %bitcast.28, bf16[256,256]{1,0:T(8,128)(2,1)S(1)} %copy-done.27, f32[2,128,128]{2,1,0:T(8,128)S(1)} %copy-done.26, bf16[256,256]{1,0:T(8,128)(2,1)S(1)} %copy-done.25), custom_call_target="tpu_custom_call" | custom-call | flops 1073741824 | bytes 2097152 | tf_op jit(solution)/shard_map/dft_rest/pallas_call | solution.py:148
  22.4 18.8 %all-to-all-done = bf16[16,2,16,1024]{3,2,1,0:T(8,128)(2,1)} async-done(((bf16[16,2,16,1024]{3,2,1,0:T(8,128)(2,1)}), bf16[16,2,16,1024]{3,2,1,0:T(8,128)(2,1)}, u32[]{:S(2)}, u32[]{:S(2)}) %all-to-all-start) | async-done | bytes 1048608 | tf_op jit(solution)/shard_map/all_to_all | solution.py:466
  41.3 8.4 %all-to-all-start.1 = ((bf16[16,32,1024]{2,1,0:T(8,128)(2,1)}), bf16[16,32,1024]{2,1,0:T(8,128)(2,1)S(1)}, u32[]{:S(2)}, u32[]{:S(2)}) async-start(bf16[16,32,1024]{2,1,0:T(8,128)(2,1)} %constant_dynamic-update-slice_fusion), calls=%async_computation.1 | async-start | bytes 2097152 | tf_op jit(solution)/shard_map/all_to_all | solution.py:467
  51.0 1.9 %collective-permute-done.swapped_ref.refs_1_ = bf16[256,1024]{1,0:T(8,128)(2,1)S(1)} collective-permute-done((bf16[256,1024]{1,0:T(8,128)(2,1)S(1)}, bf16[256,1024]{1,0:T(8,128)(2,1)S(1)}, u32[]{:S(2)}, u32[]{:S(2)}) %collective-permute-start) | collective-permute-done | bytes 524320 | tf_op jit(solution)/shard_map/ppermute | solution.py:425
  52.9 21.3 %all-to-all-done.1 = bf16[16,32,1024]{2,1,0:T(8,128)(2,1)S(1)} async-done(((bf16[16,32,1024]{2,1,0:T(8,128)(2,1)}), bf16[16,32,1024]{2,1,0:T(8,128)(2,1)S(1)}, u32[]{:S(2)}, u32[]{:S(2)}) %all-to-all-start.1) | async-done | bytes 1048608 | tf_op jit(solution)/shard_map/all_to_all | solution.py:467
  74.2 2.3 %gram_cross.1 = bf16[8,2,64,512]{3,2,1,0:T(8,128)(2,1)} custom-call(bf16[512,1024]{1,0:T(8,128)(2,1)S(1)} %bitcast.20, bf16[256,1024]{1,0:T(8,128)(2,1)S(1)} %bitcast.24, bf16[256,1024]{1,0:T(8,128)(2,1)S(1)} %collective-permute-done.swapped_ref.refs_1_), custom_call_target="tpu_custom_call" | custom-call | flops 1073741824 | bytes 4194304 | tf_op jit(solution)/shard_map/gram_cross/pallas_call | solution.py:227
  76.5 4.5 %all-to-all-start.3 = ((bf16[8,2,64,512]{3,2,1,0:T(8,128)(2,1)}), bf16[8,2,64,512]{3,2,1,0:T(8,128)(2,1)S(1)}, u32[]{:S(2)}, u32[]{:S(2)}) async-start(bf16[8,2,64,512]{3,2,1,0:T(8,128)(2,1)} %gram_cross.1), calls=%async_computation.3 | async-start | bytes 2097152 | tf_op jit(solution)/shard_map/all_to_all | solution.py:474
  81.1 3.6 %collective-permute-start.3 = (bf16[2,32,256]{2,1,0:T(8,128)(2,1)S(1)}, bf16[2,32,256]{2,1,0:T(8,128)(2,1)S(1)}, u32[]{:S(2)}, u32[]{:S(2)}) collective-permute-start(bf16[2,32,256]{2,1,0:T(8,128)(2,1)S(1)} %copy-done.30), channel_id=1, source_target_pairs={{0,128},{1,145},{2,162},{3,179},{4,196},{5,213},{6,230},{7,247},{1... | collective-permute-start | bytes 98312 | tf_op jit(solution)/shard_map/ppermute | solution.py:453
  85.3 11.8 %collective-permute-done.3 = bf16[2,32,256]{2,1,0:T(8,128)(2,1)S(1)} collective-permute-done((bf16[2,32,256]{2,1,0:T(8,128)(2,1)S(1)}, bf16[2,32,256]{2,1,0:T(8,128)(2,1)S(1)}, u32[]{:S(2)}, u32[]{:S(2)}) %collective-permute-start.3) | collective-permute-done | bytes 32800 | tf_op jit(solution)/shard_map/ppermute | solution.py:453
  98.7 7.5 %collective-permute-start.9 = (bf16[2,2,2,32,256]{4,3,2,1,0:T(8,128)(2,1)S(1)}, bf16[2,2,2,32,256]{4,3,2,1,0:T(8,128)(2,1)S(1)}, u32[]{:S(2)}, u32[]{:S(2)}) collective-permute-start(bf16[2,2,2,32,256]{4,3,2,1,0:T(8,128)(2,1)S(1)} %pad_maximum_fusion.refs_0_), channel_id=1, source_target_pairs={{0,5},{1,4},{2,7},{3,6},{4,1},{5,0},{6,3},{7,2},{8,13},{9,12},{10,... | collective-permute-start | bytes 393224 | tf_op jit(solution)/shard_map/ppermute | solution.py:430
  106.3 1.5 collective-permute-start.7
  108.2 3.0 %collective-permute-done.10.refs_6_ = bf16[2,2,2,32,256]{4,3,2,1,0:T(8,128)(2,1)S(1)} collective-permute-done((bf16[2,2,2,32,256]{4,3,2,1,0:T(8,128)(2,1)S(1)}, bf16[2,2,2,32,256]{4,3,2,1,0:T(8,128)(2,1)S(1)}, u32[]{:S(2)}, u32[]{:S(2)}) %collective-permute-start.10) | collective-permute-done | bytes 131104 | tf_op jit(solution)/shard_map/ppermute | solution.py:430
  111.2 4.0 %collective-permute-done.8.refs_4_ = bf16[2,2,2,32,256]{4,3,2,1,0:T(8,128)(2,1)S(1)} collective-permute-done((bf16[2,2,2,32,256]{4,3,2,1,0:T(8,128)(2,1)S(1)}, bf16[2,2,2,32,256]{4,3,2,1,0:T(8,128)(2,1)S(1)}, u32[]{:S(2)}, u32[]{:S(2)}) %collective-permute-start.8) | collective-permute-done | bytes 131104 | tf_op jit(solution)/shard_map/ppermute | solution.py:430
  115.2 3.4 %collective-permute-done.6.refs_2_ = bf16[2,2,2,32,256]{4,3,2,1,0:T(8,128)(2,1)S(1)} collective-permute-done((bf16[2,2,2,32,256]{4,3,2,1,0:T(8,128)(2,1)S(1)}, bf16[2,2,2,32,256]{4,3,2,1,0:T(8,128)(2,1)S(1)}, u32[]{:S(2)}, u32[]{:S(2)}) %collective-permute-start.6) | collective-permute-done | bytes 131104 | tf_op jit(solution)/shard_map/ppermute | solution.py:430
  121.1 2.1 %gram_second.1 = bf16[8,2,64,512]{3,2,1,0:T(8,128)(2,1)} custom-call(bf16[512,1024]{1,0:T(8,128)(2,1)S(1)} %bitcast.21), custom_call_target="tpu_custom_call" | custom-call | flops 1073741824 | bytes 4194304 | tf_op jit(solution)/shard_map/gram_second/pallas_call | solution.py:227
  123.3 4.2 %all-to-all-start.2 = ((bf16[8,2,64,512]{3,2,1,0:T(8,128)(2,1)}), bf16[8,2,64,512]{3,2,1,0:T(8,128)(2,1)}, u32[]{:S(2)}, u32[]{:S(2)}) async-start(bf16[8,2,64,512]{3,2,1,0:T(8,128)(2,1)} %gram_second.1), calls=%async_computation.2 | async-start | bytes 2097152 | tf_op jit(solution)/shard_map/all_to_all | solution.py:476
  127.6 2.6 %gram_first.1 = (bf16[2,64,512]{2,1,0:T(8,128)(2,1)S(1)}, bf16[2,64,512]{2,1,0:T(8,128)(2,1)S(1)}, bf16[2,64,512]{2,1,0:T(8,128)(2,1)S(1)}, bf16[2,64,512]{2,1,0...) custom-call(s32[4]{0:T(128)S(1)} %copy-done.18, ...), custom_call_target="tpu_custom_call" | custom-call | flops 2147483648 | bytes 6291456 | tf_op jit(solution)/shard_map/gram_first/pallas_call | solution.py:193
  130.2 1.9 %collective-permute-start.12 = (bf16[2,64,512]{2,1,0:T(8,128)(2,1)S(1)}, bf16[2,64,512]{2,1,0:T(8,128)(2,1)S(1)}, u32[]{:S(2)}, u32[]{:S(2)}) collective-permute-start(bf16[2,64,512]{2,1,0:T(8,128)(2,1)S(1)} %get-tuple-element.25), channel_id=1, source_target_pairs={{0,1},{1,0},{2,3},{3,2},{4,5},{5,4},{6,7},{7,6},{8,9},{9,8},{10,11... | collective-permute-start | bytes 393224 | tf_op jit(solution)/shard_map/ppermute | solution.py:435
  132.1 1.5 collective-permute-start.13
  133.8 3.4 %collective-permute-start.15 = (bf16[2,64,512]{2,1,0:T(8,128)(2,1)S(1)}, bf16[2,64,512]{2,1,0:T(8,128)(2,1)S(1)}, u32[]{:S(2)}, u32[]{:S(2)}) collective-permute-start(bf16[2,64,512]{2,1,0:T(8,128)(2,1)S(1)} %get-tuple-element.28), channel_id=1, source_target_pairs={{0,4},{1,5},{2,6},{3,7},{4,0},{5,1},{6,2},{7,3},{8,12},{9,13},{10,... | collective-permute-start | bytes 393224 | tf_op jit(solution)/shard_map/ppermute | solution.py:435
  138.6 6.6 %collective-permute-done.12.refs_1_ = bf16[2,64,512]{2,1,0:T(8,128)(2,1)S(1)} collective-permute-done((bf16[2,64,512]{2,1,0:T(8,128)(2,1)S(1)}, bf16[2,64,512]{2,1,0:T(8,128)(2,1)S(1)}, u32[]{:S(2)}, u32[]{:S(2)}) %collective-permute-start.12) | collective-permute-done | bytes 131104 | tf_op jit(solution)/shard_map/ppermute | solution.py:435
  145.9 2.8 %collective-permute-start.17 = (bf16[2,64,512]{2,1,0:T(8,128)(2,1)}, bf16[2,64,512]{2,1,0:T(8,128)(2,1)}, u32[]{:S(2)}, u32[]{:S(2)}) collective-permute-start(bf16[2,64,512]{2,1,0:T(8,128)(2,1)} %get-tuple-element.30), channel_id=1, source_target_pairs={{0,6},{1,7},{2,4},{3,5},{4,2},{5,3},{6,0},{7,1},{8,14},{9,15},{10,... | collective-permute-start | bytes 393224 | tf_op jit(solution)/shard_map/ppermute | solution.py:435
  150.5 3.9 %collective-permute-start.18 = (bf16[2,64,512]{2,1,0:T(8,128)(2,1)}, bf16[2,64,512]{2,1,0:T(8,128)(2,1)}, u32[]{:S(2)}, u32[]{:S(2)}) collective-permute-start(bf16[2,64,512]{2,1,0:T(8,128)(2,1)} %get-tuple-element.31), channel_id=1, source_target_pairs={{0,7},{1,6},{2,5},{3,4},{4,3},{5,2},{6,1},{7,0},{8,15},{9,14},{10,... | collective-permute-start | bytes 393224 | tf_op jit(solution)/shard_map/ppermute | solution.py:435
  158.8 1.5 collective-permute-start.20
  164.7 2.1 %collective-permute-start.21 = (bf16[2,64,128]{2,1,0:T(8,128)(2,1)}, bf16[2,64,128]{2,1,0:T(8,128)(2,1)S(1)}, u32[]{:S(2)}, u32[]{:S(2)}) collective-permute-start(bf16[2,64,128]{2,1,0:T(8,128)(2,1)} %copy-done.24), channel_id=1, source_target_pairs={{0,3},{1,2},{2,1},{3,0},{4,7},{5,6},{6,5},{7,4},{8,11},{9,10},{10,... | collective-permute-start | bytes 98312 | tf_op jit(solution)/shard_map/ppermute | solution.py:435
  167.4 2.3 %collective-permute-start.23 = (bf16[2,64,128]{2,1,0:T(8,128)(2,1)}, bf16[2,64,128]{2,1,0:T(8,128)(2,1)S(1)}, u32[]{:S(2)}, u32[]{:S(2)}) collective-permute-start(bf16[2,64,128]{2,1,0:T(8,128)(2,1)} %copy-done.22), channel_id=1, source_target_pairs={{0,5},{1,4},{2,7},{3,6},{4,1},{5,0},{6,3},{7,2},{8,13},{9,12},{10,... | collective-permute-start | bytes 98312 | tf_op jit(solution)/shard_map/ppermute | solution.py:435
  170.5 3.9 %collective-permute-start.25 = (bf16[2,64,128]{2,1,0:T(8,128)(2,1)}, bf16[2,64,128]{2,1,0:T(8,128)(2,1)S(1)}, u32[]{:S(2)}, u32[]{:S(2)}) collective-permute-start(bf16[2,64,128]{2,1,0:T(8,128)(2,1)} %copy-done.20), channel_id=1, source_target_pairs={{0,7},{1,6},{2,5},{3,4},{4,3},{5,2},{6,1},{7,0},{8,15},{9,14},{10,... | collective-permute-start | bytes 98312 | tf_op jit(solution)/shard_map/ppermute | solution.py:435
  174.4 1.5 spread_first.1.base_ref
  178.1 1.8 finish.1
  179.9 1.8 copy.10
  (111 shorter events, 26.6 us)
Async XLA Ops:
  5.9 35.3 %all-to-all-start = ((bf16[16,2,16,1024]{3,2,1,0:T(8,128)(2,1)}), bf16[16,2,16,1024]{3,2,1,0:T(8,128)(2,1)}, u32[]{:S(2)}, u32[]{:S(2)}) async-start(bf16[16,2,16,1024]{3,2,1,0:T(8,128)(2,1)} %dft_lead.1), calls=%async_computation | async-start | bytes 2097152 | tf_op jit(solution)/shard_map/all_to_all | solution.py:466
  19.6 2.0 %collective-permute-start.1 = (bf16[16,16,1024]{2,1,0:T(8,128)(2,1)S(1)}, bf16[16,16,1024]{2,1,0:T(8,128)(2,1)S(1)}, u32[]{:S(2)}, u32[]{:S(2)}) collective-permute-start(bf16[16,16,1024]{2,1,0:T(8,128)(2,1)S(1)} %get-tuple-element.23), channel_id=1, source_target_pairs={{0,8},{8,0},{1,9},{9,1},{2,10},{10,2},{3,11},{11,3},{4,12},{12,4},... | collective-permute-start | bytes 1572872 | tf_op jit(solution)/shard_map/ppermute | solution.py:425
  41.3 33.0 %all-to-all-start.1 = ((bf16[16,32,1024]{2,1,0:T(8,128)(2,1)}), bf16[16,32,1024]{2,1,0:T(8,128)(2,1)S(1)}, u32[]{:S(2)}, u32[]{:S(2)}) async-start(bf16[16,32,1024]{2,1,0:T(8,128)(2,1)} %constant_dynamic-update-slice_fusion), calls=%async_computation.1 | async-start | bytes 2097152 | tf_op jit(solution)/shard_map/all_to_all | solution.py:467
  50.9 76.6 %copy-start.4 = (bf16[16,1,16,1024]{3,2,1,0:T(8,128)(2,1)}, bf16[16,1,16,1024]{3,2,1,0:T(8,128)(2,1)S(1)}, u32[]{:S(2)}) copy-start(bf16[16,1,16,1024]{3,2,1,0:T(8,128)(2,1)S(1)} %get-tuple-element.45) | copy-start | bytes 1572868
  50.9 2.0 %collective-permute-start = (bf16[256,1024]{1,0:T(8,128)(2,1)S(1)}, bf16[256,1024]{1,0:T(8,128)(2,1)S(1)}, u32[]{:S(2)}, u32[]{:S(2)}) collective-permute-start(bf16[256,1024]{1,0:T(8,128)(2,1)S(1)} %bitcast.29), channel_id=1, source_target_pairs={{0,8},{8,0},{1,9},{9,1},{2,10},{10,2},{3,11},{11,3},{4,12},{12,4},... | collective-permute-start | bytes 1572872 | tf_op jit(solution)/shard_map/ppermute | solution.py:425
  52.9 74.6 %copy-start.6 = (bf16[256,1024]{1,0:T(8,128)(2,1)}, bf16[256,1024]{1,0:T(8,128)(2,1)S(1)}, u32[]{:S(2)}) copy-start(bf16[256,1024]{1,0:T(8,128)(2,1)S(1)} %collective-permute-done.swapped_ref.refs_1_) | copy-start | bytes 1572868
  76.5 46.7 %all-to-all-start.3 = ((bf16[8,2,64,512]{3,2,1,0:T(8,128)(2,1)}), bf16[8,2,64,512]{3,2,1,0:T(8,128)(2,1)S(1)}, u32[]{:S(2)}, u32[]{:S(2)}) async-start(bf16[8,2,64,512]{3,2,1,0:T(8,128)(2,1)} %gram_cross.1), calls=%async_computation.3 | async-start | bytes 2097152 | tf_op jit(solution)/shard_map/all_to_all | solution.py:474
  81.1 16.1 %collective-permute-start.3 = (bf16[2,32,256]{2,1,0:T(8,128)(2,1)S(1)}, bf16[2,32,256]{2,1,0:T(8,128)(2,1)S(1)}, u32[]{:S(2)}, u32[]{:S(2)}) collective-permute-start(bf16[2,32,256]{2,1,0:T(8,128)(2,1)S(1)} %copy-done.30), channel_id=1, source_target_pairs={{0,128},{1,145},{2,162},{3,179},{4,196},{5,213},{6,230},{7,247},{1... | collective-permute-start | bytes 98312 | tf_op jit(solution)/shard_map/ppermute | solution.py:453
  84.7 12.5 %collective-permute-start.2 = (bf16[2,32,256]{2,1,0:T(8,128)(2,1)S(1)}, bf16[2,32,256]{2,1,0:T(8,128)(2,1)S(1)}, u32[]{:S(2)}, u32[]{:S(2)}) collective-permute-start(bf16[2,32,256]{2,1,0:T(8,128)(2,1)S(1)} %copy-done.30), channel_id=1, source_target_pairs={{0,0},{1,17},{2,34},{3,51},{4,68},{5,85},{6,102},{7,119},{16,16},{... | collective-permute-start | bytes 98312 | tf_op jit(solution)/shard_map/ppermute | solution.py:453
  97.2 1.3 collective-permute-start.4
  98.5 9.2 %collective-permute-start.11 = (bf16[2,2,2,32,256]{4,3,2,1,0:T(8,128)(2,1)S(1)}, bf16[2,2,2,32,256]{4,3,2,1,0:T(8,128)(2,1)S(1)}, u32[]{:S(2)}, u32[]{:S(2)}) collective-permute-start(bf16[2,2,2,32,256]{4,3,2,1,0:T(8,128)(2,1)S(1)} %pad_maximum_fusion.refs_0_), channel_id=1, source_target_pairs={{0,7},{1,6},{2,5},{3,4},{4,3},{5,2},{6,1},{7,0},{8,15},{9,14},{10,... | collective-permute-start | bytes 393224 | tf_op jit(solution)/shard_map/ppermute | solution.py:430
  98.6 12.6 %collective-permute-start.10 = (bf16[2,2,2,32,256]{4,3,2,1,0:T(8,128)(2,1)S(1)}, bf16[2,2,2,32,256]{4,3,2,1,0:T(8,128)(2,1)S(1)}, u32[]{:S(2)}, u32[]{:S(2)}) collective-permute-start(bf16[2,2,2,32,256]{4,3,2,1,0:T(8,128)(2,1)S(1)} %pad_maximum_fusion.refs_0_), channel_id=1, source_target_pairs={{0,6},{1,7},{2,4},{3,5},{4,2},{5,3},{6,0},{7,1},{8,14},{9,15},{10,... | collective-permute-start | bytes 393224 | tf_op jit(solution)/shard_map/ppermute | solution.py:430
  98.7 12.5 %collective-permute-start.9 = (bf16[2,2,2,32,256]{4,3,2,1,0:T(8,128)(2,1)S(1)}, bf16[2,2,2,32,256]{4,3,2,1,0:T(8,128)(2,1)S(1)}, u32[]{:S(2)}, u32[]{:S(2)}) collective-permute-start(bf16[2,2,2,32,256]{4,3,2,1,0:T(8,128)(2,1)S(1)} %pad_maximum_fusion.refs_0_), channel_id=1, source_target_pairs={{0,5},{1,4},{2,7},{3,6},{4,1},{5,0},{6,3},{7,2},{8,13},{9,12},{10,... | collective-permute-start | bytes 393224 | tf_op jit(solution)/shard_map/ppermute | solution.py:430
  106.2 9.0 %collective-permute-start.8 = (bf16[2,2,2,32,256]{4,3,2,1,0:T(8,128)(2,1)S(1)}, bf16[2,2,2,32,256]{4,3,2,1,0:T(8,128)(2,1)S(1)}, u32[]{:S(2)}, u32[]{:S(2)}) collective-permute-start(bf16[2,2,2,32,256]{4,3,2,1,0:T(8,128)(2,1)S(1)} %pad_maximum_fusion.refs_0_), channel_id=1, source_target_pairs={{0,4},{1,5},{2,6},{3,7},{4,0},{5,1},{6,2},{7,3},{8,12},{9,13},{10,... | collective-permute-start | bytes 393224 | tf_op jit(solution)/shard_map/ppermute | solution.py:430
  106.3 8.9 %collective-permute-start.7 = (bf16[2,2,2,32,256]{4,3,2,1,0:T(8,128)(2,1)S(1)}, bf16[2,2,2,32,256]{4,3,2,1,0:T(8,128)(2,1)S(1)}, u32[]{:S(2)}, u32[]{:S(2)}) collective-permute-start(bf16[2,2,2,32,256]{4,3,2,1,0:T(8,128)(2,1)S(1)} %pad_maximum_fusion.refs_0_), channel_id=1, source_target_pairs={{0,3},{1,2},{2,1},{3,0},{4,7},{5,6},{6,5},{7,4},{8,11},{9,10},{10,... | collective-permute-start | bytes 393224 | tf_op jit(solution)/shard_map/ppermute | solution.py:430
  107.8 10.8 %collective-permute-start.6 = (bf16[2,2,2,32,256]{4,3,2,1,0:T(8,128)(2,1)S(1)}, bf16[2,2,2,32,256]{4,3,2,1,0:T(8,128)(2,1)S(1)}, u32[]{:S(2)}, u32[]{:S(2)}) collective-permute-start(bf16[2,2,2,32,256]{4,3,2,1,0:T(8,128)(2,1)S(1)} %pad_maximum_fusion.refs_0_), channel_id=1, source_target_pairs={{0,2},{1,3},{2,0},{3,1},{4,6},{5,7},{6,4},{7,5},{8,10},{9,11},{10,... | collective-permute-start | bytes 393224 | tf_op jit(solution)/shard_map/ppermute | solution.py:430
  111.2 7.4 %collective-permute-start.5 = (bf16[2,2,2,32,256]{4,3,2,1,0:T(8,128)(2,1)S(1)}, bf16[2,2,2,32,256]{4,3,2,1,0:T(8,128)(2,1)S(1)}, u32[]{:S(2)}, u32[]{:S(2)}) collective-permute-start(bf16[2,2,2,32,256]{4,3,2,1,0:T(8,128)(2,1)S(1)} %pad_maximum_fusion.refs_0_), channel_id=1, source_target_pairs={{0,1},{1,0},{2,3},{3,2},{4,5},{5,4},{6,7},{7,6},{8,9},{9,8},{10,11... | collective-permute-start | bytes 393224 | tf_op jit(solution)/shard_map/ppermute | solution.py:430
  123.3 54.8 %all-to-all-start.2 = ((bf16[8,2,64,512]{3,2,1,0:T(8,128)(2,1)}), bf16[8,2,64,512]{3,2,1,0:T(8,128)(2,1)}, u32[]{:S(2)}, u32[]{:S(2)}) async-start(bf16[8,2,64,512]{3,2,1,0:T(8,128)(2,1)} %gram_second.1), calls=%async_computation.2 | async-start | bytes 2097152 | tf_op jit(solution)/shard_map/all_to_all | solution.py:476
  130.2 15.0 %collective-permute-start.12 = (bf16[2,64,512]{2,1,0:T(8,128)(2,1)S(1)}, bf16[2,64,512]{2,1,0:T(8,128)(2,1)S(1)}, u32[]{:S(2)}, u32[]{:S(2)}) collective-permute-start(bf16[2,64,512]{2,1,0:T(8,128)(2,1)S(1)} %get-tuple-element.25), channel_id=1, source_target_pairs={{0,1},{1,0},{2,3},{3,2},{4,5},{5,4},{6,7},{7,6},{8,9},{9,8},{10,11... | collective-permute-start | bytes 393224 | tf_op jit(solution)/shard_map/ppermute | solution.py:435
  132.1 17.7 %collective-permute-start.13 = (bf16[2,64,512]{2,1,0:T(8,128)(2,1)S(1)}, bf16[2,64,512]{2,1,0:T(8,128)(2,1)S(1)}, u32[]{:S(2)}, u32[]{:S(2)}) collective-permute-start(bf16[2,64,512]{2,1,0:T(8,128)(2,1)S(1)} %get-tuple-element.26), channel_id=1, source_target_pairs={{0,2},{1,3},{2,0},{3,1},{4,6},{5,7},{6,4},{7,5},{8,10},{9,11},{10,... | collective-permute-start | bytes 393224 | tf_op jit(solution)/shard_map/ppermute | solution.py:435
  133.6 23.8 %collective-permute-start.14 = (bf16[2,64,512]{2,1,0:T(8,128)(2,1)S(1)}, bf16[2,64,512]{2,1,0:T(8,128)(2,1)S(1)}, u32[]{:S(2)}, u32[]{:S(2)}) collective-permute-start(bf16[2,64,512]{2,1,0:T(8,128)(2,1)S(1)} %get-tuple-element.27), channel_id=1, source_target_pairs={{0,3},{1,2},{2,1},{3,0},{4,7},{5,6},{6,5},{7,4},{8,11},{9,10},{10,... | collective-permute-start | bytes 393224 | tf_op jit(solution)/shard_map/ppermute | solution.py:435
  133.8 24.3 %collective-permute-start.15 = (bf16[2,64,512]{2,1,0:T(8,128)(2,1)S(1)}, bf16[2,64,512]{2,1,0:T(8,128)(2,1)S(1)}, u32[]{:S(2)}, u32[]{:S(2)}) collective-permute-start(bf16[2,64,512]{2,1,0:T(8,128)(2,1)S(1)} %get-tuple-element.28), channel_id=1, source_target_pairs={{0,4},{1,5},{2,6},{3,7},{4,0},{5,1},{6,2},{7,3},{8,12},{9,13},{10,... | collective-permute-start | bytes 393224 | tf_op jit(solution)/shard_map/ppermute | solution.py:435
  137.2 27.5 %collective-permute-start.16 = (bf16[2,64,512]{2,1,0:T(8,128)(2,1)}, bf16[2,64,512]{2,1,0:T(8,128)(2,1)}, u32[]{:S(2)}, u32[]{:S(2)}) collective-permute-start(bf16[2,64,512]{2,1,0:T(8,128)(2,1)} %get-tuple-element.29), channel_id=1, source_target_pairs={{0,5},{1,4},{2,7},{3,6},{4,1},{5,0},{6,3},{7,2},{8,13},{9,12},{10,... | collective-permute-start | bytes 393224 | tf_op jit(solution)/shard_map/ppermute | solution.py:435
  145.9 20.9 %collective-permute-start.17 = (bf16[2,64,512]{2,1,0:T(8,128)(2,1)}, bf16[2,64,512]{2,1,0:T(8,128)(2,1)}, u32[]{:S(2)}, u32[]{:S(2)}) collective-permute-start(bf16[2,64,512]{2,1,0:T(8,128)(2,1)} %get-tuple-element.30), channel_id=1, source_target_pairs={{0,6},{1,7},{2,4},{3,5},{4,2},{5,3},{6,0},{7,1},{8,14},{9,15},{10,... | collective-permute-start | bytes 393224 | tf_op jit(solution)/shard_map/ppermute | solution.py:435
  150.5 16.9 %collective-permute-start.18 = (bf16[2,64,512]{2,1,0:T(8,128)(2,1)}, bf16[2,64,512]{2,1,0:T(8,128)(2,1)}, u32[]{:S(2)}, u32[]{:S(2)}) collective-permute-start(bf16[2,64,512]{2,1,0:T(8,128)(2,1)} %get-tuple-element.31), channel_id=1, source_target_pairs={{0,7},{1,6},{2,5},{3,4},{4,3},{5,2},{6,1},{7,0},{8,15},{9,14},{10,... | collective-permute-start | bytes 393224 | tf_op jit(solution)/shard_map/ppermute | solution.py:435
  158.1 11.6 %collective-permute-start.19 = (bf16[2,64,128]{2,1,0:T(8,128)(2,1)}, bf16[2,64,128]{2,1,0:T(8,128)(2,1)}, u32[]{:S(2)}, u32[]{:S(2)}) collective-permute-start(bf16[2,64,128]{2,1,0:T(8,128)(2,1)} %get-tuple-element.35), channel_id=1, source_target_pairs={{0,1},{1,0},{2,3},{3,2},{4,5},{5,4},{6,7},{7,6},{8,9},{9,8},{10,11... | collective-permute-start | bytes 98312 | tf_op jit(solution)/shard_map/ppermute | solution.py:435
  158.8 11.7 %collective-permute-start.20 = (bf16[2,64,128]{2,1,0:T(8,128)(2,1)}, bf16[2,64,128]{2,1,0:T(8,128)(2,1)}, u32[]{:S(2)}, u32[]{:S(2)}) collective-permute-start(bf16[2,64,128]{2,1,0:T(8,128)(2,1)} %get-tuple-element.36), channel_id=1, source_target_pairs={{0,2},{1,3},{2,0},{3,1},{4,6},{5,7},{6,4},{7,5},{8,10},{9,11},{10,... | collective-permute-start | bytes 98312 | tf_op jit(solution)/shard_map/ppermute | solution.py:435
  164.7 11.3 %collective-permute-start.21 = (bf16[2,64,128]{2,1,0:T(8,128)(2,1)}, bf16[2,64,128]{2,1,0:T(8,128)(2,1)S(1)}, u32[]{:S(2)}, u32[]{:S(2)}) collective-permute-start(bf16[2,64,128]{2,1,0:T(8,128)(2,1)} %copy-done.24), channel_id=1, source_target_pairs={{0,3},{1,2},{2,1},{3,0},{4,7},{5,6},{6,5},{7,4},{8,11},{9,10},{10,... | collective-permute-start | bytes 98312 | tf_op jit(solution)/shard_map/ppermute | solution.py:435
  166.7 9.2 %collective-permute-start.22 = (bf16[2,64,128]{2,1,0:T(8,128)(2,1)}, bf16[2,64,128]{2,1,0:T(8,128)(2,1)S(1)}, u32[]{:S(2)}, u32[]{:S(2)}) collective-permute-start(bf16[2,64,128]{2,1,0:T(8,128)(2,1)} %copy-done.23), channel_id=1, source_target_pairs={{0,4},{1,5},{2,6},{3,7},{4,0},{5,1},{6,2},{7,3},{8,12},{9,13},{10,... | collective-permute-start | bytes 98312 | tf_op jit(solution)/shard_map/ppermute | solution.py:435
  167.4 8.6 %collective-permute-start.23 = (bf16[2,64,128]{2,1,0:T(8,128)(2,1)}, bf16[2,64,128]{2,1,0:T(8,128)(2,1)S(1)}, u32[]{:S(2)}, u32[]{:S(2)}) collective-permute-start(bf16[2,64,128]{2,1,0:T(8,128)(2,1)} %copy-done.22), channel_id=1, source_target_pairs={{0,5},{1,4},{2,7},{3,6},{4,1},{5,0},{6,3},{7,2},{8,13},{9,12},{10,... | collective-permute-start | bytes 98312 | tf_op jit(solution)/shard_map/ppermute | solution.py:435
  169.7 6.3 %collective-permute-start.24 = (bf16[2,64,128]{2,1,0:T(8,128)(2,1)}, bf16[2,64,128]{2,1,0:T(8,128)(2,1)S(1)}, u32[]{:S(2)}, u32[]{:S(2)}) collective-permute-start(bf16[2,64,128]{2,1,0:T(8,128)(2,1)} %copy-done.21), channel_id=1, source_target_pairs={{0,6},{1,7},{2,4},{3,5},{4,2},{5,3},{6,0},{7,1},{8,14},{9,15},{10,... | collective-permute-start | bytes 98312 | tf_op jit(solution)/shard_map/ppermute | solution.py:435
  170.5 6.2 %collective-permute-start.25 = (bf16[2,64,128]{2,1,0:T(8,128)(2,1)}, bf16[2,64,128]{2,1,0:T(8,128)(2,1)S(1)}, u32[]{:S(2)}, u32[]{:S(2)}) collective-permute-start(bf16[2,64,128]{2,1,0:T(8,128)(2,1)} %copy-done.20), channel_id=1, source_target_pairs={{0,7},{1,6},{2,5},{3,4},{4,3},{5,2},{6,1},{7,0},{8,15},{9,14},{10,... | collective-permute-start | bytes 98312 | tf_op jit(solution)/shard_map/ppermute | solution.py:435
  (29 other events, 275.4 us)

commit v6 on v4

--- a/solution.py
+++ b/solution.py
@@ -279,36 +279,38 @@
     )(*terms, order)
 
 
-def finish_kernel(place_ref, terms_ref, base_ref, order_ref, out_ref):
+def finish_kernel(place_ref, terms_hbm, base_ref, order_ref, out_ref, terms_ref, sems):
+    loads = [pltpu.make_async_copy(terms_hbm.at[:, q], terms_ref.at[:, q], sems.at[q]) for q in (0, 1)]
+    for load in loads:
+        load.start()
     core = place_ref[0]
     rows = 2 * OWN_B
-    last, extra = [], []
     for q in (0, 1):
+        loads[q].wait()
         total = terms_ref[0, q].astype(F32)
         for t in range(1, N_TM):
             total = total + terms_ref[t, q].astype(F32)
-        last.append(jnp.concatenate([total[rows * j : rows * j + rows] for j in range(PIECES + 1)], 1))
-        extra.append(total[(PIECES + 1) * rows :])
-    lower = placed(last, order_ref[...])
-    upper = placed(extra, order_ref[COLS_A:, :])
-    for q in (0, 1):
-        top = base_ref[q] + upper[q]
+        last = jnp.concatenate([total[rows * j : rows * j + rows] for j in range(PIECES + 1)], 1)
+        (low,) = placed([last], order_ref[...])
+        (extra,) = placed([total[(PIECES + 1) * rows :]], order_ref[COLS_A:, :])
+        top = base_ref[q] + extra
         for rel in (0, 1):
             for chip in (0, 1):
                 row = pl.multiple_of(64 * chip + 32 * (rel ^ core), 8)
                 src = OWN_A * rel + FIRST * chip
-                out_ref[q, pl.ds(row, FIRST), :] = top[src : src + FIRST]
+                out_ref[pl.ds(row, FIRST), q, :] = top[src : src + FIRST]
                 src = 2 * SECOND * chip + SECOND * rel
-                out_ref[q, pl.ds(pl.multiple_of(row + FIRST, 8), SECOND), :] = lower[q][src : src + SECOND]
+                out_ref[pl.ds(row + FIRST, SECOND), q, :] = low[src : src + SECOND]
 
 
 def finish(place, terms, base, order):
     return pl.pallas_call(
         finish_kernel,
-        in_specs=[SMEM] + [VMEM] * 3,
+        in_specs=[SMEM, HBM, VMEM, VMEM],
         out_specs=VMEM,
-        out_shape=jax.ShapeDtypeStruct((2, 128, 1024), F32),
-        compiler_params=params(8),
+        out_shape=jax.ShapeDtypeStruct((128, 2, 1024), F32),
+        scratch_shapes=[pltpu.VMEM(terms.shape, BF16), pltpu.SemaphoreType.DMA((2,))],
+        compiler_params=params(10),
         cost_estimate=cost(1 << 28, 1 << 22),
         name="finish",
     )(place, terms, base, order)
@@ -430,7 +432,7 @@
     beams = beams.reshape(NF // 32, SPECTRA, 2, 256)
     base = spread_first(terms, order)
     rows = finish(place, last, base, order)
-    return beams, rows.transpose(1, 0, 2)[:, None]
+    return beams, rows[:, None]
 
 
 def solution(mesh):

time: 177 us -> 174 us (0.983)
  local copies, waits for them, and re-layouts: 12.9 us -> 9.26 us
    unnamed x36 -> x31, local copies, waits for them, and re-layouts: 8.78 us -> 5.17 us
where the time goes in v6:
time: 174 us
  waiting for transfers between devices  91.4 us (53%)
  starting transfers between devices  48.5 us (28%)
  Pallas kernels  22.6 us (13%)
  local copies, waits for them, and re-layouts  9.26 us (5%)
    ppermute x2, waiting for transfers between devices, step(): lax.ppermute(beam_weights, (*CHIP, *TM), ring)  35.1 us
    all_to_all x1, waiting for transfers between devices, step(): lax.all_to_all(ready_b, CHIP, 0, 0, tiled=True).reshape(COLS_B, 1024)  21.3 us
    all_to_all x1, waiting for transfers between devices, step(): arrived = lax.all_to_all(ready_a, CHIP, 0, 0, tiled=True)  18.8 us
    ppermute x7, starting transfers between devices, to_partners(): lax.ppermute(arrays[k], TM, pairs(k))  12.7 us
    ppermute x7, waiting for transfers between devices, with_partners(): return [array] + [lax.ppermute(array, TM, pairs(k)) for k in range(1, N_TM)]  10.8 us
    all_to_all x1, starting transfers between devices, step(): arrived = lax.all_to_all(ready_a, CHIP, 0, 0, tiled=True)  10.6 us
    all_to_all x1, starting transfers between devices, step(): lax.all_to_all(ready_b, CHIP, 0, 0, tiled=True).reshape(COLS_B, 1024)  8.37 us
    ppermute x7, starting transfers between devices, with_partners(): return [array] + [lax.ppermute(array, TM, pairs(k)) for k in range(1, N_TM)]  7.74 us
  transfers between devices with their start and end apart: 22, of which 12 were waited for; matrix products, arithmetic and copies ran while one was open for 3% of the time, Pallas kernels for 6%

profile of v6, /device:TPU:64, one launch (start us, length us, event | category | flops | bytes accessed | tf_op | source)
XLA Modules:
  0.0 173.9 jit_solution(1432066764112870150)
XLA Ops:
  1.3 4.7 %dft_lead.1 = bf16[16,2,16,1024]{3,2,1,0:T(8,128)(2,1)} custom-call(s32[4]{0:T(128)} %pad_add_fusion.place_ref, bf16[2,32,128,128]{3,2,1,0:T(8,128)(2,1)} %bitcast.25, bf16[256,256]{1,0:T(8,128)(2,1)} %constant.33.clone.left_hbm, f32[2,128,128]{2,1,0:T(8,128)} %constant.34.clone.turn_hbm, bf16[256,256]{1,0:T(8,128)(2,1)} %constant.35.clone.right_hbm), custom_call_target="tpu_custom_call" | custom-call | flops 1073741824 | bytes 2097152 | tf_op jit(solution)/shard_map/dft_lead/pallas_call | solution.py:148
  6.0 10.6 %all-to-all-start = ((bf16[16,2,16,1024]{3,2,1,0:T(8,128)(2,1)}), bf16[16,2,16,1024]{3,2,1,0:T(8,128)(2,1)}, u32[]{:S(2)}, u32[]{:S(2)}) async-start(bf16[16,2,16,1024]{3,2,1,0:T(8,128)(2,1)} %dft_lead.1), calls=%async_computation | async-start | bytes 2097152 | tf_op jit(solution)/shard_map/all_to_all | solution.py:420
  16.6 3.0 %dft_rest.1 = (bf16[16,16,1024]{2,1,0:T(8,128)(2,1)S(1)}, bf16[16,16,1024]{2,1,0:T(8,128)(2,1)S(1)}) custom-call(s32[4]{0:T(128)S(1)} %copy-done.7, bf16[2,32,128,128]{3,2,1,0:T(8,128)(2,1)S(1)} %bitcast.26, bf16[256,256]{1,0:T(8,128)(2,1)S(1)} %copy-done.11, f32[2,128,128]{2,1,0:T(8,128)S(1)} %copy-done.10, bf16[256,256]{1,0:T(8,128)(2,1)S(1)} %copy-done.9), custom_call_target="tpu_custom_call" | custom-call | flops 1073741824 | bytes 2097152 | tf_op jit(solution)/shard_map/dft_rest/pallas_call | solution.py:148
  20.6 1.0 collective-permute-done.1
  22.5 18.8 %all-to-all-done = bf16[16,2,16,1024]{3,2,1,0:T(8,128)(2,1)} async-done(((bf16[16,2,16,1024]{3,2,1,0:T(8,128)(2,1)}), bf16[16,2,16,1024]{3,2,1,0:T(8,128)(2,1)}, u32[]{:S(2)}, u32[]{:S(2)}) %all-to-all-start) | async-done | bytes 1048608 | tf_op jit(solution)/shard_map/all_to_all | solution.py:420
  41.3 8.4 %all-to-all-start.1 = ((bf16[16,32,1024]{2,1,0:T(8,128)(2,1)}), bf16[16,32,1024]{2,1,0:T(8,128)(2,1)S(1)}, u32[]{:S(2)}, u32[]{:S(2)}) async-start(bf16[16,32,1024]{2,1,0:T(8,128)(2,1)} %constant_dynamic-update-slice_fusion), calls=%async_computation.1 | async-start | bytes 2097152 | tf_op jit(solution)/shard_map/all_to_all | solution.py:421
  49.7 1.3 fusion.2
  51.1 1.9 %collective-permute-done.swapped_ref = bf16[256,1024]{1,0:T(8,128)(2,1)S(1)} collective-permute-done((bf16[256,1024]{1,0:T(8,128)(2,1)S(1)}, bf16[256,1024]{1,0:T(8,128)(2,1)S(1)}, u32[]{:S(2)}, u32[]{:S(2)}) %collective-permute-start) | collective-permute-done | bytes 524320 | tf_op jit(solution)/shard_map/ppermute | solution.py:379
  53.0 21.3 %all-to-all-done.1 = bf16[16,32,1024]{2,1,0:T(8,128)(2,1)S(1)} async-done(((bf16[16,32,1024]{2,1,0:T(8,128)(2,1)}), bf16[16,32,1024]{2,1,0:T(8,128)(2,1)S(1)}, u32[]{:S(2)}, u32[]{:S(2)}) %all-to-all-start.1) | async-done | bytes 1048608 | tf_op jit(solution)/shard_map/all_to_all | solution.py:421
  74.3 3.6 %gram_second.1 = bf16[8,2,192,512]{3,2,1,0:T(8,128)(2,1)} custom-call(bf16[512,1024]{1,0:T(8,128)(2,1)S(1)} %bitcast.20, bf16[256,1024]{1,0:T(8,128)(2,1)S(1)} %bitcast.22, bf16[256,1024]{1,0:T(8,128)(2,1)S(1)} %collective-permute-done.swapped_ref), custom_call_target="tpu_custom_call" | custom-call | flops 1073741824 | bytes 6291456 | tf_op jit(solution)/shard_map/gram_second/pallas_call | solution.py:232
  78.0 4.5 %all-to-all-start.2 = ((bf16[8,2,192,512]{3,2,1,0:T(8,128)(2,1)}), bf16[8,2,192,512]{3,2,1,0:T(8,128)(2,1)}, u32[]{:S(2)}, u32[]{:S(2)}) async-start(bf16[8,2,192,512]{3,2,1,0:T(8,128)(2,1)} %gram_second.1), calls=%async_computation.2 | async-start | bytes 6291456 | tf_op jit(solution)/shard_map/all_to_all | solution.py:428
  82.5 3.6 %collective-permute-start.3 = (bf16[2,32,256]{2,1,0:T(8,128)(2,1)S(1)}, bf16[2,32,256]{2,1,0:T(8,128)(2,1)S(1)}, u32[]{:S(2)}, u32[]{:S(2)}) collective-permute-start(bf16[2,32,256]{2,1,0:T(8,128)(2,1)S(1)} %copy-done.14), channel_id=1, source_target_pairs={{0,128},{1,145},{2,162},{3,179},{4,196},{5,213},{6,230},{7,247},{1... | collective-permute-start | bytes 98312 | tf_op jit(solution)/shard_map/ppermute | solution.py:407
  86.8 35.1 %collective-permute-done.3 = bf16[2,32,256]{2,1,0:T(8,128)(2,1)S(1)} collective-permute-done((bf16[2,32,256]{2,1,0:T(8,128)(2,1)S(1)}, bf16[2,32,256]{2,1,0:T(8,128)(2,1)S(1)}, u32[]{:S(2)}, u32[]{:S(2)}) %collective-permute-start.3) | collective-permute-done | bytes 32800 | tf_op jit(solution)/shard_map/ppermute | solution.py:407
  122.0 1.2 collective-permute-done.4
  123.5 7.5 %collective-permute-start.8 = (bf16[2,2,2,32,256]{4,3,2,1,0:T(8,128)(2,1)S(1)}, bf16[2,2,2,32,256]{4,3,2,1,0:T(8,128)(2,1)S(1)}, u32[]{:S(2)}, u32[]{:S(2)}) collective-permute-start(bf16[2,2,2,32,256]{4,3,2,1,0:T(8,128)(2,1)S(1)} %pad_maximum_fusion.refs_0_), channel_id=1, source_target_pairs={{0,4},{1,5},{2,6},{3,7},{4,0},{5,1},{6,2},{7,3},{8,12},{9,13},{10,... | collective-permute-start | bytes 393224 | tf_op jit(solution)/shard_map/ppermute | solution.py:384
  131.0 2.6 %collective-permute-done.11.refs_7_ = bf16[2,2,2,32,256]{4,3,2,1,0:T(8,128)(2,1)S(1)} collective-permute-done((bf16[2,2,2,32,256]{4,3,2,1,0:T(8,128)(2,1)S(1)}, bf16[2,2,2,32,256]{4,3,2,1,0:T(8,128)(2,1)S(1)}, u32[]{:S(2)}, u32[]{:S(2)}) %collective-permute-start.11) | collective-permute-done | bytes 131104 | tf_op jit(solution)/shard_map/ppermute | solution.py:384
  133.6 3.3 %collective-permute-done.10.refs_6_ = bf16[2,2,2,32,256]{4,3,2,1,0:T(8,128)(2,1)S(1)} collective-permute-done((bf16[2,2,2,32,256]{4,3,2,1,0:T(8,128)(2,1)S(1)}, bf16[2,2,2,32,256]{4,3,2,1,0:T(8,128)(2,1)S(1)}, u32[]{:S(2)}, u32[]{:S(2)}) %collective-permute-start.10) | collective-permute-done | bytes 131104 | tf_op jit(solution)/shard_map/ppermute | solution.py:384
  136.8 2.3 %collective-permute-done.8.refs_4_ = bf16[2,2,2,32,256]{4,3,2,1,0:T(8,128)(2,1)S(1)} collective-permute-done((bf16[2,2,2,32,256]{4,3,2,1,0:T(8,128)(2,1)S(1)}, bf16[2,2,2,32,256]{4,3,2,1,0:T(8,128)(2,1)S(1)}, u32[]{:S(2)}, u32[]{:S(2)}) %collective-permute-start.8) | collective-permute-done | bytes 131104 | tf_op jit(solution)/shard_map/ppermute | solution.py:384
  140.0 1.8 %collective-permute-done.5.refs_1_ = bf16[2,2,2,32,256]{4,3,2,1,0:T(8,128)(2,1)S(1)} collective-permute-done((bf16[2,2,2,32,256]{4,3,2,1,0:T(8,128)(2,1)S(1)}, bf16[2,2,2,32,256]{4,3,2,1,0:T(8,128)(2,1)S(1)}, u32[]{:S(2)}, u32[]{:S(2)}) %collective-permute-start.5) | collective-permute-done | bytes 131104 | tf_op jit(solution)/shard_map/ppermute | solution.py:384
  141.8 1.2 weights.1.weight_ref
  143.0 1.4 copy-done
  144.4 2.7 %gram_first.1 = (bf16[2,64,512]{2,1,0:T(8,128)(2,1)S(1)}, bf16[2,64,512]{2,1,0:T(8,128)(2,1)S(1)}, bf16[2,64,512]{2,1,0:T(8,128)(2,1)S(1)}, bf16[2,64,512]{2,1,0...) custom-call(s32[4]{0:T(128)S(1)} %copy-done.7, ...), custom_call_target="tpu_custom_call" | custom-call | flops 2147483648 | bytes 6291456 | tf_op jit(solution)/shard_map/gram_first/pallas_call | solution.py:193
  147.2 3.5 %collective-permute-start.14 = (bf16[2,64,512]{2,1,0:T(8,128)(2,1)}, bf16[2,64,512]{2,1,0:T(8,128)(2,1)}, u32[]{:S(2)}, u32[]{:S(2)}) collective-permute-start(bf16[2,64,512]{2,1,0:T(8,128)(2,1)} %get-tuple-element.18), channel_id=1, source_target_pairs={{0,3},{1,2},{2,1},{3,0},{4,7},{5,6},{6,5},{7,4},{8,11},{9,10},{10,... | collective-permute-start | bytes 393224 | tf_op jit(solution)/shard_map/ppermute | solution.py:389
  150.8 1.9 %collective-permute-start.15 = (bf16[2,64,512]{2,1,0:T(8,128)(2,1)}, bf16[2,64,512]{2,1,0:T(8,128)(2,1)}, u32[]{:S(2)}, u32[]{:S(2)}) collective-permute-start(bf16[2,64,512]{2,1,0:T(8,128)(2,1)} %get-tuple-element.19), channel_id=1, source_target_pairs={{0,4},{1,5},{2,6},{3,7},{4,0},{5,1},{6,2},{7,3},{8,12},{9,13},{10,... | collective-permute-start | bytes 393224 | tf_op jit(solution)/shard_map/ppermute | solution.py:389
  152.6 1.1 collective-permute-start.16
  153.7 2.0 %collective-permute-start.17 = (bf16[2,64,512]{2,1,0:T(8,128)(2,1)}, bf16[2,64,512]{2,1,0:T(8,128)(2,1)}, u32[]{:S(2)}, u32[]{:S(2)}) collective-permute-start(bf16[2,64,512]{2,1,0:T(8,128)(2,1)} %get-tuple-element.21), channel_id=1, source_target_pairs={{0,6},{1,7},{2,4},{3,5},{4,2},{5,3},{6,0},{7,1},{8,14},{9,15},{10,... | collective-permute-start | bytes 393224 | tf_op jit(solution)/shard_map/ppermute | solution.py:389
  155.7 1.2 collective-permute-done.13.refs_2_
  156.9 4.2 %collective-permute-start.18 = (bf16[2,64,512]{2,1,0:T(8,128)(2,1)}, bf16[2,64,512]{2,1,0:T(8,128)(2,1)}, u32[]{:S(2)}, u32[]{:S(2)}) collective-permute-start(bf16[2,64,512]{2,1,0:T(8,128)(2,1)} %get-tuple-element.22), channel_id=1, source_target_pairs={{0,7},{1,6},{2,5},{3,4},{4,3},{5,2},{6,1},{7,0},{8,15},{9,14},{10,... | collective-permute-start | bytes 393224 | tf_op jit(solution)/shard_map/ppermute | solution.py:389
  163.6 1.3 beams.1
  165.7 2.0 %reshape.20 = bf16[128,4,2,256]{3,2,1,0:T(2,128)(2,1)} reshape(bf16[512,512]{1,0:T(8,128)(2,1)} %copy-done.6) | data formatting | bytes 1048576 | tf_op jit(solution)/shard_map/reshape | solution.py:432
  167.7 1.7 spread_first.1.base_ref
  169.4 4.3 %finish.1 = f32[128,2,1024]{2,1,0:T(2,128)} custom-call(s32[4]{0:T(128)S(1)} %copy-done.7, bf16[8,2,192,512]{3,2,1,0:T(8,128)(2,1)} %all-to-all-done.2.terms_hbm, f32[2,64,1024]{2,1,0:T(8,128)S(1)} %spread_first.1.base_ref, bf16[1024,1024]{1,0:T(8,128)(2,1)S(1)} %fusion.refs_8_.order_ref), custom_call_target="tpu_custom_call" | custom-call | flops 536870912 | bytes 4194304 | tf_op jit(solution)/shard_map/finish/pallas_call | solution.py:307
  (59 shorter events, 7.8 us)
Async XLA Ops:
  0.6 16.0 %copy-start.9 = (bf16[256,256]{1,0:T(8,128)(2,1)S(1)}, bf16[256,256]{1,0:T(8,128)(2,1)}, u32[]{:S(2)}) copy-start(bf16[256,256]{1,0:T(8,128)(2,1)} %constant.35.clone.right_hbm) | copy-start | bytes 393220
  0.6 16.0 %copy-start.10 = (f32[2,128,128]{2,1,0:T(8,128)S(1)}, f32[2,128,128]{2,1,0:T(8,128)}, u32[]{:S(2)}) copy-start(f32[2,128,128]{2,1,0:T(8,128)} %constant.34.clone.turn_hbm) | copy-start | bytes 393220
  0.7 15.9 %copy-start.11 = (bf16[256,256]{1,0:T(8,128)(2,1)S(1)}, bf16[256,256]{1,0:T(8,128)(2,1)}, u32[]{:S(2)}) copy-start(bf16[256,256]{1,0:T(8,128)(2,1)} %constant.33.clone.left_hbm) | copy-start | bytes 393220
  0.7 15.9 %copy-start.8 = (bf16[2,32,4,4096]{3,2,1,0:T(4,128)(2,1)S(1)}, bf16[2,32,4,4096]{3,2,1,0:T(4,128)(2,1)}, u32[]{:S(2)}) copy-start(bf16[2,32,4,4096]{3,2,1,0:T(4,128)(2,1)} %param.7) | copy-start | bytes 6291460
  1.3 15.3 %copy-start.7 = (s32[4]{0:T(128)S(1)}, s32[4]{0:T(128)}, u32[]{:S(2)}) copy-start(s32[4]{0:T(128)} %pad_add_fusion.place_ref) | copy-start | bytes 52
  6.0 35.3 %all-to-all-start = ((bf16[16,2,16,1024]{3,2,1,0:T(8,128)(2,1)}), bf16[16,2,16,1024]{3,2,1,0:T(8,128)(2,1)}, u32[]{:S(2)}, u32[]{:S(2)}) async-start(bf16[16,2,16,1024]{3,2,1,0:T(8,128)(2,1)} %dft_lead.1), calls=%async_computation | async-start | bytes 2097152 | tf_op jit(solution)/shard_map/all_to_all | solution.py:420
  19.6 2.0 %collective-permute-start.1 = (bf16[16,16,1024]{2,1,0:T(8,128)(2,1)S(1)}, bf16[16,16,1024]{2,1,0:T(8,128)(2,1)S(1)}, u32[]{:S(2)}, u32[]{:S(2)}) collective-permute-start(bf16[16,16,1024]{2,1,0:T(8,128)(2,1)S(1)} %get-tuple-element.14), channel_id=1, source_target_pairs={{0,8},{8,0},{1,9},{9,1},{2,10},{10,2},{3,11},{11,3},{4,12},{12,4},... | collective-permute-start | bytes 1572872 | tf_op jit(solution)/shard_map/ppermute | solution.py:379
  41.3 33.0 %all-to-all-start.1 = ((bf16[16,32,1024]{2,1,0:T(8,128)(2,1)}), bf16[16,32,1024]{2,1,0:T(8,128)(2,1)S(1)}, u32[]{:S(2)}, u32[]{:S(2)}) async-start(bf16[16,32,1024]{2,1,0:T(8,128)(2,1)} %constant_dynamic-update-slice_fusion), calls=%async_computation.1 | async-start | bytes 2097152 | tf_op jit(solution)/shard_map/all_to_all | solution.py:421
  51.0 93.4 %copy-start.2 = (bf16[16,1,16,1024]{3,2,1,0:T(8,128)(2,1)}, bf16[16,1,16,1024]{3,2,1,0:T(8,128)(2,1)S(1)}, u32[]{:S(2)}) copy-start(bf16[16,1,16,1024]{3,2,1,0:T(8,128)(2,1)S(1)} %get-tuple-element.27) | copy-start | bytes 1572868
  51.0 2.0 %collective-permute-start = (bf16[256,1024]{1,0:T(8,128)(2,1)S(1)}, bf16[256,1024]{1,0:T(8,128)(2,1)S(1)}, u32[]{:S(2)}, u32[]{:S(2)}) collective-permute-start(bf16[256,1024]{1,0:T(8,128)(2,1)S(1)} %bitcast.28), channel_id=1, source_target_pairs={{0,8},{8,0},{1,9},{9,1},{2,10},{10,2},{3,11},{11,3},{4,12},{12,4},... | collective-permute-start | bytes 1572872 | tf_op jit(solution)/shard_map/ppermute | solution.py:379
  53.0 91.4 %copy-start.4 = (bf16[256,1024]{1,0:T(8,128)(2,1)}, bf16[256,1024]{1,0:T(8,128)(2,1)S(1)}, u32[]{:S(2)}) copy-start(bf16[256,1024]{1,0:T(8,128)(2,1)S(1)} %collective-permute-done.swapped_ref) | copy-start | bytes 1572868
  77.9 4.5 %copy-start.14 = (bf16[2,32,256]{2,1,0:T(8,128)(2,1)S(1)}, bf16[2,32,256]{2,1,0:T(8,128)(2,1)}, u32[]{:S(2)}) copy-start(bf16[2,32,256]{2,1,0:T(8,128)(2,1)} %param.8) | copy-start | bytes 98308
  78.0 91.4 %all-to-all-start.2 = ((bf16[8,2,192,512]{3,2,1,0:T(8,128)(2,1)}), bf16[8,2,192,512]{3,2,1,0:T(8,128)(2,1)}, u32[]{:S(2)}, u32[]{:S(2)}) async-start(bf16[8,2,192,512]{3,2,1,0:T(8,128)(2,1)} %gram_second.1), calls=%async_computation.2 | async-start | bytes 6291456 | tf_op jit(solution)/shard_map/all_to_all | solution.py:428
  82.5 39.4 %collective-permute-start.3 = (bf16[2,32,256]{2,1,0:T(8,128)(2,1)S(1)}, bf16[2,32,256]{2,1,0:T(8,128)(2,1)S(1)}, u32[]{:S(2)}, u32[]{:S(2)}) collective-permute-start(bf16[2,32,256]{2,1,0:T(8,128)(2,1)S(1)} %copy-done.14), channel_id=1, source_target_pairs={{0,128},{1,145},{2,162},{3,179},{4,196},{5,213},{6,230},{7,247},{1... | collective-permute-start | bytes 98312 | tf_op jit(solution)/shard_map/ppermute | solution.py:407
  86.1 35.8 %collective-permute-start.2 = (bf16[2,32,256]{2,1,0:T(8,128)(2,1)S(1)}, bf16[2,32,256]{2,1,0:T(8,128)(2,1)S(1)}, u32[]{:S(2)}, u32[]{:S(2)}) collective-permute-start(bf16[2,32,256]{2,1,0:T(8,128)(2,1)S(1)} %copy-done.14), channel_id=1, source_target_pairs={{0,0},{1,17},{2,34},{3,51},{4,68},{5,85},{6,102},{7,119},{16,16},{... | collective-permute-start | bytes 98312 | tf_op jit(solution)/shard_map/ppermute | solution.py:407
  121.9 1.3 collective-permute-start.4
  123.2 10.3 %collective-permute-start.11 = (bf16[2,2,2,32,256]{4,3,2,1,0:T(8,128)(2,1)S(1)}, bf16[2,2,2,32,256]{4,3,2,1,0:T(8,128)(2,1)S(1)}, u32[]{:S(2)}, u32[]{:S(2)}) collective-permute-start(bf16[2,2,2,32,256]{4,3,2,1,0:T(8,128)(2,1)S(1)} %pad_maximum_fusion.refs_0_), channel_id=1, source_target_pairs={{0,7},{1,6},{2,5},{3,4},{4,3},{5,2},{6,1},{7,0},{8,15},{9,14},{10,... | collective-permute-start | bytes 393224 | tf_op jit(solution)/shard_map/ppermute | solution.py:384
  123.3 13.5 %collective-permute-start.10 = (bf16[2,2,2,32,256]{4,3,2,1,0:T(8,128)(2,1)S(1)}, bf16[2,2,2,32,256]{4,3,2,1,0:T(8,128)(2,1)S(1)}, u32[]{:S(2)}, u32[]{:S(2)}) collective-permute-start(bf16[2,2,2,32,256]{4,3,2,1,0:T(8,128)(2,1)S(1)} %pad_maximum_fusion.refs_0_), channel_id=1, source_target_pairs={{0,6},{1,7},{2,4},{3,5},{4,2},{5,3},{6,0},{7,1},{8,14},{9,15},{10,... | collective-permute-start | bytes 393224 | tf_op jit(solution)/shard_map/ppermute | solution.py:384
  123.4 13.4 %collective-permute-start.9 = (bf16[2,2,2,32,256]{4,3,2,1,0:T(8,128)(2,1)S(1)}, bf16[2,2,2,32,256]{4,3,2,1,0:T(8,128)(2,1)S(1)}, u32[]{:S(2)}, u32[]{:S(2)}) collective-permute-start(bf16[2,2,2,32,256]{4,3,2,1,0:T(8,128)(2,1)S(1)} %pad_maximum_fusion.refs_0_), channel_id=1, source_target_pairs={{0,5},{1,4},{2,7},{3,6},{4,1},{5,0},{6,3},{7,2},{8,13},{9,12},{10,... | collective-permute-start | bytes 393224 | tf_op jit(solution)/shard_map/ppermute | solution.py:384
  123.5 15.6 %collective-permute-start.8 = (bf16[2,2,2,32,256]{4,3,2,1,0:T(8,128)(2,1)S(1)}, bf16[2,2,2,32,256]{4,3,2,1,0:T(8,128)(2,1)S(1)}, u32[]{:S(2)}, u32[]{:S(2)}) collective-permute-start(bf16[2,2,2,32,256]{4,3,2,1,0:T(8,128)(2,1)S(1)} %pad_maximum_fusion.refs_0_), channel_id=1, source_target_pairs={{0,4},{1,5},{2,6},{3,7},{4,0},{5,1},{6,2},{7,3},{8,12},{9,13},{10,... | collective-permute-start | bytes 393224 | tf_op jit(solution)/shard_map/ppermute | solution.py:384
  131.0 8.1 %collective-permute-start.7 = (bf16[2,2,2,32,256]{4,3,2,1,0:T(8,128)(2,1)S(1)}, bf16[2,2,2,32,256]{4,3,2,1,0:T(8,128)(2,1)S(1)}, u32[]{:S(2)}, u32[]{:S(2)}) collective-permute-start(bf16[2,2,2,32,256]{4,3,2,1,0:T(8,128)(2,1)S(1)} %pad_maximum_fusion.refs_0_), channel_id=1, source_target_pairs={{0,3},{1,2},{2,1},{3,0},{4,7},{5,6},{6,5},{7,4},{8,11},{9,10},{10,... | collective-permute-start | bytes 393224 | tf_op jit(solution)/shard_map/ppermute | solution.py:384
  133.6 6.4 %collective-permute-start.6 = (bf16[2,2,2,32,256]{4,3,2,1,0:T(8,128)(2,1)S(1)}, bf16[2,2,2,32,256]{4,3,2,1,0:T(8,128)(2,1)S(1)}, u32[]{:S(2)}, u32[]{:S(2)}) collective-permute-start(bf16[2,2,2,32,256]{4,3,2,1,0:T(8,128)(2,1)S(1)} %pad_maximum_fusion.refs_0_), channel_id=1, source_target_pairs={{0,2},{1,3},{2,0},{3,1},{4,6},{5,7},{6,4},{7,5},{8,10},{9,11},{10,... | collective-permute-start | bytes 393224 | tf_op jit(solution)/shard_map/ppermute | solution.py:384
  136.8 5.0 %collective-permute-start.5 = (bf16[2,2,2,32,256]{4,3,2,1,0:T(8,128)(2,1)S(1)}, bf16[2,2,2,32,256]{4,3,2,1,0:T(8,128)(2,1)S(1)}, u32[]{:S(2)}, u32[]{:S(2)}) collective-permute-start(bf16[2,2,2,32,256]{4,3,2,1,0:T(8,128)(2,1)S(1)} %pad_maximum_fusion.refs_0_), channel_id=1, source_target_pairs={{0,1},{1,0},{2,3},{3,2},{4,5},{5,4},{6,7},{7,6},{8,9},{9,8},{10,11... | collective-permute-start | bytes 393224 | tf_op jit(solution)/shard_map/ppermute | solution.py:384
  144.4 2.8 %copy-start.13 = (s32[1024]{0:T(1024)S(1)}, s32[1024]{0:T(1024)}, u32[]{:S(2)}) copy-start(s32[1024]{0:T(1024)} %constant.36.clone) | copy-start | bytes 12292
  144.4 17.1 %copy-start.1 = (bf16[512,2048]{1,0:T(8,128)(2,1)S(1)}, bf16[512,2048]{1,0:T(8,128)(2,1)}, u32[]{:S(2)}) copy-start(bf16[512,2048]{1,0:T(8,128)(2,1)} %copy-done) | copy-start | bytes 6291460
  147.2 6.6 %collective-permute-start.12 = (bf16[2,64,512]{2,1,0:T(8,128)(2,1)S(1)}, bf16[2,64,512]{2,1,0:T(8,128)(2,1)S(1)}, u32[]{:S(2)}, u32[]{:S(2)}) collective-permute-start(bf16[2,64,512]{2,1,0:T(8,128)(2,1)S(1)} %get-tuple-element.16), channel_id=1, source_target_pairs={{0,1},{1,0},{2,3},{3,2},{4,5},{5,4},{6,7},{7,6},{8,9},{9,8},{10,11... | collective-permute-start | bytes 393224 | tf_op jit(solution)/shard_map/ppermute | solution.py:389
  147.2 9.7 %collective-permute-start.13 = (bf16[2,64,512]{2,1,0:T(8,128)(2,1)S(1)}, bf16[2,64,512]{2,1,0:T(8,128)(2,1)S(1)}, u32[]{:S(2)}, u32[]{:S(2)}) collective-permute-start(bf16[2,64,512]{2,1,0:T(8,128)(2,1)S(1)} %get-tuple-element.17), channel_id=1, source_target_pairs={{0,2},{1,3},{2,0},{3,1},{4,6},{5,7},{6,4},{7,5},{8,10},{9,11},{10,... | collective-permute-start | bytes 393224 | tf_op jit(solution)/shard_map/ppermute | solution.py:389
  147.2 20.5 %collective-permute-start.14 = (bf16[2,64,512]{2,1,0:T(8,128)(2,1)}, bf16[2,64,512]{2,1,0:T(8,128)(2,1)}, u32[]{:S(2)}, u32[]{:S(2)}) collective-permute-start(bf16[2,64,512]{2,1,0:T(8,128)(2,1)} %get-tuple-element.18), channel_id=1, source_target_pairs={{0,3},{1,2},{2,1},{3,0},{4,7},{5,6},{6,5},{7,4},{8,11},{9,10},{10,... | collective-permute-start | bytes 393224 | tf_op jit(solution)/shard_map/ppermute | solution.py:389
  150.8 16.9 %collective-permute-start.15 = (bf16[2,64,512]{2,1,0:T(8,128)(2,1)}, bf16[2,64,512]{2,1,0:T(8,128)(2,1)}, u32[]{:S(2)}, u32[]{:S(2)}) collective-permute-start(bf16[2,64,512]{2,1,0:T(8,128)(2,1)} %get-tuple-element.19), channel_id=1, source_target_pairs={{0,4},{1,5},{2,6},{3,7},{4,0},{5,1},{6,2},{7,3},{8,12},{9,13},{10,... | collective-permute-start | bytes 393224 | tf_op jit(solution)/shard_map/ppermute | solution.py:389
  152.6 15.0 %collective-permute-start.16 = (bf16[2,64,512]{2,1,0:T(8,128)(2,1)}, bf16[2,64,512]{2,1,0:T(8,128)(2,1)}, u32[]{:S(2)}, u32[]{:S(2)}) collective-permute-start(bf16[2,64,512]{2,1,0:T(8,128)(2,1)} %get-tuple-element.20), channel_id=1, source_target_pairs={{0,5},{1,4},{2,7},{3,6},{4,1},{5,0},{6,3},{7,2},{8,13},{9,12},{10,... | collective-permute-start | bytes 393224 | tf_op jit(solution)/shard_map/ppermute | solution.py:389
  153.7 14.0 %collective-permute-start.17 = (bf16[2,64,512]{2,1,0:T(8,128)(2,1)}, bf16[2,64,512]{2,1,0:T(8,128)(2,1)}, u32[]{:S(2)}, u32[]{:S(2)}) collective-permute-start(bf16[2,64,512]{2,1,0:T(8,128)(2,1)} %get-tuple-element.21), channel_id=1, source_target_pairs={{0,6},{1,7},{2,4},{3,5},{4,2},{5,3},{6,0},{7,1},{8,14},{9,15},{10,... | collective-permute-start | bytes 393224 | tf_op jit(solution)/shard_map/ppermute | solution.py:389
  156.9 10.8 %collective-permute-start.18 = (bf16[2,64,512]{2,1,0:T(8,128)(2,1)}, bf16[2,64,512]{2,1,0:T(8,128)(2,1)}, u32[]{:S(2)}, u32[]{:S(2)}) collective-permute-start(bf16[2,64,512]{2,1,0:T(8,128)(2,1)} %get-tuple-element.22), channel_id=1, source_target_pairs={{0,7},{1,6},{2,5},{3,4},{4,3},{5,2},{6,1},{7,0},{8,15},{9,14},{10,... | collective-permute-start | bytes 393224 | tf_op jit(solution)/shard_map/ppermute | solution.py:389
  (5 other events, 7.1 us)
